TPU v7x, 256 devices: a whole 4x4x8 slice. The times are simulated.
256 devices in a mesh: pop: 64 (over x, z, core), mp: 4 (over y).
Axes of the slice: x: 4, y: 4, z: 8, core: 2. Of those that a mesh axis runs over, the one named last changes fastest.
Arguments:
- tokens: bfloat16 [256, 3584], replicated, may hold values from -60 to 60
- target: bfloat16 [256, 3584], P(None, 'mp'), may hold values from -6 to 6
- w_query: bfloat16 [3584, 3584], P('pop', 'mp'), may hold values from -0.09375 to 0.09375
- w_key: bfloat16 [3584, 512], P(None, 'mp'), may hold values from -0.09375 to 0.09375
- w_value: bfloat16 [3584, 512], P(None, 'mp'), may hold values from -0.09375 to 0.09375
- w_out: bfloat16 [3584, 3584], P('mp', 'pop'), may hold values from -0.09375 to 0.09375
- query_left_factors: bfloat16 [64, 3584, 4], P('pop'), may hold values from -0.09375 to 0.09375
- query_right_factors: bfloat16 [64, 4, 3584], P('pop', None, 'mp'), may hold values from -6 to 6
- o_left: bfloat16 [64, 3584, 4], P('pop', 'mp'), may hold values from -0.09375 to 0.09375
- o_right: bfloat16 [64, 4, 3584], P('pop'), may hold values from -6 to 6
- member_ids: int32 [64], P('pop'), may hold values from 0 to 63, each once
Outputs:
- grad_query: float32 [3584, 3584], P('pop', 'mp')
- grad_out: float32 [3584, 3584], P('mp', 'pop')
- fitness: float32 [64], P('pop')
Inputs may be any that keep to these rules, and one draw needn't show every extreme that they name: `member_ids`: every number from 0 to 63 appears once.
All inputs are finite; a program needn't handle non-finite values.
Results may differ from a plain program's by a relative error of at most 0.005.
Values may be sent and summed in bfloat16 or wider, within the bound.
No kernel may reach another device: no remote copies, remote signals or barrier semaphores. Data moves between devices by JAX's collectives and lax.ppermute only.
A program may use at most 64 MiB of HBM per device.

v0:
```python
import functools
import math

import jax
import jax.numpy as jnp
from jax import lax
from jax.experimental import pallas as pl
from jax.experimental.pallas import tpu as pltpu
from jax.sharding import Mesh
from jax.sharding import PartitionSpec as P

D = 3584
HEAD_DIM = 128
RANK = 4
POP = ("pop_0", "pop_1", "pop_2")
CHIPS = ("pop_0", "pop_1")

rope_base = 1000000.0
spread_floor = 0.001

F32 = jnp.float32
BF16 = jnp.bfloat16
NT = (((1,), (1,)), ((), ()))
TN = (((0,), (0,)), ((), ()))


def iota(shape, dim):
    return lax.broadcasted_iota(jnp.int32, shape, dim)


def shift(x, axis, size, step):
    return lax.ppermute(x, axis, [(i, (i + step) % size) for i in range(size)])


def swap(x):
    return lax.ppermute(x, "pop_2", [(0, 1), (1, 0)])


def tables(position, head_size):
    index = jnp.arange(head_size // 2, dtype=F32)
    freq = jnp.exp(-math.log(rope_base) * 2.0 * index / head_size)
    angle = position[:, None] * freq[None, :]
    c, s = jnp.cos(angle), jnp.sin(angle)
    return jnp.concatenate([c, c], axis=-1), jnp.concatenate([-s, s], axis=-1)


def front_kernel(where_ref, tokens_ref, w_ref, left_ref, right_ref, o_ref, out_ref, pad_ref):
    p = where_ref[0]
    start = pl.multiple_of(jnp.minimum((56 * p) // 128 * 128, 3584 - 256), 128)
    at = pl.multiple_of(56 * p - start, 8)
    pad_ref[...] = jnp.zeros_like(pad_ref)
    pad_ref[pl.ds(at, 56), :] = w_ref[...].astype(F32)
    window = tokens_ref[:, pl.ds(start, 256)]
    share = jnp.dot(window, pad_ref[...].astype(BF16), preferred_element_type=F32)
    out_ref[:, :, 0:896] = share.reshape(32, 8, 896).astype(BF16)
    left = left_ref[...].astype(F32)
    left = jnp.concatenate([left, jnp.zeros_like(left)], axis=0).astype(BF16)
    low = lax.dot_general(tokens_ref[...], left, NT, preferred_element_type=F32)
    low = low.astype(BF16).astype(F32) * jnp.where(where_ref[1] == 0, 0.5, -0.5)
    out_ref[:, :, 896:1024] = jnp.zeros((32, 8, 128), BF16)
    out_ref[:, :, 896:904] = low.reshape(32, 8, 8).astype(BF16)
    both = jnp.concatenate([right_ref[...].astype(F32), o_ref[...].astype(F32)], axis=0)
    out_ref[:, :, 1024:1920] = jnp.broadcast_to(both[None], (32, 8, 896)).astype(BF16)


def attention_kernel(heads, where_ref, recv_ref, base_ref, other_ref, keys_ref, values_ref, cos_ref, sin_ref, mixed_ref):
    tok = keys_ref.shape[0]
    rows = 256
    scale = HEAD_DIM ** (-0.5)
    factors = recv_ref[:, :, 1024:1920].astype(F32).reshape(rows, 896).astype(BF16)
    small = recv_ref[:, :, 896:1024].astype(F32).reshape(rows, 128).astype(BF16)
    lane = iota((128, rows), 1)
    pick = (iota((128, rows), 0) == (lane & 3)).astype(BF16)
    spread = jnp.dot(small, pick, preferred_element_type=F32)
    r, c = iota((rows, rows), 0), iota((rows, rows), 1)
    mine = (r >> 3) == (c >> 3)
    left = jnp.where(mine & ((c & 7) < 4), spread, 0.0).astype(BF16)
    low = jnp.dot(left, factors, preferred_element_type=F32)
    cos = jnp.broadcast_to(cos_ref[...][None], (rows // 8, 8, 128)).reshape(rows, 128)
    sin = jnp.broadcast_to(sin_ref[...][None], (rows // 8, 8, 128)).reshape(rows, 128)
    keys, values = keys_ref[...], values_ref[...]
    seen = (iota((rows, tok), 0) & 7) + where_ref[0] >= iota((rows, tok), 1)
    for h in range(heads):
        at = slice(h * 128, (h + 1) * 128)
        base = base_ref[:, at] + other_ref[:, at]
        q = jnp.broadcast_to(base[None], (rows // 8, 8, 128)).reshape(rows, 128) + low[:, at]
        q = (q * cos + pltpu.roll(q, 64, 1) * sin).astype(BF16)
        s = lax.dot_general(q, keys, NT, preferred_element_type=F32) * scale
        s = jnp.where(seen, s, -1e30)
        e = jnp.exp(s - jnp.max(s, axis=1, keepdims=True))
        p = (e / jnp.sum(e, axis=1, keepdims=True)).astype(BF16)
        mixed_ref[0:256, at] = jnp.dot(p, values, preferred_element_type=F32).astype(BF16)
    d = lax.dot_general(factors, mixed_ref[0:256, :], NT, preferred_element_type=F32)
    d = jnp.where(mine & ((r & 7) >= 4), d, 0.0).reshape(rows // 8, 8, rows)
    d = jnp.sum(d, axis=0)
    hi = d.astype(BF16).astype(F32)
    mixed_ref[256:272, :] = jnp.zeros((16, 896), BF16)
    mixed_ref[256:272, 0:256] = jnp.concatenate([hi, d - hi], axis=0).astype(BF16)


def stack_kernel(*refs):
    for e in range(8):
        for (at, high), out_ref in zip(PARTS, refs[8:]):
            out_ref[e] = refs[e][at : at + high]


def project_kernel(high, where_ref, *refs):
    pieces, (own_ref, other_ref), out_refs = refs[:5], refs[5:7], refs[7:11]
    w_ref, mixed_ref, hold_ref, sems = refs[11:]
    copies = []
    for d in range(4):
        for e in range(8):
            piece = pieces[d].at[e] if d < 3 else pieces[3 + e // 4].at[e % 4]
            place = w_ref.at[where_ref[1 + d], where_ref[5 + e]]
            copies.append(pltpu.make_async_copy(piece, place, sems.at[8 * d + e]))
    copies.append(pltpu.make_async_copy(own_ref, mixed_ref.at[0], sems.at[32]))
    copies.append(pltpu.make_async_copy(other_ref, mixed_ref.at[1], sems.at[33]))
    for copy in copies:
        copy.start()
    for copy in copies:
        copy.wait()
    groups = high
    sides = [pl.ds(pl.multiple_of(256 * a, 128), 256) for a in (where_ref[0], 1 - where_ref[0])]
    outs = []
    for j in range(4):
        w = w_ref[j].astype(F32).reshape(8 * high, 896).astype(BF16)
        for i, at in enumerate(sides):
            got = lax.dot_general(w, mixed_ref[i, 0:256, :], NT, preferred_element_type=F32)
            hold_ref[j, 0:groups, :, at] = got.reshape(groups, 8, 256).astype(BF16)
            low = mixed_ref[i, 256:272, 0:256].astype(F32).reshape(2, 8, 256)
            hold_ref[j, groups : groups + 2, :, at] = low.astype(BF16)
        outs.append(pltpu.make_async_copy(hold_ref.at[j], out_refs[j], sems.at[34 + j]))
        outs[-1].start()
    for copy in outs:
        copy.wait()


def error_kernel(*refs):
    recv_refs, (right_ref, target_ref, so_far_ref, err_ref) = refs[:4], refs[4:]
    groups = recv_refs[0].shape[0] - 2
    feats = groups * 8
    total = low = 0.0
    for ref in recv_refs:
        total = total + ref[0:groups].astype(F32)
        low = low + ref[groups : groups + 2].astype(F32)
    tile = (iota((8, 512), 0) == (iota((8, 512), 1) & 7)).astype(BF16)
    target = lax.dot_general(target_ref[...], tile, TN, preferred_element_type=F32)
    total = total.reshape(feats, 512) - target
    low = low[0] + low[1]
    low = pltpu.roll(low, 4, 0) + low
    low = jnp.broadcast_to(low[None], (32, 8, 512)).reshape(256, 512)
    r, c = iota((256, 512), 0), iota((256, 512), 1)
    mine = ((r >> 3) == ((c & 255) >> 3)) & (((r & 7) >> 2) == (c >> 8))
    low = jnp.where(mine, low, 0.0)
    right = right_ref[...]
    for _ in range(3):
        piece = low.astype(BF16)
        total = total + lax.dot_general(right, piece, TN, preferred_element_type=F32)
        low = low - piece.astype(F32)
    err = jnp.sum((total * total).reshape(groups, 8, 512), axis=0)
    err = jnp.sum(err, axis=0, keepdims=True) + so_far_ref[0]
    err_ref[...] = jnp.broadcast_to(err[None], (8, 1, 512))


def final_kernel(where_ref, err_ref, left_ref, own_ref, other_ref, query_ref, out_ref, fit_ref):
    core, chip = where_ref[0], where_ref[1]
    err = jnp.sum(err_ref[...], axis=0)
    at = iota((256, 512), 1)
    row = iota((256, 512), 0)
    member = ((at & 255) >> 3) * 2 + (at >> 8)
    err = jnp.where(member == (row >> 2), jnp.broadcast_to(err, (256, 512)), 0.0)
    fit = -(jnp.sum(err, axis=1, keepdims=True) / (256 * D))
    mean = jnp.sum(fit, axis=0, keepdims=True) / 256
    away = fit - mean
    spread = jnp.sum(away * away, axis=0, keepdims=True) / 256
    weight = away / jnp.sqrt(spread + spread_floor)
    me = iota((256, 128), 0) == 4 * (2 * chip + core)
    fit_ref[...] = jnp.sum(jnp.where(me, jnp.broadcast_to(fit, (256, 128)), 0.0), axis=0, keepdims=True)
    left = left_ref[...].astype(F32).reshape(256, 128) * weight
    left = left.reshape(32, 8, 128)
    turned = pltpu.roll(left, 4, 1)
    low = jnp.where(core == 0, left, turned)
    high = jnp.where(core == 0, turned, left)
    upper, narrow = iota((32, 8, 128), 1) < 4, iota((32, 8, 128), 2) < 64
    total = 0.0
    for ref, a, b in ((own_ref, low, high), (other_ref, high, low)):
        l = jnp.where(narrow, jnp.where(upper, a, 0.0), jnp.where(upper, 0.0, b)).reshape(256, 128)
        parts = []
        for _ in range(3):
            parts.append(l.astype(BF16))
            l = l - parts[-1].astype(F32)
        right = ref[...].astype(F32).reshape(256, 896).astype(BF16)
        g = lax.dot_general(jnp.concatenate(parts, axis=1), right, TN, preferred_element_type=F32)
        total = total + g[0:128] + g[128:256] + g[256:384]
    query_ref[...] = total[0:56]
    out_ref[...] = total[64:120]


def loaded(kernel, smem, n_in, n_out):
    def body(*refs):
        scalars, refs = refs[:smem], refs[smem:]
        ins, outs, refs = refs[:n_in], refs[n_in : n_in + n_out], refs[n_in + n_out :]
        held, results, refs = refs[:n_in], refs[n_in : n_in + n_out], refs[n_in + n_out :]
        *rest, sems = refs
        copies = [pltpu.make_async_copy(a, b, sems.at[i]) for i, (a, b) in enumerate(zip(ins, held))]
        for copy in copies:
            copy.start()
        for copy in copies:
            copy.wait()
        kernel(*scalars, *held, *results, *rest)
        copies = [pltpu.make_async_copy(b, a, sems.at[n_in + i]) for i, (a, b) in enumerate(zip(outs, results))]
        for copy in copies:
            copy.start()
        for copy in copies:
            copy.wait()

    return body


def call(kernel, out, args, smem=0, flops=10**9, scratch=(), load=True):
    outs = out if isinstance(out, (list, tuple)) else [out]
    ins = args[smem:]
    scratch = list(scratch)
    if load:
        kernel = loaded(kernel, smem, len(ins), len(outs))
        scratch = [pltpu.VMEM(a.shape, a.dtype) for a in (*ins, *outs)] + scratch
        scratch.append(pltpu.SemaphoreType.DMA((len(ins) + len(outs),)))
    hbm = pl.BlockSpec(memory_space=pltpu.HBM)
    return pl.pallas_call(
        kernel,
        out_shape=out,
        in_specs=[pl.BlockSpec(memory_space=pltpu.SMEM)] * smem + [hbm] * len(ins),
        out_specs=jax.tree.map(lambda _: hbm, out),
        scratch_shapes=scratch,
        cost_estimate=pl.CostEstimate(flops=flops, bytes_accessed=2 * 10**6, transcendentals=0),
    )(*args)


def shape(s, t=BF16):
    return jax.ShapeDtypeStruct(s, t)


def after(x, y):
    return lax.optimization_barrier((x, y))[0]


def ints(*values):
    return jnp.stack([jnp.asarray(v, jnp.int32) for v in values])


PARTS = ((0, 32), (32, 24))


def per_device(
    tokens,
    target,
    w_query,
    w_key,
    w_value,
    w_out,
    query_left_factors,
    query_right_factors,
    o_left,
    o_right,
    member_ids,
):
    tok = tokens.shape[0]
    feats = w_query.shape[1]
    heads = feats // HEAD_DIM
    x, z, c = (lax.axis_index(a) for a in POP)
    y = lax.axis_index("mp")
    k = x * 8 + z
    p = 2 * k + c
    odd = member_ids[0] % 2
    half = jnp.where(odd == 0, 0.5, -0.5).astype(BF16)
    twice = jnp.where(odd == 0, 2.0, -2.0).astype(BF16)
    left_t = query_left_factors[0].T

    sent = call(
        front_kernel,
        shape((32, 8, 1920)),
        (ints(p, odd), tokens, w_query, left_t, query_right_factors[0], o_left[0].T),
        smem=1,
        scratch=[pltpu.VMEM((256, feats), F32)],
    )
    recv = lax.all_to_all(sent, CHIPS, 0, 0, tiled=True)

    w_t, parts = after(w_out.T, sent), []
    by_z = [w_t] + [shift(w_t, "pop_1", 8, e) for e in (1, 2, 3, 4, 5, 6, 7)]
    stacked = call(stack_kernel, [shape((8, high, feats)) for _, high in PARTS], by_z)
    for own in stacked:
        up, down = shift(own, "pop_0", 4, 1), shift(own, "pop_0", 4, 3)
        far = [shift(up[:4], "pop_0", 4, 1), shift(down[4:], "pop_0", 4, 3)]
        parts.append([own, up, down, *far])
    where = ints(c, *[(x + d - y) % 4 for d in (0, -1, 1, 2)], *[(z - e) % 8 for e in range(8)])

    cos_all, sin_all = tables(jnp.arange(tok, dtype=F32), HEAD_DIM)
    k32 = jnp.dot(tokens, w_key, preferred_element_type=F32)
    keys = (k32 * cos_all + jnp.roll(k32, 64, axis=1) * sin_all).astype(BF16)
    values = jnp.dot(tokens, w_value, preferred_element_type=F32).astype(BF16)
    cos8, sin8 = tables((k * 8).astype(F32) + jnp.arange(8, dtype=F32), HEAD_DIM)

    half_base = jnp.sum(recv[:, :, :feats].astype(F32), axis=0)
    mixed = call(
        functools.partial(attention_kernel, heads),
        shape((272, feats)),
        (ints(k * 8), recv, half_base, swap(half_base), keys, values, cos8, sin8),
        smem=1,
    )
    mixed_b = swap(mixed)

    outs = [
        call(
            functools.partial(project_kernel, high),
            [shape((high + 2, 8, 512))] * 4,
            (where, *pieces, mixed, mixed_b),
            smem=1,
            scratch=[
                pltpu.VMEM((4, 8, high, feats), BF16),
                pltpu.VMEM((2, 272, feats), BF16),
                pltpu.VMEM((4, high + 2, 8, 512), BF16),
                pltpu.SemaphoreType.DMA((38,)),
            ],
            load=False,
        )
        for (_, high), pieces in zip(PARTS, parts)
    ]
    mets = []
    for out in outs:
        mets.append([out[0]] + [shift(out[s], "mp", 4, s) for s in (2, 1, 3)])

    def in_parts(a):
        return [a[..., at : at + high].reshape(*a.shape[:-2], 8 * high) for at, high in PARTS]

    o_r = after(o_right[0], mixed)
    o_cut = lax.dynamic_slice(o_r, (0, feats * y), (RANK, feats)).reshape(RANK, 8, 2, 56)
    o_cut = jnp.concatenate(in_parts(jnp.moveaxis(o_cut, 2, 0)), axis=-1) * half
    o_cut = jnp.broadcast_to(o_cut[None], (32, 2, RANK, 448)).reshape(64, RANK, 448)
    cut_q = jnp.moveaxis((after(left_t, mixed) * twice).reshape(RANK, 64, 56), 1, 0)
    cut_o = jnp.moveaxis((o_r * twice).reshape(RANK, 64, 56), 1, 0)
    gap = jnp.zeros((64, RANK, 8), BF16)
    late = jnp.concatenate([cut_q, gap, cut_o, gap, o_cut, jnp.zeros((64, RANK, 64), BF16)], axis=2)
    late = lax.all_to_all(late, POP, 0, 0, tiled=True)
    factors = after(recv, outs[0][0])[:, :, 1024:1920]
    factors_b = swap(factors)
    lefts = late[:, :, :128].reshape(32, 8, 128)
    goal = lax.dynamic_slice(target, (8 * k, 0), (8, feats)).reshape(8, 8, 2, 56)
    goals = in_parts(jnp.where(c == 0, goal[:, :, 0], goal[:, :, 1]))

    err = jnp.zeros((8, 1, 512), F32)
    start = 128
    for (_, high), met, goal in zip(PARTS, mets, goals):
        right = late[:, :, start : start + 8 * high].reshape(256, 8 * high)
        start += 8 * high
        err = call(error_kernel, shape((8, 1, 512), F32), (*met, right, goal, err))

    err = lax.all_to_all(err, ("pop_2", "mp"), 0, 0, tiled=True)
    err = jnp.sum(err, axis=0, keepdims=True)
    err = lax.all_to_all(jnp.broadcast_to(err, (32, 1, 512)), CHIPS, 0, 0, tiled=True)
    grad_query, grad_out, fitness = call(
        final_kernel,
        [shape((56, feats), F32), shape((56, feats), F32), shape((1, 128), F32)],
        (ints(c, k), err, lefts, factors, factors_b),
        smem=1,
    )
    return (grad_query, grad_out.T, fitness[0, :1])


def solution(mesh):
    torus = Mesh(mesh.devices.reshape(4, 8, 2, mesh.shape["mp"]), ("pop_0", "pop_1", "pop_2", "mp"))
    placed = (
        P(),
        P(None, "mp"),
        P(POP, "mp"),
        P(None, "mp"),
        P(None, "mp"),
        P("mp", POP),
        P(POP, None, None),
        P(POP, None, "mp"),
        P(POP, "mp", None),
        P(POP, None, None),
        P(POP),
    )
    return jax.shard_map(
        per_device,
        mesh=torus,
        in_specs=placed,
        out_specs=(P(POP, "mp"), P("mp", POP), P(POP)),
        check_vma=False,
    )
```

profile of v0, /device:TPU:1, one launch (start us, length us, event | category | flops | bytes accessed | tf_op | source)
XLA Modules:
  0.0 167.6 jit_solution(3490684568137706982)
XLA Ops:
  2.0 4.1 %shard_map.130 = bf16[32,8,1920]{2,1,0:T(8,128)(2,1)} custom-call(s32[2]{0:T(128)} %pad_add_fusion.1.refs_0_, bf16[256,3584]{1,0:T(8,128)(2,1)} %refs_1_.1, bf16[56,896]{1,0:T(8,128)(2,1)} %refs_2_.1, bf16[4,3584]{1,0:T(4,128)(2,1)} %bitcast.61, bf16[4,896]{1,0:T(4,128)(2,1)} %bitcast.71, bf16[4,896]{1,0:T(4,128)(2,1)} %bitcast.72), custom_call_target="tpu_custom_call" | custom-call | flops 1000000000 | bytes 2000000 | tf_op jit(solution)/shard_map/pallas_call | solution.py:229
  6.1 12.1 %all-to-all-start = ((bf16[32,8,1920]{2,1,0:T(8,128)(2,1)}), bf16[32,8,1920]{2,1,0:T(8,128)(2,1)}, u32[]{:S(2)}, u32[]{:S(2)}) async-start(bf16[32,8,1920]{2,1,0:T(8,128)(2,1)} %shard_map.130), calls=%async_computation | async-start | bytes 1966080 | tf_op jit(solution)/shard_map/all_to_all | solution.py:286
  18.2 1.2 collective-permute-start
  19.5 2.1 %collective-permute-start.1 = (bf16[56,896]{1,0:T(8,128)(2,1)S(1)}, bf16[56,896]{1,0:T(8,128)(2,1)S(1)}, u32[]{:S(2)}, u32[]{:S(2)}) collective-permute-start(bf16[56,896]{1,0:T(8,128)(2,1)S(1)} %bitcast.65), channel_id=1, source_target_pairs={{0,16},{8,24},{16,32},{24,40},{32,48},{40,56},{48,0},{56,8},{1,17}... | collective-permute-start | bytes 301064 | tf_op jit(solution)/shard_map/ppermute | solution.py:32
  21.5 2.4 %collective-permute-start.2 = (bf16[56,896]{1,0:T(8,128)(2,1)S(1)}, bf16[56,896]{1,0:T(8,128)(2,1)S(1)}, u32[]{:S(2)}, u32[]{:S(2)}) collective-permute-start(bf16[56,896]{1,0:T(8,128)(2,1)S(1)} %bitcast.66), channel_id=1, source_target_pairs={{0,24},{8,32},{16,40},{24,48},{32,56},{40,0},{48,8},{56,16},{1,25}... | collective-permute-start | bytes 301064 | tf_op jit(solution)/shard_map/ppermute | solution.py:32
  23.9 2.1 %collective-permute-start.3 = (bf16[56,896]{1,0:T(8,128)(2,1)S(1)}, bf16[56,896]{1,0:T(8,128)(2,1)}, u32[]{:S(2)}, u32[]{:S(2)}) collective-permute-start(bf16[56,896]{1,0:T(8,128)(2,1)S(1)} %bitcast.67), channel_id=1, source_target_pairs={{0,32},{8,40},{16,48},{24,56},{32,0},{40,8},{48,16},{56,24},{1,33}... | collective-permute-start | bytes 301064 | tf_op jit(solution)/shard_map/ppermute | solution.py:32
  26.0 2.4 %collective-permute-start.4 = (bf16[56,896]{1,0:T(8,128)(2,1)S(1)}, bf16[56,896]{1,0:T(8,128)(2,1)}, u32[]{:S(2)}, u32[]{:S(2)}) collective-permute-start(bf16[56,896]{1,0:T(8,128)(2,1)S(1)} %bitcast.68), channel_id=1, source_target_pairs={{0,40},{8,48},{16,56},{24,0},{32,8},{40,16},{48,24},{56,32},{1,41}... | collective-permute-start | bytes 301064 | tf_op jit(solution)/shard_map/ppermute | solution.py:32
  29.7 1.3 convolution_convert_fusion.refs_5_
  31.0 0.8 fusion.1.refs_4_
  31.7 12.0 %collective-permute-done.refs_1_ = bf16[56,896]{1,0:T(8,128)(2,1)S(1)} collective-permute-done((bf16[56,896]{1,0:T(8,128)(2,1)S(1)}, bf16[56,896]{1,0:T(8,128)(2,1)S(1)}, u32[]{:S(2)}, u32[]{:S(2)}) %collective-permute-start) | collective-permute-done | bytes 100384 | tf_op jit(solution)/shard_map/ppermute | solution.py:32
  43.7 2.1 %collective-permute-start.5 = (bf16[56,896]{1,0:T(8,128)(2,1)S(1)}, bf16[56,896]{1,0:T(8,128)(2,1)S(1)}, u32[]{:S(2)}, u32[]{:S(2)}) collective-permute-start(bf16[56,896]{1,0:T(8,128)(2,1)S(1)} %bitcast.69), channel_id=1, source_target_pairs={{0,48},{8,56},{16,0},{24,8},{32,16},{40,24},{48,32},{56,40},{1,49}... | collective-permute-start | bytes 301064 | tf_op jit(solution)/shard_map/ppermute | solution.py:32
  45.8 2.3 %collective-permute-done.1.refs_2_ = bf16[56,896]{1,0:T(8,128)(2,1)S(1)} collective-permute-done((bf16[56,896]{1,0:T(8,128)(2,1)S(1)}, bf16[56,896]{1,0:T(8,128)(2,1)S(1)}, u32[]{:S(2)}, u32[]{:S(2)}) %collective-permute-start.1) | collective-permute-done | bytes 100384 | tf_op jit(solution)/shard_map/ppermute | solution.py:32
  48.1 0.7 collective-permute-start.6
  48.9 4.4 %collective-permute-done.2.refs_3_ = bf16[56,896]{1,0:T(8,128)(2,1)S(1)} collective-permute-done((bf16[56,896]{1,0:T(8,128)(2,1)S(1)}, bf16[56,896]{1,0:T(8,128)(2,1)S(1)}, u32[]{:S(2)}, u32[]{:S(2)}) %collective-permute-start.2) | collective-permute-done | bytes 100384 | tf_op jit(solution)/shard_map/ppermute | solution.py:32
  53.3 7.4 %collective-permute-done.3.refs_4_ = bf16[56,896]{1,0:T(8,128)(2,1)} collective-permute-done((bf16[56,896]{1,0:T(8,128)(2,1)S(1)}, bf16[56,896]{1,0:T(8,128)(2,1)}, u32[]{:S(2)}, u32[]{:S(2)}) %collective-permute-start.3) | collective-permute-done | bytes 100384 | tf_op jit(solution)/shard_map/ppermute | solution.py:32
  62.0 2.2 %shard_map.131 = (bf16[8,32,896]{2,1,0:T(8,128)(2,1)}, bf16[8,24,896]{2,1,0:T(8,128)(2,1)}) custom-call(bf16[56,896]{1,0:T(8,128)(2,1)} %bitcast.63, bf16[56,896]{1,0:T(8,128)(2,1)} %copy-done.18, bf16[56,896]{1,0:T(8,128)(2,1)} %copy-done.19, bf16[56,896]{1,0:T(8,128)(2,1)} %copy-done.20, bf16[56,896]{1,0:T(8,128)(2,1)} %collective-permute-done.3.refs_4_, ...), custom_call_target="tpu_custom_call" | custom-call | flops 1000000000 | bytes 2000000 | tf_op jit(solution)/shard_map/pallas_call | solution.py:229
  64.2 1.4 collective-permute-start.16
  65.6 1.3 collective-permute-start.17
  67.1 1.1 convert_reduce_fusion.refs_2_
  68.2 1.8 %collective-permute-start.11 = (f32[8,896]{1,0:T(8,128)S(1)}, f32[8,896]{1,0:T(8,128)S(1)}, u32[]{:S(2)}, u32[]{:S(2)}) collective-permute-start(f32[8,896]{1,0:T(8,128)S(1)} %convert_reduce_fusion.refs_2_), channel_id=1, source_target_pairs={{0,4},{4,0},{1,5},{5,1},{2,6},{6,2},{3,7},{7,3},{8,12},{12,8},{9,1... | collective-permute-start | bytes 86024 | tf_op jit(solution)/shard_map/ppermute | solution.py:36
  70.7 1.4 collective-permute-start.8
  72.1 4.5 %collective-permute-done.16.refs_1_ = bf16[8,32,896]{2,1,0:T(8,128)(2,1)S(1)} collective-permute-done((bf16[8,32,896]{2,1,0:T(8,128)(2,1)}, bf16[8,32,896]{2,1,0:T(8,128)(2,1)S(1)}, u32[]{:S(2)}, u32[]{:S(2)}) %collective-permute-start.16) | collective-permute-done | bytes 458784 | tf_op jit(solution)/shard_map/ppermute | solution.py:32
  76.9 2.6 %collective-permute-start.19 = (bf16[4,32,896]{2,1,0:T(8,128)(2,1)S(1)}, bf16[4,32,896]{2,1,0:T(8,128)(2,1)}, u32[]{:S(2)}, u32[]{:S(2)}) collective-permute-start(bf16[4,32,896]{2,1,0:T(8,128)(2,1)S(1)} %slice.86), channel_id=1, source_target_pairs={{0,192},{64,0},{128,64},{192,128},{1,193},{65,1},{129,65},{193,129... | collective-permute-start | bytes 688136 | tf_op jit(solution)/shard_map/ppermute | solution.py:32
  80.2 5.3 %shard_map.132.refs_5_ = bf16[272,896]{1,0:T(8,128)(2,1)} custom-call(s32[1]{0:T(128)} %bitcast.23.refs_0_, bf16[32,8,1920]{2,1,0:T(8,128)(2,1)} %all-to-all-done.refs_1_, f32[8,896]{1,0:T(8,128)} %copy-done.11, f32[8,896]{1,0:T(8,128)} %copy-done.23, bf16[256,128]{1,0:T(8,128)(2,1)} %fusion.1.refs_4_, bf16[256,128]{1,0:T(8,128)(2,1)} %convolution_convert_fusion.refs_5_, ...), custom_call_target="tpu_custom_call" | custom-call | flops 1000000000 | bytes 2000000 | tf_op jit(solution)/shard_map/pallas_call | solution.py:229
  85.5 4.2 %collective-permute-start.12 = (bf16[272,896]{1,0:T(8,128)(2,1)}, bf16[272,896]{1,0:T(8,128)(2,1)}, u32[]{:S(2)}, u32[]{:S(2)}) collective-permute-start(bf16[272,896]{1,0:T(8,128)(2,1)} %shard_map.132.refs_5_), channel_id=1, source_target_pairs={{0,4},{4,0},{1,5},{5,1},{2,6},{6,2},{3,7},{7,3},{8,12},{12,8},{9,1... | collective-permute-start | bytes 1462280 | tf_op jit(solution)/shard_map/ppermute | solution.py:36
  90.7 1.3 concatenate.38
  92.1 4.2 %all-to-all-start.1 = ((bf16[64,4,640]{2,1,0:T(4,128)(2,1)}), bf16[64,4,640]{2,1,0:T(4,128)(2,1)S(1)}, u32[]{:S(2)}, u32[]{:S(2)}) async-start(bf16[64,4,640]{2,1,0:T(4,128)(2,1)} %concatenate.38), calls=%async_computation.1 | async-start | bytes 655360 | tf_op jit(solution)/shard_map/all_to_all | solution.py:343
  97.1 4.9 %shard_map.134 = (bf16[34,8,512]{2,1,0:T(8,128)(2,1)}, bf16[34,8,512]{2,1,0:T(8,128)(2,1)}, bf16[34,8,512]{2,1,0:T(8,128)(2,1)}, bf16[34,8,512]{2,1,0:T(8,128)(2,1)}) custom-call(s32[13]{0:T(128)} %stack.76.where_ref, bf16[8,32,896]{2,1,0:T(8,128)(2,1)} %get-tuple-element.28.refs_0_, bf16[8,32,896]{2,1,0:T(8,128)(2,1)} %copy-done.4, ...), custom_call_target="tpu_custom_call" | custom-call | flops 1000000000 | bytes 2000000 | tf_op jit(solution)/shard_map/pallas_call | solution.py:229
  102.0 3.0 %collective-permute-start.20 = (bf16[34,8,512]{2,1,0:T(8,128)(2,1)}, bf16[34,8,512]{2,1,0:T(8,128)(2,1)}, u32[]{:S(2)}, u32[]{:S(2)}) collective-permute-start(bf16[34,8,512]{2,1,0:T(8,128)(2,1)} %get-tuple-element.30), channel_id=1, source_target_pairs={{0,2},{1,3},{2,0},{3,1},{4,6},{5,7},{6,4},{7,5},{8,10},{9,11},{10,... | collective-permute-start | bytes 835592 | tf_op jit(solution)/shard_map/ppermute | solution.py:32
  105.4 2.9 %collective-permute-start.10 = (bf16[4,24,896]{2,1,0:T(8,128)(2,1)S(1)}, bf16[4,24,896]{2,1,0:T(8,128)(2,1)S(1)}, u32[]{:S(2)}, u32[]{:S(2)}) collective-permute-start(bf16[4,24,896]{2,1,0:T(8,128)(2,1)S(1)} %slice.75), channel_id=1, source_target_pairs={{0,192},{64,0},{128,64},{192,128},{1,193},{65,1},{129,65},{193,129... | collective-permute-start | bytes 516104 | tf_op jit(solution)/shard_map/ppermute | solution.py:32
  108.4 0.7 constant_dynamic-slice_fusion
  109.2 1.1 slice.72.refs_3_
  110.3 1.4 collective-permute-start.23
  111.7 2.3 %collective-permute-start.22 = (bf16[34,8,512]{2,1,0:T(8,128)(2,1)}, bf16[34,8,512]{2,1,0:T(8,128)(2,1)}, u32[]{:S(2)}, u32[]{:S(2)}) collective-permute-start(bf16[34,8,512]{2,1,0:T(8,128)(2,1)} %get-tuple-element.32), channel_id=1, source_target_pairs={{0,3},{1,0},{2,1},{3,2},{4,7},{5,4},{6,5},{7,6},{8,11},{9,8},{10,9... | collective-permute-start | bytes 835592 | tf_op jit(solution)/shard_map/ppermute | solution.py:32
  114.4 4.8 %shard_map.133 = (bf16[26,8,512]{2,1,0:T(8,128)(2,1)}, bf16[26,8,512]{2,1,0:T(8,128)(2,1)}, bf16[26,8,512]{2,1,0:T(8,128)(2,1)}, bf16[26,8,512]{2,1,0:T(8,128)(2,1)}) custom-call(s32[13]{0:T(128)} %stack.76.where_ref, bf16[8,24,896]{2,1,0:T(8,128)(2,1)} %get-tuple-element.21.refs_0_, bf16[8,24,896]{2,1,0:T(8,128)(2,1)} %copy-done.7, ...), custom_call_target="tpu_custom_call" | custom-call | flops 1000000000 | bytes 2000000 | tf_op jit(solution)/shard_map/pallas_call | solution.py:229
  119.2 1.6 collective-permute-start.13
  120.8 1.3 collective-permute-start.14
  122.1 1.4 collective-permute-start.15
  123.7 0.7 reshape.79.refs_5_
  125.1 0.7 reshape.78.refs_4_
  125.8 0.7 reshape.75.refs_4_
  127.2 2.5 %shard_map.135.refs_6_ = f32[8,1,512]{2,1,0:T(1,128)} custom-call(bf16[34,8,512]{2,1,0:T(8,128)(2,1)} %get-tuple-element.29.refs_0_, bf16[34,8,512]{2,1,0:T(8,128)(2,1)} %collective-permute-done.20.refs_1_, bf16[34,8,512]{2,1,0:T(8,128)(2,1)} %collective-permute-done.21.refs_2_, bf16[34,8,512]{2,1,0:T(8,128)(2,1)} %collective-permute-done.22.refs_3_, ...), custom_call_target="tpu_custom_call" | custom-call | flops 1000000000 | bytes 2000000 | tf_op jit(solution)/shard_map/pallas_call | solution.py:229
  129.7 2.1 %collective-permute-done.14.refs_2_ = bf16[26,8,512]{2,1,0:T(8,128)(2,1)S(1)} collective-permute-done((bf16[26,8,512]{2,1,0:T(8,128)(2,1)}, bf16[26,8,512]{2,1,0:T(8,128)(2,1)S(1)}, u32[]{:S(2)}, u32[]{:S(2)}) %collective-permute-start.14) | collective-permute-done | bytes 213024 | tf_op jit(solution)/shard_map/ppermute | solution.py:32
  132.5 2.5 %shard_map.136 = f32[8,1,512]{2,1,0:T(1,128)} custom-call(bf16[26,8,512]{2,1,0:T(8,128)(2,1)} %get-tuple-element.22.refs_0_, bf16[26,8,512]{2,1,0:T(8,128)(2,1)} %copy-done.13, bf16[26,8,512]{2,1,0:T(8,128)(2,1)} %copy-done.14, bf16[26,8,512]{2,1,0:T(8,128)(2,1)} %copy-done.15, bf16[256,192]{1,0:T(8,128)(2,1)} %reshape.75.refs_4_, ...), custom_call_target="tpu_custom_call" | custom-call | flops 1000000000 | bytes 2000000 | tf_op jit(solution)/shard_map/pallas_call | solution.py:229
  135.0 10.1 %all_to_all.20 = f32[8,1,512]{2,1,0:T(1,128)S(1)} all-to-all(f32[8,1,512]{2,1,0:T(1,128)} %shard_map.136), channel_id=1, replica_groups=mesh['pop_0'=4,'pop_1'=8,'pop_2'=2,'mp'=4] {'pop_2','mp'}, dimensions={0} | all-to-all | bytes 32768 | tf_op jit(solution)/shard_map/all_to_all | solution.py:357
  145.9 8.3 %all-to-all-start.3 = ((f32[32,1,512]{2,1,0:T(1,128)}), f32[32,1,512]{2,1,0:T(1,128)S(1)}, u32[]{:S(2)}, u32[]{:S(2)}) async-start(f32[32,1,512]{2,1,0:T(1,128)} %broadcast_in_dim.14), calls=%async_computation.3 | async-start | bytes 131072 | tf_op jit(solution)/shard_map/all_to_all | solution.py:359
  155.5 7.6 %all-to-all-done.3.refs_1_ = f32[32,1,512]{2,1,0:T(1,128)S(1)} async-done(((f32[32,1,512]{2,1,0:T(1,128)}), f32[32,1,512]{2,1,0:T(1,128)S(1)}, u32[]{:S(2)}, u32[]{:S(2)}) %all-to-all-start.3) | async-done | bytes 65568 | tf_op jit(solution)/shard_map/all_to_all | solution.py:359
  163.9 3.5 %shard_map.137 = (f32[56,896]{1,0:T(8,128)}, f32[56,896]{1,0:T(8,128)}, f32[1,128]{1,0:T(1,128)}) custom-call(s32[2]{0:T(128)} %pad_add_fusion.refs_0_, f32[32,1,512]{2,1,0:T(1,128)} %copy-done.8, bf16[32,8,128]{2,1,0:T(8,128)(2,1)} %bitcast.58, bf16[32,8,896]{2,1,0:T(8,128)(2,1)} %copy-done.3, bf16[32,8,896]{2,1,0:T(8,128)(2,1)} %copy-done.12), custom_call_target="tpu_custom_call" | custom-call | flops 1000000000 | bytes 2000000 | tf_op jit(solution)/shard_map/pallas_call | solution.py:229
  (114 shorter events, 12.6 us)
Async XLA Ops:
  0.6 27.8 %copy-start = (bf16[3584,128]{1,0:T(8,128)(2,1)S(1)}, bf16[3584,128]{1,0:T(8,128)(2,1)}, u32[]{:S(2)}) copy-start(bf16[3584,128]{1,0:T(8,128)(2,1)} %param.14) | copy-start | bytes 2752516
  6.1 12.2 %copy-start.17 = (bf16[896,56]{0,1:T(8,128)(2,1)S(1)}, bf16[896,56]{0,1:T(8,128)(2,1)}, u32[]{:S(2)}) copy-start(bf16[896,56]{0,1:T(8,128)(2,1)} %param.16) | copy-start | bytes 301060
  6.1 22.4 %copy-start.1 = (bf16[256,3584]{1,0:T(8,128)(2,1)S(1)}, bf16[256,3584]{1,0:T(8,128)(2,1)}, u32[]{:S(2)}) copy-start(bf16[256,3584]{1,0:T(8,128)(2,1)} %refs_1_.1) | copy-start | bytes 5505028
  6.1 61.0 %all-to-all-start = ((bf16[32,8,1920]{2,1,0:T(8,128)(2,1)}), bf16[32,8,1920]{2,1,0:T(8,128)(2,1)}, u32[]{:S(2)}, u32[]{:S(2)}) async-start(bf16[32,8,1920]{2,1,0:T(8,128)(2,1)} %shard_map.130), calls=%async_computation | async-start | bytes 1966080 | tf_op jit(solution)/shard_map/all_to_all | solution.py:286
  18.2 25.5 %collective-permute-start = (bf16[56,896]{1,0:T(8,128)(2,1)S(1)}, bf16[56,896]{1,0:T(8,128)(2,1)S(1)}, u32[]{:S(2)}, u32[]{:S(2)}) collective-permute-start(bf16[56,896]{1,0:T(8,128)(2,1)S(1)} %bitcast.64), channel_id=1, source_target_pairs={{0,8},{8,16},{16,24},{24,32},{32,40},{40,48},{48,56},{56,0},{1,9},... | collective-permute-start | bytes 301064 | tf_op jit(solution)/shard_map/ppermute | solution.py:32
  19.5 28.7 %collective-permute-start.1 = (bf16[56,896]{1,0:T(8,128)(2,1)S(1)}, bf16[56,896]{1,0:T(8,128)(2,1)S(1)}, u32[]{:S(2)}, u32[]{:S(2)}) collective-permute-start(bf16[56,896]{1,0:T(8,128)(2,1)S(1)} %bitcast.65), channel_id=1, source_target_pairs={{0,16},{8,24},{16,32},{24,40},{32,48},{40,56},{48,0},{56,8},{1,17}... | collective-permute-start | bytes 301064 | tf_op jit(solution)/shard_map/ppermute | solution.py:32
  21.5 31.7 %collective-permute-start.2 = (bf16[56,896]{1,0:T(8,128)(2,1)S(1)}, bf16[56,896]{1,0:T(8,128)(2,1)S(1)}, u32[]{:S(2)}, u32[]{:S(2)}) collective-permute-start(bf16[56,896]{1,0:T(8,128)(2,1)S(1)} %bitcast.66), channel_id=1, source_target_pairs={{0,24},{8,32},{16,40},{24,48},{32,56},{40,0},{48,8},{56,16},{1,25}... | collective-permute-start | bytes 301064 | tf_op jit(solution)/shard_map/ppermute | solution.py:32
  23.9 36.8 %collective-permute-start.3 = (bf16[56,896]{1,0:T(8,128)(2,1)S(1)}, bf16[56,896]{1,0:T(8,128)(2,1)}, u32[]{:S(2)}, u32[]{:S(2)}) collective-permute-start(bf16[56,896]{1,0:T(8,128)(2,1)S(1)} %bitcast.67), channel_id=1, source_target_pairs={{0,32},{8,40},{16,48},{24,56},{32,0},{40,8},{48,16},{56,24},{1,33}... | collective-permute-start | bytes 301064 | tf_op jit(solution)/shard_map/ppermute | solution.py:32
  26.0 34.7 %collective-permute-start.4 = (bf16[56,896]{1,0:T(8,128)(2,1)S(1)}, bf16[56,896]{1,0:T(8,128)(2,1)}, u32[]{:S(2)}, u32[]{:S(2)}) collective-permute-start(bf16[56,896]{1,0:T(8,128)(2,1)S(1)} %bitcast.68), channel_id=1, source_target_pairs={{0,40},{8,48},{16,56},{24,0},{32,8},{40,16},{48,24},{56,32},{1,41}... | collective-permute-start | bytes 301064 | tf_op jit(solution)/shard_map/ppermute | solution.py:32
  28.4 1.3 copy-start.2
  43.7 17.0 %copy-start.18 = (bf16[56,896]{1,0:T(8,128)(2,1)}, bf16[56,896]{1,0:T(8,128)(2,1)S(1)}, u32[]{:S(2)}) copy-start(bf16[56,896]{1,0:T(8,128)(2,1)S(1)} %collective-permute-done.refs_1_) | copy-start | bytes 301060
  43.7 17.0 %collective-permute-start.5 = (bf16[56,896]{1,0:T(8,128)(2,1)S(1)}, bf16[56,896]{1,0:T(8,128)(2,1)S(1)}, u32[]{:S(2)}, u32[]{:S(2)}) collective-permute-start(bf16[56,896]{1,0:T(8,128)(2,1)S(1)} %bitcast.69), channel_id=1, source_target_pairs={{0,48},{8,56},{16,0},{24,8},{32,16},{40,24},{48,32},{56,40},{1,49}... | collective-permute-start | bytes 301064 | tf_op jit(solution)/shard_map/ppermute | solution.py:32
  48.1 12.6 %copy-start.19 = (bf16[56,896]{1,0:T(8,128)(2,1)}, bf16[56,896]{1,0:T(8,128)(2,1)S(1)}, u32[]{:S(2)}) copy-start(bf16[56,896]{1,0:T(8,128)(2,1)S(1)} %collective-permute-done.1.refs_2_) | copy-start | bytes 301060
  48.1 12.6 %collective-permute-start.6 = (bf16[56,896]{1,0:T(8,128)(2,1)S(1)}, bf16[56,896]{1,0:T(8,128)(2,1)S(1)}, u32[]{:S(2)}, u32[]{:S(2)}) collective-permute-start(bf16[56,896]{1,0:T(8,128)(2,1)S(1)} %bitcast.70), channel_id=1, source_target_pairs={{0,56},{8,0},{16,8},{24,16},{32,24},{40,32},{48,40},{56,48},{1,57}... | collective-permute-start | bytes 301064 | tf_op jit(solution)/shard_map/ppermute | solution.py:32
  53.3 7.5 %copy-start.20 = (bf16[56,896]{1,0:T(8,128)(2,1)}, bf16[56,896]{1,0:T(8,128)(2,1)S(1)}, u32[]{:S(2)}) copy-start(bf16[56,896]{1,0:T(8,128)(2,1)S(1)} %collective-permute-done.2.refs_3_) | copy-start | bytes 301060
  60.7 0.6 copy-start.21
  64.2 12.4 %collective-permute-start.16 = (bf16[8,32,896]{2,1,0:T(8,128)(2,1)}, bf16[8,32,896]{2,1,0:T(8,128)(2,1)S(1)}, u32[]{:S(2)}, u32[]{:S(2)}) collective-permute-start(bf16[8,32,896]{2,1,0:T(8,128)(2,1)} %get-tuple-element.28.refs_0_), channel_id=1, source_target_pairs={{0,64},{64,128},{128,192},{192,0},{1,65},{65,129},{129,193},{193,1... | collective-permute-start | bytes 1376264 | tf_op jit(solution)/shard_map/ppermute | solution.py:32
  65.6 11.3 %collective-permute-start.17 = (bf16[8,32,896]{2,1,0:T(8,128)(2,1)}, bf16[8,32,896]{2,1,0:T(8,128)(2,1)S(1)}, u32[]{:S(2)}, u32[]{:S(2)}) collective-permute-start(bf16[8,32,896]{2,1,0:T(8,128)(2,1)} %get-tuple-element.28.refs_0_), channel_id=1, source_target_pairs={{0,192},{64,0},{128,64},{192,128},{1,193},{65,1},{129,65},{193,129... | collective-permute-start | bytes 1376264 | tf_op jit(solution)/shard_map/ppermute | solution.py:32
  68.2 11.4 %copy-start.11 = (f32[8,896]{1,0:T(8,128)}, f32[8,896]{1,0:T(8,128)S(1)}, u32[]{:S(2)}) copy-start(f32[8,896]{1,0:T(8,128)S(1)} %convert_reduce_fusion.refs_2_) | copy-start | bytes 86020
  68.2 11.3 %collective-permute-start.11 = (f32[8,896]{1,0:T(8,128)S(1)}, f32[8,896]{1,0:T(8,128)S(1)}, u32[]{:S(2)}, u32[]{:S(2)}) collective-permute-start(f32[8,896]{1,0:T(8,128)S(1)} %convert_reduce_fusion.refs_2_), channel_id=1, source_target_pairs={{0,4},{4,0},{1,5},{5,1},{2,6},{6,2},{3,7},{7,3},{8,12},{12,8},{9,1... | collective-permute-start | bytes 86024 | tf_op jit(solution)/shard_map/ppermute | solution.py:36
  70.7 34.7 %collective-permute-start.8 = (bf16[8,24,896]{2,1,0:T(8,128)(2,1)}, bf16[8,24,896]{2,1,0:T(8,128)(2,1)S(1)}, u32[]{:S(2)}, u32[]{:S(2)}) collective-permute-start(bf16[8,24,896]{2,1,0:T(8,128)(2,1)} %get-tuple-element.21.refs_0_), channel_id=1, source_target_pairs={{0,192},{64,0},{128,64},{192,128},{1,193},{65,1},{129,65},{193,129... | collective-permute-start | bytes 1032200 | tf_op jit(solution)/shard_map/ppermute | solution.py:32
  72.0 36.2 %collective-permute-start.7 = (bf16[8,24,896]{2,1,0:T(8,128)(2,1)}, bf16[8,24,896]{2,1,0:T(8,128)(2,1)S(1)}, u32[]{:S(2)}, u32[]{:S(2)}) collective-permute-start(bf16[8,24,896]{2,1,0:T(8,128)(2,1)} %get-tuple-element.21.refs_0_), channel_id=1, source_target_pairs={{0,64},{64,128},{128,192},{192,0},{1,65},{65,129},{129,193},{193,1... | collective-permute-start | bytes 1032200 | tf_op jit(solution)/shard_map/ppermute | solution.py:32
  76.7 8.8 %copy-start.4 = (bf16[8,32,896]{2,1,0:T(8,128)(2,1)}, bf16[8,32,896]{2,1,0:T(8,128)(2,1)S(1)}, u32[]{:S(2)}) copy-start(bf16[8,32,896]{2,1,0:T(8,128)(2,1)S(1)} %collective-permute-done.16.refs_1_) | copy-start | bytes 1376260
  76.7 20.4 %collective-permute-start.18 = (bf16[4,32,896]{2,1,0:T(8,128)(2,1)S(1)}, bf16[4,32,896]{2,1,0:T(8,128)(2,1)}, u32[]{:S(2)}, u32[]{:S(2)}) collective-permute-start(bf16[4,32,896]{2,1,0:T(8,128)(2,1)S(1)} %slice.85), channel_id=1, source_target_pairs={{0,64},{64,128},{128,192},{192,0},{1,65},{65,129},{129,193},{193,1... | collective-permute-start | bytes 688136 | tf_op jit(solution)/shard_map/ppermute | solution.py:32
  76.9 8.5 %copy-start.5 = (bf16[8,32,896]{2,1,0:T(8,128)(2,1)}, bf16[8,32,896]{2,1,0:T(8,128)(2,1)S(1)}, u32[]{:S(2)}) copy-start(bf16[8,32,896]{2,1,0:T(8,128)(2,1)S(1)} %collective-permute-done.17.refs_2_) | copy-start | bytes 1376260
  76.9 20.2 %collective-permute-start.19 = (bf16[4,32,896]{2,1,0:T(8,128)(2,1)S(1)}, bf16[4,32,896]{2,1,0:T(8,128)(2,1)}, u32[]{:S(2)}, u32[]{:S(2)}) collective-permute-start(bf16[4,32,896]{2,1,0:T(8,128)(2,1)S(1)} %slice.86), channel_id=1, source_target_pairs={{0,192},{64,0},{128,64},{192,128},{1,193},{65,1},{129,65},{193,129... | collective-permute-start | bytes 688136 | tf_op jit(solution)/shard_map/ppermute | solution.py:32
  80.2 9.5 %copy-start.10 = (bf16[1,3584,4]{1,2,0:T(4,128)(2,1)S(1)}, bf16[1,3584,4]{1,2,0:T(4,128)(2,1)}, u32[]{:S(2)}) copy-start(bf16[1,3584,4]{1,2,0:T(4,128)(2,1)} %param.17) | copy-start | bytes 86020
  80.2 9.6 %copy-start.9 = (bf16[1,4,3584]{2,1,0:T(4,128)(2,1)S(1)}, bf16[1,4,3584]{2,1,0:T(4,128)(2,1)}, u32[]{:S(2)}) copy-start(bf16[1,4,3584]{2,1,0:T(4,128)(2,1)} %param.20) | copy-start | bytes 86020
  85.5 11.6 %collective-permute-start.12 = (bf16[272,896]{1,0:T(8,128)(2,1)}, bf16[272,896]{1,0:T(8,128)(2,1)}, u32[]{:S(2)}, u32[]{:S(2)}) collective-permute-start(bf16[272,896]{1,0:T(8,128)(2,1)} %shard_map.132.refs_5_), channel_id=1, source_target_pairs={{0,4},{4,0},{1,5},{5,1},{2,6},{6,2},{3,7},{7,3},{8,12},{12,8},{9,1... | collective-permute-start | bytes 1462280 | tf_op jit(solution)/shard_map/ppermute | solution.py:36
  92.1 33.0 %all-to-all-start.1 = ((bf16[64,4,640]{2,1,0:T(4,128)(2,1)}), bf16[64,4,640]{2,1,0:T(4,128)(2,1)S(1)}, u32[]{:S(2)}, u32[]{:S(2)}) async-start(bf16[64,4,640]{2,1,0:T(4,128)(2,1)} %concatenate.38), calls=%async_computation.1 | async-start | bytes 655360 | tf_op jit(solution)/shard_map/all_to_all | solution.py:343
  102.0 18.8 %collective-permute-start.20 = (bf16[34,8,512]{2,1,0:T(8,128)(2,1)}, bf16[34,8,512]{2,1,0:T(8,128)(2,1)}, u32[]{:S(2)}, u32[]{:S(2)}) collective-permute-start(bf16[34,8,512]{2,1,0:T(8,128)(2,1)} %get-tuple-element.30), channel_id=1, source_target_pairs={{0,2},{1,3},{2,0},{3,1},{4,6},{5,7},{6,4},{7,5},{8,10},{9,11},{10,... | collective-permute-start | bytes 835592 | tf_op jit(solution)/shard_map/ppermute | solution.py:32
  105.0 17.2 %collective-permute-start.21 = (bf16[34,8,512]{2,1,0:T(8,128)(2,1)}, bf16[34,8,512]{2,1,0:T(8,128)(2,1)}, u32[]{:S(2)}, u32[]{:S(2)}) collective-permute-start(bf16[34,8,512]{2,1,0:T(8,128)(2,1)} %get-tuple-element.31), channel_id=1, source_target_pairs={{0,1},{1,2},{2,3},{3,0},{4,5},{5,6},{6,7},{7,4},{8,9},{9,10},{10,1... | collective-permute-start | bytes 835592 | tf_op jit(solution)/shard_map/ppermute | solution.py:32
  105.4 9.0 %copy-start.6 = (bf16[8,24,896]{2,1,0:T(8,128)(2,1)}, bf16[8,24,896]{2,1,0:T(8,128)(2,1)S(1)}, u32[]{:S(2)}) copy-start(bf16[8,24,896]{2,1,0:T(8,128)(2,1)S(1)} %collective-permute-done.8.refs_2_) | copy-start | bytes 1032196
  105.4 6.2 %collective-permute-start.10 = (bf16[4,24,896]{2,1,0:T(8,128)(2,1)S(1)}, bf16[4,24,896]{2,1,0:T(8,128)(2,1)S(1)}, u32[]{:S(2)}, u32[]{:S(2)}) collective-permute-start(bf16[4,24,896]{2,1,0:T(8,128)(2,1)S(1)} %slice.75), channel_id=1, source_target_pairs={{0,192},{64,0},{128,64},{192,128},{1,193},{65,1},{129,65},{193,129... | collective-permute-start | bytes 516104 | tf_op jit(solution)/shard_map/ppermute | solution.py:32
  108.3 6.1 %copy-start.7 = (bf16[8,24,896]{2,1,0:T(8,128)(2,1)}, bf16[8,24,896]{2,1,0:T(8,128)(2,1)S(1)}, u32[]{:S(2)}) copy-start(bf16[8,24,896]{2,1,0:T(8,128)(2,1)S(1)} %collective-permute-done.7.refs_1_) | copy-start | bytes 1032196
  108.3 6.1 %collective-permute-start.9 = (bf16[4,24,896]{2,1,0:T(8,128)(2,1)S(1)}, bf16[4,24,896]{2,1,0:T(8,128)(2,1)}, u32[]{:S(2)}, u32[]{:S(2)}) collective-permute-start(bf16[4,24,896]{2,1,0:T(8,128)(2,1)S(1)} %slice.74), channel_id=1, source_target_pairs={{0,64},{64,128},{128,192},{192,0},{1,65},{65,129},{129,193},{193,1... | collective-permute-start | bytes 516104 | tf_op jit(solution)/shard_map/ppermute | solution.py:32
  110.3 8.9 %copy-start.3 = (bf16[32,8,896]{2,1,0:T(8,128)(2,1)}, bf16[32,8,896]{2,1,0:T(8,128)(2,1)S(1)}, u32[]{:S(2)}) copy-start(bf16[32,8,896]{2,1,0:T(8,128)(2,1)S(1)} %slice.72.refs_3_) | copy-start | bytes 1376260
  110.3 52.7 %collective-permute-start.23 = (bf16[32,8,896]{2,1,0:T(8,128)(2,1)S(1)}, bf16[32,8,896]{2,1,0:T(8,128)(2,1)S(1)}, u32[]{:S(2)}, u32[]{:S(2)}) collective-permute-start(bf16[32,8,896]{2,1,0:T(8,128)(2,1)S(1)} %slice.72.refs_3_), channel_id=1, source_target_pairs={{0,4},{4,0},{1,5},{5,1},{2,6},{6,2},{3,7},{7,3},{8,12},{12,8},{9,1... | collective-permute-start | bytes 1376264 | tf_op jit(solution)/shard_map/ppermute | solution.py:36
  111.7 2.7 %copy-start.16 = (bf16[4,24,896]{2,1,0:T(8,128)(2,1)}, bf16[4,24,896]{2,1,0:T(8,128)(2,1)S(1)}, u32[]{:S(2)}) copy-start(bf16[4,24,896]{2,1,0:T(8,128)(2,1)S(1)} %collective-permute-done.10.refs_4_) | copy-start | bytes 516100
  111.7 14.9 %collective-permute-start.22 = (bf16[34,8,512]{2,1,0:T(8,128)(2,1)}, bf16[34,8,512]{2,1,0:T(8,128)(2,1)}, u32[]{:S(2)}, u32[]{:S(2)}) collective-permute-start(bf16[34,8,512]{2,1,0:T(8,128)(2,1)} %get-tuple-element.32), channel_id=1, source_target_pairs={{0,3},{1,0},{2,1},{3,2},{4,7},{5,4},{6,5},{7,6},{8,11},{9,8},{10,9... | collective-permute-start | bytes 835592 | tf_op jit(solution)/shard_map/ppermute | solution.py:32
  119.2 10.5 %collective-permute-start.13 = (bf16[26,8,512]{2,1,0:T(8,128)(2,1)}, bf16[26,8,512]{2,1,0:T(8,128)(2,1)S(1)}, u32[]{:S(2)}, u32[]{:S(2)}) collective-permute-start(bf16[26,8,512]{2,1,0:T(8,128)(2,1)} %get-tuple-element.23), channel_id=1, source_target_pairs={{0,2},{1,3},{2,0},{3,1},{4,6},{5,7},{6,4},{7,5},{8,10},{9,11},{10,... | collective-permute-start | bytes 638984 | tf_op jit(solution)/shard_map/ppermute | solution.py:32
  120.8 10.9 %collective-permute-start.14 = (bf16[26,8,512]{2,1,0:T(8,128)(2,1)}, bf16[26,8,512]{2,1,0:T(8,128)(2,1)S(1)}, u32[]{:S(2)}, u32[]{:S(2)}) collective-permute-start(bf16[26,8,512]{2,1,0:T(8,128)(2,1)} %get-tuple-element.24), channel_id=1, source_target_pairs={{0,1},{1,2},{2,3},{3,0},{4,5},{5,6},{6,7},{7,4},{8,9},{9,10},{10,1... | collective-permute-start | bytes 638984 | tf_op jit(solution)/shard_map/ppermute | solution.py:32
  122.1 9.6 %collective-permute-start.15 = (bf16[26,8,512]{2,1,0:T(8,128)(2,1)}, bf16[26,8,512]{2,1,0:T(8,128)(2,1)S(1)}, u32[]{:S(2)}, u32[]{:S(2)}) collective-permute-start(bf16[26,8,512]{2,1,0:T(8,128)(2,1)} %get-tuple-element.25), channel_id=1, source_target_pairs={{0,3},{1,0},{2,1},{3,2},{4,7},{5,4},{6,5},{7,6},{8,11},{9,8},{10,9... | collective-permute-start | bytes 638984 | tf_op jit(solution)/shard_map/ppermute | solution.py:32
  129.7 2.1 %copy-start.13 = (bf16[26,8,512]{2,1,0:T(8,128)(2,1)}, bf16[26,8,512]{2,1,0:T(8,128)(2,1)S(1)}, u32[]{:S(2)}) copy-start(bf16[26,8,512]{2,1,0:T(8,128)(2,1)S(1)} %collective-permute-done.13.refs_1_) | copy-start | bytes 638980
  131.8 0.7 copy-start.14
  131.8 0.8 copy-start.15
  145.9 17.2 %all-to-all-start.3 = ((f32[32,1,512]{2,1,0:T(1,128)}), f32[32,1,512]{2,1,0:T(1,128)S(1)}, u32[]{:S(2)}, u32[]{:S(2)}) async-start(f32[32,1,512]{2,1,0:T(1,128)} %broadcast_in_dim.14), calls=%async_computation.3 | async-start | bytes 131072 | tf_op jit(solution)/shard_map/all_to_all | solution.py:359
  163.0 0.8 copy-start.12
  (3 other events, 1.9 us)
where the time goes:
time: 168 us
  starting transfers between devices  65 us (39%)
  waiting for transfers between devices  40.7 us (24%)
  Pallas kernels  29.8 us (18%)
  local copies, waits for them, and re-layouts  13.3 us (8%)
  blocking collectives  10.1 us (6%)
  other arithmetic  4.56 us (3%)
  between operations  2.26 us (1%)
  matrix products  1.88 us (1%)
    ppermute x21, waiting for transfers between devices, shift(): return lax.ppermute(x, axis, [(i, (i + step) % size) for i in range(size)])  33.2 us
    ppermute x21, starting transfers between devices, shift(): return lax.ppermute(x, axis, [(i, (i + step) % size) for i in range(size)])  33 us
    pallas_call x8, Pallas kernels, call(): pl.pallas_call(kernel, out_shape=out, in_specs=[pl.BlockSpec(memory_space...  29.8 us
    all_to_all x1, starting transfers between devices, per_device(): recv = lax.all_to_all(sent, CHIPS, 0, 0, tiled=True)  12.1 us
    all_to_all x1, blocking collectives, per_device(): err = lax.all_to_all(err, ('pop_2', 'mp'), 0, 0, tiled=True)  10.1 us
    all_to_all x1, starting transfers between devices, per_device(): lax.all_to_all(jnp.broadcast_to(err, (32, 1, 512)), CHIPS, 0, 0, tiled=True)  8.31 us
    all_to_all x1, waiting for transfers between devices, per_device(): lax.all_to_all(jnp.broadcast_to(err, (32, 1, 512)), CHIPS, 0, 0, tiled=True)  7.55 us
    ppermute x3, starting transfers between devices, swap(): return lax.ppermute(x, 'pop_2', [(0, 1), (1, 0)])  7.39 us
  transfers between devices with their start and end apart: 27, of which 8 were waited for; matrix products, arithmetic and copies ran while one was open for 9% of the time, Pallas kernels for 13%

commit v1 on v0

--- a/solution.py
+++ b/solution.py
@@ -99,31 +99,35 @@
 
 
 def stack_kernel(*refs):
-    for e in range(8):
-        for (at, high), out_ref in zip(PARTS, refs[8:]):
-            out_ref[e] = refs[e][at : at + high]
-
-
-def project_kernel(high, where_ref, *refs):
+    *ins, out_ref = refs
+    for e in range(out_ref.shape[0] - 1):
+        out_ref[e] = ins[e][...]
+    at = 0
+    for ref in ins[out_ref.shape[0] - 1 :]:
+        out_ref[out_ref.shape[0] - 1, at : at + ref.shape[0]] = ref[...]
+        at += ref.shape[0]
+
+
+def project_kernel(where_ref, *refs):
     pieces, (own_ref, other_ref), out_refs = refs[:5], refs[5:7], refs[7:11]
     w_ref, mixed_ref, hold_ref, sems = refs[11:]
+    groups = 7 * w_ref.shape[1]
     copies = []
-    for d in range(4):
-        for e in range(8):
-            piece = pieces[d].at[e] if d < 3 else pieces[3 + e // 4].at[e % 4]
-            place = w_ref.at[where_ref[1 + d], where_ref[5 + e]]
-            copies.append(pltpu.make_async_copy(piece, place, sems.at[8 * d + e]))
+    for d, piece in enumerate(pieces):
+        place = w_ref.at[where_ref[1 + min(d, 3)]]
+        if d >= 3:
+            place = place.at[pl.ds(pieces[3].shape[0] * (d - 3), piece.shape[0])]
+        copies.append(pltpu.make_async_copy(piece, place, sems.at[d]))
     copies.append(pltpu.make_async_copy(own_ref, mixed_ref.at[0], sems.at[32]))
     copies.append(pltpu.make_async_copy(other_ref, mixed_ref.at[1], sems.at[33]))
     for copy in copies:
         copy.start()
     for copy in copies:
         copy.wait()
-    groups = high
     sides = [pl.ds(pl.multiple_of(256 * a, 128), 256) for a in (where_ref[0], 1 - where_ref[0])]
     outs = []
     for j in range(4):
-        w = w_ref[j].astype(F32).reshape(8 * high, 896).astype(BF16)
+        w = w_ref[j].astype(F32).reshape(8 * groups, 896).astype(BF16)
         for i, at in enumerate(sides):
             got = lax.dot_general(w, mixed_ref[i, 0:256, :], NT, preferred_element_type=F32)
             hold_ref[j, 0:groups, :, at] = got.reshape(groups, 8, 256).astype(BF16)
@@ -248,7 +252,8 @@
     return jnp.stack([jnp.asarray(v, jnp.int32) for v in values])
 
 
-PARTS = ((0, 32), (32, 24))
+GROUPS = ((0, 1, 7, 2, 6), (3, 5, 4))
+VIA_UP = (3, 1)
 
 
 def per_device(
@@ -286,13 +291,16 @@
     recv = lax.all_to_all(sent, CHIPS, 0, 0, tiled=True)
 
     w_t, parts = after(w_out.T, sent), []
-    by_z = [w_t] + [shift(w_t, "pop_1", 8, e) for e in (1, 2, 3, 4, 5, 6, 7)]
-    stacked = call(stack_kernel, [shape((8, high, feats)) for _, high in PARTS], by_z)
-    for own in stacked:
+    z1, z7, z2, z6 = [shift(w_t, "pop_1", 8, e) for e in (1, 7, 2, 6)]
+    z3, z5 = shift(z1, "pop_1", 8, 2), shift(z7, "pop_1", 8, 6)
+    z4 = [shift(z2[:24], "pop_1", 8, 2), shift(z6[24:], "pop_1", 8, 6)]
+    for i, ins in enumerate(([w_t, z1, z7, z2, z6], [z3, z5, *z4])):
+        n, via = len(GROUPS[i]), VIA_UP[i]
+        own = call(stack_kernel, shape((n, 56, feats)), ins)
         up, down = shift(own, "pop_0", 4, 1), shift(own, "pop_0", 4, 3)
-        far = [shift(up[:4], "pop_0", 4, 1), shift(down[4:], "pop_0", 4, 3)]
+        far = [shift(up[:via], "pop_0", 4, 1), shift(down[via:], "pop_0", 4, 3)]
         parts.append([own, up, down, *far])
-    where = ints(c, *[(x + d - y) % 4 for d in (0, -1, 1, 2)], *[(z - e) % 8 for e in range(8)])
+    where = ints(c, *[(x + d - y) % 4 for d in (0, -1, 1, 2)])
 
     cos_all, sin_all = tables(jnp.arange(tok, dtype=F32), HEAD_DIM)
     k32 = jnp.dot(tokens, w_key, preferred_element_type=F32)
@@ -311,32 +319,32 @@
 
     outs = [
         call(
-            functools.partial(project_kernel, high),
-            [shape((high + 2, 8, 512))] * 4,
+            project_kernel,
+            [shape((7 * len(group) + 2, 8, 512))] * 4,
             (where, *pieces, mixed, mixed_b),
             smem=1,
             scratch=[
-                pltpu.VMEM((4, 8, high, feats), BF16),
+                pltpu.VMEM((4, len(group), 56, feats), BF16),
                 pltpu.VMEM((2, 272, feats), BF16),
-                pltpu.VMEM((4, high + 2, 8, 512), BF16),
+                pltpu.VMEM((4, 7 * len(group) + 2, 8, 512), BF16),
                 pltpu.SemaphoreType.DMA((38,)),
             ],
             load=False,
         )
-        for (_, high), pieces in zip(PARTS, parts)
+        for group, pieces in zip(GROUPS, parts)
     ]
     mets = []
     for out in outs:
         mets.append([out[0]] + [shift(out[s], "mp", 4, s) for s in (2, 1, 3)])
 
-    def in_parts(a):
-        return [a[..., at : at + high].reshape(*a.shape[:-2], 8 * high) for at, high in PARTS]
-
-    o_r = after(o_right[0], mixed)
-    o_cut = lax.dynamic_slice(o_r, (0, feats * y), (RANK, feats)).reshape(RANK, 8, 2, 56)
-    o_cut = jnp.concatenate(in_parts(jnp.moveaxis(o_cut, 2, 0)), axis=-1) * half
-    o_cut = jnp.broadcast_to(o_cut[None], (32, 2, RANK, 448)).reshape(64, RANK, 448)
-    cut_q = jnp.moveaxis((after(left_t, mixed) * twice).reshape(RANK, 64, 56), 1, 0)
+    order = jnp.array([e for group in GROUPS for e in group])
+    which = (jnp.arange(8)[:, None] - order[None]) % 8
+    o_r = after(o_right[0], sent)
+    o_cut = lax.dynamic_slice(o_r, (0, feats * y), (RANK, feats)).reshape(RANK, 8, 2, 56) * half
+    one = (which[:, :, None] == jnp.arange(8)).astype(BF16)
+    o_cut = jnp.einsum("kiz,rzcf->kcrif", one, o_cut, preferred_element_type=F32).astype(BF16)
+    o_cut = jnp.broadcast_to(o_cut.reshape(1, 16, RANK, 448), (4, 16, RANK, 448)).reshape(64, RANK, 448)
+    cut_q = jnp.moveaxis((after(left_t, sent) * twice).reshape(RANK, 64, 56), 1, 0)
     cut_o = jnp.moveaxis((o_r * twice).reshape(RANK, 64, 56), 1, 0)
     gap = jnp.zeros((64, RANK, 8), BF16)
     late = jnp.concatenate([cut_q, gap, cut_o, gap, o_cut, jnp.zeros((64, RANK, 64), BF16)], axis=2)
@@ -345,14 +353,17 @@
     factors_b = swap(factors)
     lefts = late[:, :, :128].reshape(32, 8, 128)
     goal = lax.dynamic_slice(target, (8 * k, 0), (8, feats)).reshape(8, 8, 2, 56)
-    goals = in_parts(jnp.where(c == 0, goal[:, :, 0], goal[:, :, 1]))
-
+    goal = jnp.where(c == 0, goal[:, :, 0], goal[:, :, 1])
+    here = (((z - order) % 8)[:, None] == jnp.arange(8)).astype(BF16)
+    goal = jnp.einsum("iz,tzf->tif", here, goal, preferred_element_type=F32).astype(BF16).reshape(8, 448)
     err = jnp.zeros((8, 1, 512), F32)
     start = 128
-    for (_, high), met, goal in zip(PARTS, mets, goals):
-        right = late[:, :, start : start + 8 * high].reshape(256, 8 * high)
-        start += 8 * high
-        err = call(error_kernel, shape((8, 1, 512), F32), (*met, right, goal, err))
+    for group, met in zip(GROUPS, mets):
+        n = 56 * len(group)
+        right = late[:, :, start : start + n].reshape(256, n)
+        part = goal[:, start - 128 : start - 128 + n]
+        start += n
+        err = call(error_kernel, shape((8, 1, 512), F32), (*met, right, part, err))
 
     err = lax.all_to_all(err, ("pop_2", "mp"), 0, 0, tiled=True)
     err = jnp.sum(err, axis=0, keepdims=True)

time: 168 us -> 169 us (level)
  starting transfers between devices: 65 us -> 61.6 us
  local copies, waits for them, and re-layouts: 13.3 us -> 15.8 us
    slice x10, local copies, waits for them, and re-layouts: 0.34 us -> 4.05 us  [the longest x2 1.61 us: per_device(): z4 = [shift(z2[:24], 'pop_1', 8, 2), shift(z6[24:], 'pop_1', 8, 6)]]
    ppermute x3, starting transfers between devices: 7.39 us -> 3.9 us  [swap(): return lax.ppermute(x, 'pop_2', [(0, 1), (1, 0)])]
    all_to_all x1, starting transfers between devices: 4.19 us -> 7.39 us  [per_device(): late = lax.all_to_all(late, POP, 0, 0, tiled=True)]
    all_to_all x1, starting transfers between devices: 8.31 us -> 5.67 us  [per_device(): lax.all_to_all(jnp.broadcast_to(err, (32, 1, 512)), CHIPS, 0, 0, tiled=True)]
    pallas_call x8 -> x9, Pallas kernels: 29.8 us -> 31 us  [call(): pl.pallas_call(kernel, out_shape=out, in_specs=[pl.BlockSpec(memory_space...]
    ppermute x21 -> x22, waiting for transfers between devices: 33.2 us -> 32.4 us  [shift(): return lax.ppermute(x, axis, [(i, (i + step) % size) for i in range(size)])]
    ppermute x21 -> x22, starting transfers between devices: 33 us -> 32.5 us  [shift(): return lax.ppermute(x, axis, [(i, (i + step) % size) for i in range(size)])]
    unnamed x49 -> x50, local copies, waits for them, and re-layouts: 3.51 us -> 3.48 us
  transfers between devices with their start and end apart: 27 -> 28, of which waited for: 8 -> 9; matrix products, arithmetic and copies ran while one was open for 9% -> 12% of each run, Pallas kernels for 13% -> 14%
where the time goes in v1:
time: 169 us; the launch traced here: 168 us
  starting transfers between devices  61.6 us (36%)
  waiting for transfers between devices  40 us (24%)
  Pallas kernels  31 us (18%)
  local copies, waits for them, and re-layouts  15.8 us (9%)
  blocking collectives  9.43 us (6%)
  other arithmetic  4.62 us (3%)
  matrix products  3.47 us (2%)
  between operations  2.21 us (1%)
    ppermute x22, starting transfers between devices, shift(): return lax.ppermute(x, axis, [(i, (i + step) % size) for i in range(size)])  32.5 us
    ppermute x22, waiting for transfers between devices, shift(): return lax.ppermute(x, axis, [(i, (i + step) % size) for i in range(size)])  32.4 us
    pallas_call x9, Pallas kernels, call(): pl.pallas_call(kernel, out_shape=out, in_specs=[pl.BlockSpec(memory_space...  31 us
    all_to_all x1, starting transfers between devices, per_device(): recv = lax.all_to_all(sent, CHIPS, 0, 0, tiled=True)  12.1 us
    all_to_all x1, blocking collectives, per_device(): err = lax.all_to_all(err, ('pop_2', 'mp'), 0, 0, tiled=True)  9.43 us
    all_to_all x1, waiting for transfers between devices, per_device(): lax.all_to_all(jnp.broadcast_to(err, (32, 1, 512)), CHIPS, 0, 0, tiled=True)  7.55 us
    all_to_all x1, starting transfers between devices, per_device(): late = lax.all_to_all(late, POP, 0, 0, tiled=True)  7.39 us
    all_to_all x1, starting transfers between devices, per_device(): lax.all_to_all(jnp.broadcast_to(err, (32, 1, 512)), CHIPS, 0, 0, tiled=True)  5.67 us
  transfers between devices with their start and end apart: 28, of which 9 were waited for; matrix products, arithmetic and copies ran while one was open for 12% of the time, Pallas kernels for 14%

profile of v1, /device:TPU:1, one launch (start us, length us, event | category | flops | bytes accessed | tf_op | source)
XLA Modules:
  0.0 168.2 jit_solution(7125603705258231615)
XLA Ops:
  2.0 4.1 %shard_map.139 = bf16[32,8,1920]{2,1,0:T(8,128)(2,1)} custom-call(s32[2]{0:T(128)} %pad_add_fusion.1.refs_0_, bf16[256,3584]{1,0:T(8,128)(2,1)} %refs_1_.1, bf16[56,896]{1,0:T(8,128)(2,1)} %refs_2_.1, bf16[4,3584]{1,0:T(4,128)(2,1)} %bitcast.58, bf16[4,896]{1,0:T(4,128)(2,1)} %bitcast.65, bf16[4,896]{1,0:T(4,128)(2,1)} %bitcast.66), custom_call_target="tpu_custom_call" | custom-call | flops 1000000000 | bytes 2000000 | tf_op jit(solution)/shard_map/pallas_call | solution.py:233
  6.1 12.1 %all-to-all-start = ((bf16[32,8,1920]{2,1,0:T(8,128)(2,1)}), bf16[32,8,1920]{2,1,0:T(8,128)(2,1)}, u32[]{:S(2)}, u32[]{:S(2)}) async-start(bf16[32,8,1920]{2,1,0:T(8,128)(2,1)} %shard_map.139), calls=%async_computation | async-start | bytes 1966080 | tf_op jit(solution)/shard_map/all_to_all | solution.py:291
  18.2 3.4 %collective-permute-start.6 = (bf16[56,896]{1,0:T(8,128)(2,1)S(1)}, bf16[56,896]{1,0:T(8,128)(2,1)S(1)}, u32[]{:S(2)}, u32[]{:S(2)}) collective-permute-start(bf16[56,896]{1,0:T(8,128)(2,1)S(1)} %bitcast.61), channel_id=1, source_target_pairs={{0,48},{8,56},{16,0},{24,8},{32,16},{40,24},{48,32},{56,40},{1,49}... | collective-permute-start | bytes 301064 | tf_op jit(solution)/shard_map/ppermute | solution.py:32
  21.6 2.7 %collective-permute-start.2 = (bf16[56,896]{1,0:T(8,128)(2,1)S(1)}, bf16[56,896]{1,0:T(8,128)(2,1)}, u32[]{:S(2)}, u32[]{:S(2)}) collective-permute-start(bf16[56,896]{1,0:T(8,128)(2,1)S(1)} %bitcast.63), channel_id=1, source_target_pairs={{0,56},{8,0},{16,8},{24,16},{32,24},{40,32},{48,40},{56,48},{1,57}... | collective-permute-start | bytes 301064 | tf_op jit(solution)/shard_map/ppermute | solution.py:32
  25.8 0.8 fusion.3.refs_4_
  26.6 2.4 %convolution_convert_fusion.1.refs_5_ = bf16[256,128]{1,0:T(8,128)(2,1)} fusion(bf16[256,3584]{1,0:T(8,128)(2,1)S(1)} %copy-done.1, bf16[3584,128]{1,0:T(8,128)(2,1)} %param.16), kind=kOutput, calls=%fused_computation.2 | convolution fusion | flops 234913792 | bytes 2818048 | tf_op jit(solution)/shard_map/dot_general | solution.py:308
  29.7 15.0 %collective-permute-done.6.refs_4_ = bf16[56,896]{1,0:T(8,128)(2,1)S(1)} collective-permute-done((bf16[56,896]{1,0:T(8,128)(2,1)S(1)}, bf16[56,896]{1,0:T(8,128)(2,1)S(1)}, u32[]{:S(2)}, u32[]{:S(2)}) %collective-permute-start.6) | collective-permute-done | bytes 100384 | tf_op jit(solution)/shard_map/ppermute | solution.py:32
  44.7 1.3 collective-permute-done.4.refs_3_
  46.1 1.1 collective-permute-done.2.refs_2_
  47.1 1.2 collective-permute-done.refs_1_
  48.4 2.0 %shard_map.143.refs_0_ = bf16[5,56,896]{2,1,0:T(8,128)(2,1)} custom-call(bf16[56,896]{1,0:T(8,128)(2,1)} %bitcast.60, bf16[56,896]{1,0:T(8,128)(2,1)} %collective-permute-done.refs_1_, bf16[56,896]{1,0:T(8,128)(2,1)} %collective-permute-done.2.refs_2_, bf16[56,896]{1,0:T(8,128)(2,1)} %copy-done.11, bf16[56,896]{1,0:T(8,128)(2,1)} %copy-done.8), custom_call_target="tpu_custom_call" | custom-call | flops 1000000000 | bytes 2000000 | tf_op jit(solution)/shard_map/pallas_call | solution.py:233
  50.4 1.2 collective-permute-start.17
  51.6 1.1 convert_reduce_fusion.refs_2_
  52.7 2.0 %collective-permute-start.12 = (f32[8,896]{1,0:T(8,128)S(1)}, f32[8,896]{1,0:T(8,128)S(1)}, u32[]{:S(2)}, u32[]{:S(2)}) collective-permute-start(f32[8,896]{1,0:T(8,128)S(1)} %convert_reduce_fusion.refs_2_), channel_id=1, source_target_pairs={{0,4},{4,0},{1,5},{5,1},{2,6},{6,2},{3,7},{7,3},{8,12},{12,8},{9,1... | collective-permute-start | bytes 86024 | tf_op jit(solution)/shard_map/ppermute | solution.py:36
  54.8 1.6 collective-permute-start.18
  56.3 0.8 slice.75
  57.1 2.1 %collective-permute-start.7 = (bf16[32,896]{1,0:T(8,128)(2,1)S(1)}, bf16[32,896]{1,0:T(8,128)(2,1)S(1)}, u32[]{:S(2)}, u32[]{:S(2)}) collective-permute-start(bf16[32,896]{1,0:T(8,128)(2,1)S(1)} %slice.75), channel_id=1, source_target_pairs={{0,48},{8,56},{16,0},{24,8},{32,16},{40,24},{48,32},{56,40},{1,49}... | collective-permute-start | bytes 172040 | tf_op jit(solution)/shard_map/ppermute | solution.py:32
  59.2 0.8 slice.74
  60.3 3.3 %collective-permute-start.3 = (bf16[56,896]{1,0:T(8,128)(2,1)}, bf16[56,896]{1,0:T(8,128)(2,1)S(1)}, u32[]{:S(2)}, u32[]{:S(2)}) collective-permute-start(bf16[56,896]{1,0:T(8,128)(2,1)} %collective-permute-done.2.refs_2_), channel_id=1, source_target_pairs={{0,48},{8,56},{16,0},{24,8},{32,16},{40,24},{48,32},{56,40},{1,49}... | collective-permute-start | bytes 301064 | tf_op jit(solution)/shard_map/ppermute | solution.py:32
  63.6 5.2 %shard_map.141.refs_5_ = bf16[272,896]{1,0:T(8,128)(2,1)} custom-call(s32[1]{0:T(128)} %bitcast.15.refs_0_, bf16[32,8,1920]{2,1,0:T(8,128)(2,1)} %all-to-all-done.refs_1_, f32[8,896]{1,0:T(8,128)} %copy-done.10, f32[8,896]{1,0:T(8,128)} %copy-done.24, bf16[256,128]{1,0:T(8,128)(2,1)} %fusion.3.refs_4_, bf16[256,128]{1,0:T(8,128)(2,1)} %convolution_convert_fusion.1.refs_5_, ...), custom_call_target="tpu_custom_call" | custom-call | flops 1000000000 | bytes 2000000 | tf_op jit(solution)/shard_map/pallas_call | solution.py:233
  68.9 0.9 collective-permute-start.1
  69.8 1.1 collective-permute-start.13
  71.9 1.3 concatenate.24
  73.2 7.4 %all-to-all-start.1 = ((bf16[64,4,640]{2,1,0:T(4,128)(2,1)}), bf16[64,4,640]{2,1,0:T(4,128)(2,1)S(1)}, u32[]{:S(2)}, u32[]{:S(2)}) async-start(bf16[64,4,640]{2,1,0:T(4,128)(2,1)} %concatenate.24), calls=%async_computation.1 | async-start | bytes 655360 | tf_op jit(solution)/shard_map/all_to_all | solution.py:351
  81.9 1.7 %shard_map.140.refs_0_ = bf16[3,56,896]{2,1,0:T(8,128)(2,1)} custom-call(bf16[56,896]{1,0:T(8,128)(2,1)} %copy-done.20, bf16[56,896]{1,0:T(8,128)(2,1)} %copy-done.19, bf16[24,896]{1,0:T(8,128)(2,1)} %copy-done.23, bf16[32,896]{1,0:T(8,128)(2,1)} %copy-done.22), custom_call_target="tpu_custom_call" | custom-call | flops 1000000000 | bytes 2000000 | tf_op jit(solution)/shard_map/pallas_call | solution.py:233
  83.6 2.9 %collective-permute-start.9 = (bf16[3,56,896]{2,1,0:T(8,128)(2,1)}, bf16[3,56,896]{2,1,0:T(8,128)(2,1)S(1)}, u32[]{:S(2)}, u32[]{:S(2)}) collective-permute-start(bf16[3,56,896]{2,1,0:T(8,128)(2,1)} %shard_map.140.refs_0_), channel_id=1, source_target_pairs={{0,192},{64,0},{128,64},{192,128},{1,193},{65,1},{129,65},{193,129... | collective-permute-start | bytes 903176 | tf_op jit(solution)/shard_map/ppermute | solution.py:32
  86.6 0.8 constant_dynamic-slice_fusion
  87.5 2.7 %collective-permute-start.20 = (bf16[2,56,896]{2,1,0:T(8,128)(2,1)S(1)}, bf16[2,56,896]{2,1,0:T(8,128)(2,1)}, u32[]{:S(2)}, u32[]{:S(2)}) collective-permute-start(bf16[2,56,896]{2,1,0:T(8,128)(2,1)S(1)} %slice.86), channel_id=1, source_target_pairs={{0,192},{64,0},{128,64},{192,128},{1,193},{65,1},{129,65},{193,129... | collective-permute-start | bytes 602120 | tf_op jit(solution)/shard_map/ppermute | solution.py:32
  91.0 4.3 %collective-permute-done.9.refs_2_ = bf16[3,56,896]{2,1,0:T(8,128)(2,1)S(1)} collective-permute-done((bf16[3,56,896]{2,1,0:T(8,128)(2,1)}, bf16[3,56,896]{2,1,0:T(8,128)(2,1)S(1)}, u32[]{:S(2)}, u32[]{:S(2)}) %collective-permute-start.9) | collective-permute-done | bytes 301088 | tf_op jit(solution)/shard_map/ppermute | solution.py:32
  95.4 2.8 %collective-permute-start.11 = (bf16[2,56,896]{2,1,0:T(8,128)(2,1)S(1)}, bf16[2,56,896]{2,1,0:T(8,128)(2,1)}, u32[]{:S(2)}, u32[]{:S(2)}) collective-permute-start(bf16[2,56,896]{2,1,0:T(8,128)(2,1)S(1)} %slice.77), channel_id=1, source_target_pairs={{0,192},{64,0},{128,64},{192,128},{1,193},{65,1},{129,65},{193,129... | collective-permute-start | bytes 602120 | tf_op jit(solution)/shard_map/ppermute | solution.py:32
  98.2 0.9 slice.76
  99.7 4.8 %collective-permute-done.19.refs_3_ = bf16[3,56,896]{2,1,0:T(8,128)(2,1)} collective-permute-done((bf16[3,56,896]{2,1,0:T(8,128)(2,1)S(1)}, bf16[3,56,896]{2,1,0:T(8,128)(2,1)}, u32[]{:S(2)}, u32[]{:S(2)}) %collective-permute-start.19) | collective-permute-done | bytes 301088 | tf_op jit(solution)/shard_map/ppermute | solution.py:32
  104.4 4.9 %shard_map.144 = (bf16[37,8,512]{2,1,0:T(8,128)(2,1)}, bf16[37,8,512]{2,1,0:T(8,128)(2,1)}, bf16[37,8,512]{2,1,0:T(8,128)(2,1)}, bf16[37,8,512]{2,1,0:T(8,128)(2,1)}) custom-call(s32[5]{0:T(128)} %stack.44.where_ref, bf16[5,56,896]{2,1,0:T(8,128)(2,1)} %shard_map.143.refs_0_, bf16[5,56,896]{2,1,0:T(8,128)(2,1)} %copy-done.3, bf16[5,56,896]{2,1,0:T(8,128)(2,1)} %copy-done.5, ...), custom_call_target="tpu_custom_call" | custom-call | flops 1000000000 | bytes 2000000 | tf_op jit(solution)/shard_map/pallas_call | solution.py:233
  109.4 3.0 %collective-permute-start.21 = (bf16[37,8,512]{2,1,0:T(8,128)(2,1)}, bf16[37,8,512]{2,1,0:T(8,128)(2,1)S(1)}, u32[]{:S(2)}, u32[]{:S(2)}) collective-permute-start(bf16[37,8,512]{2,1,0:T(8,128)(2,1)} %get-tuple-element.26), channel_id=1, source_target_pairs={{0,2},{1,3},{2,0},{3,1},{4,6},{5,7},{6,4},{7,5},{8,10},{9,11},{10,... | collective-permute-start | bytes 909320 | tf_op jit(solution)/shard_map/ppermute | solution.py:32
  112.8 2.3 %collective-permute-start.23 = (bf16[37,8,512]{2,1,0:T(8,128)(2,1)}, bf16[37,8,512]{2,1,0:T(8,128)(2,1)}, u32[]{:S(2)}, u32[]{:S(2)}) collective-permute-start(bf16[37,8,512]{2,1,0:T(8,128)(2,1)} %get-tuple-element.28), channel_id=1, source_target_pairs={{0,3},{1,0},{2,1},{3,2},{4,7},{5,4},{6,5},{7,6},{8,11},{9,8},{10,9... | collective-permute-start | bytes 909320 | tf_op jit(solution)/shard_map/ppermute | solution.py:32
  115.7 4.6 %shard_map.142 = (bf16[23,8,512]{2,1,0:T(8,128)(2,1)}, bf16[23,8,512]{2,1,0:T(8,128)(2,1)}, bf16[23,8,512]{2,1,0:T(8,128)(2,1)}, bf16[23,8,512]{2,1,0:T(8,128)(2,1)}) custom-call(s32[5]{0:T(128)} %stack.44.where_ref, bf16[3,56,896]{2,1,0:T(8,128)(2,1)} %shard_map.140.refs_0_, bf16[3,56,896]{2,1,0:T(8,128)(2,1)} %collective-permute-done.8.refs_1_, ...), custom_call_target="tpu_custom_call" | custom-call | flops 1000000000 | bytes 2000000 | tf_op jit(solution)/shard_map/pallas_call | solution.py:233
  121.0 1.1 slice.72.refs_3_
  122.1 2.2 %collective-permute-start.16 = (bf16[23,8,512]{2,1,0:T(8,128)(2,1)}, bf16[23,8,512]{2,1,0:T(8,128)(2,1)}, u32[]{:S(2)}, u32[]{:S(2)}) collective-permute-start(bf16[23,8,512]{2,1,0:T(8,128)(2,1)} %get-tuple-element.22), channel_id=1, source_target_pairs={{0,3},{1,0},{2,1},{3,2},{4,7},{5,4},{6,5},{7,6},{8,11},{9,8},{10,9... | collective-permute-start | bytes 565256 | tf_op jit(solution)/shard_map/ppermute | solution.py:32
  124.3 4.2 %collective-permute-done.22.refs_2_ = bf16[37,8,512]{2,1,0:T(8,128)(2,1)S(1)} collective-permute-done((bf16[37,8,512]{2,1,0:T(8,128)(2,1)}, bf16[37,8,512]{2,1,0:T(8,128)(2,1)S(1)}, u32[]{:S(2)}, u32[]{:S(2)}) %collective-permute-start.22) | collective-permute-done | bytes 303136 | tf_op jit(solution)/shard_map/ppermute | solution.py:32
  128.5 0.8 collective-permute-start.24
  130.9 0.8 reshape.87.refs_4_
  131.8 0.7 reshape.84.refs_4_
  133.2 2.6 %shard_map.145.refs_6_ = f32[8,1,512]{2,1,0:T(1,128)} custom-call(bf16[37,8,512]{2,1,0:T(8,128)(2,1)} %get-tuple-element.25.refs_0_, bf16[37,8,512]{2,1,0:T(8,128)(2,1)} %copy-done.14, bf16[37,8,512]{2,1,0:T(8,128)(2,1)} %copy-done.15, bf16[37,8,512]{2,1,0:T(8,128)(2,1)} %collective-permute-done.23.refs_3_, bf16[256,280]{1,0:T(8,128)(2,1)} %reshape.87.refs_4_, ...), custom_call_target="tpu_custom_call" | custom-call | flops 1000000000 | bytes 2000000 | tf_op jit(solution)/shard_map/pallas_call | solution.py:233
  136.5 2.4 %shard_map.146 = f32[8,1,512]{2,1,0:T(1,128)} custom-call(bf16[23,8,512]{2,1,0:T(8,128)(2,1)} %get-tuple-element.19.refs_0_, bf16[23,8,512]{2,1,0:T(8,128)(2,1)} %copy-done.16, bf16[23,8,512]{2,1,0:T(8,128)(2,1)} %copy-done.17, bf16[23,8,512]{2,1,0:T(8,128)(2,1)} %collective-permute-done.16.refs_3_, bf16[256,168]{1,0:T(8,128)(2,1)} %reshape.84.refs_4_, ...), custom_call_target="tpu_custom_call" | custom-call | flops 1000000000 | bytes 2000000 | tf_op jit(solution)/shard_map/pallas_call | solution.py:233
  139.0 9.4 %all_to_all.20 = f32[8,1,512]{2,1,0:T(1,128)S(1)} all-to-all(f32[8,1,512]{2,1,0:T(1,128)} %shard_map.146), channel_id=1, replica_groups=mesh['pop_0'=4,'pop_1'=8,'pop_2'=2,'mp'=4] {'pop_2','mp'}, dimensions={0} | all-to-all | bytes 32768 | tf_op jit(solution)/shard_map/all_to_all | solution.py:368
  149.1 5.7 %all-to-all-start.3 = ((f32[32,1,512]{2,1,0:T(1,128)}), f32[32,1,512]{2,1,0:T(1,128)S(1)}, u32[]{:S(2)}, u32[]{:S(2)}) async-start(f32[32,1,512]{2,1,0:T(1,128)} %broadcast_in_dim.17), calls=%async_computation.3 | async-start | bytes 131072 | tf_op jit(solution)/shard_map/all_to_all | solution.py:370
  156.1 7.5 %all-to-all-done.3.refs_1_ = f32[32,1,512]{2,1,0:T(1,128)S(1)} async-done(((f32[32,1,512]{2,1,0:T(1,128)}), f32[32,1,512]{2,1,0:T(1,128)S(1)}, u32[]{:S(2)}, u32[]{:S(2)}) %all-to-all-start.3) | async-done | bytes 65568 | tf_op jit(solution)/shard_map/all_to_all | solution.py:370
  164.4 3.6 %shard_map.147 = (f32[56,896]{1,0:T(8,128)}, f32[56,896]{1,0:T(8,128)}, f32[1,128]{1,0:T(1,128)}) custom-call(s32[2]{0:T(128)} %pad_add_fusion.refs_0_, f32[32,1,512]{2,1,0:T(1,128)} %copy-done.6, bf16[32,8,128]{2,1,0:T(8,128)(2,1)} %bitcast.55, bf16[32,8,896]{2,1,0:T(8,128)(2,1)} %copy-done.2, bf16[32,8,896]{2,1,0:T(8,128)(2,1)} %copy-done.13), custom_call_target="tpu_custom_call" | custom-call | flops 1000000000 | bytes 2000000 | tf_op jit(solution)/shard_map/pallas_call | solution.py:233
  (119 shorter events, 14.5 us)
Async XLA Ops:
  0.6 23.7 %copy-start = (bf16[3584,128]{1,0:T(8,128)(2,1)S(1)}, bf16[3584,128]{1,0:T(8,128)(2,1)}, u32[]{:S(2)}) copy-start(bf16[3584,128]{1,0:T(8,128)(2,1)} %param.15) | copy-start | bytes 2752516
  6.1 12.2 %copy-start.18 = (bf16[896,56]{0,1:T(8,128)(2,1)S(1)}, bf16[896,56]{0,1:T(8,128)(2,1)}, u32[]{:S(2)}) copy-start(bf16[896,56]{0,1:T(8,128)(2,1)} %param.17) | copy-start | bytes 301060
  6.1 18.2 %copy-start.1 = (bf16[256,3584]{1,0:T(8,128)(2,1)S(1)}, bf16[256,3584]{1,0:T(8,128)(2,1)}, u32[]{:S(2)}) copy-start(bf16[256,3584]{1,0:T(8,128)(2,1)} %refs_1_.1) | copy-start | bytes 5505028
  6.1 45.4 %all-to-all-start = ((bf16[32,8,1920]{2,1,0:T(8,128)(2,1)}), bf16[32,8,1920]{2,1,0:T(8,128)(2,1)}, u32[]{:S(2)}, u32[]{:S(2)}) async-start(bf16[32,8,1920]{2,1,0:T(8,128)(2,1)} %shard_map.139), calls=%async_computation | async-start | bytes 1966080 | tf_op jit(solution)/shard_map/all_to_all | solution.py:291
  18.2 7.0 %copy-start.12 = (s32[8]{0:T(128)S(1)}, s32[8]{0:T(128)}, u32[]{:S(2)}) copy-start(s32[8]{0:T(128)} %constant.113) | copy-start | bytes 100
  18.2 26.5 %collective-permute-start.6 = (bf16[56,896]{1,0:T(8,128)(2,1)S(1)}, bf16[56,896]{1,0:T(8,128)(2,1)S(1)}, u32[]{:S(2)}, u32[]{:S(2)}) collective-permute-start(bf16[56,896]{1,0:T(8,128)(2,1)S(1)} %bitcast.61), channel_id=1, source_target_pairs={{0,48},{8,56},{16,0},{24,8},{32,16},{40,24},{48,32},{56,40},{1,49}... | collective-permute-start | bytes 301064 | tf_op jit(solution)/shard_map/ppermute | solution.py:32
  21.6 24.5 %collective-permute-start.4 = (bf16[56,896]{1,0:T(8,128)(2,1)S(1)}, bf16[56,896]{1,0:T(8,128)(2,1)S(1)}, u32[]{:S(2)}, u32[]{:S(2)}) collective-permute-start(bf16[56,896]{1,0:T(8,128)(2,1)S(1)} %bitcast.62), channel_id=1, source_target_pairs={{0,16},{8,24},{16,32},{24,40},{32,48},{40,56},{48,0},{56,8},{1,17}... | collective-permute-start | bytes 301064 | tf_op jit(solution)/shard_map/ppermute | solution.py:32
  21.6 25.5 %collective-permute-start.2 = (bf16[56,896]{1,0:T(8,128)(2,1)S(1)}, bf16[56,896]{1,0:T(8,128)(2,1)}, u32[]{:S(2)}, u32[]{:S(2)}) collective-permute-start(bf16[56,896]{1,0:T(8,128)(2,1)S(1)} %bitcast.63), channel_id=1, source_target_pairs={{0,56},{8,0},{16,8},{24,16},{32,24},{40,32},{48,40},{56,48},{1,57}... | collective-permute-start | bytes 301064 | tf_op jit(solution)/shard_map/ppermute | solution.py:32
  24.3 24.1 %collective-permute-start = (bf16[56,896]{1,0:T(8,128)(2,1)S(1)}, bf16[56,896]{1,0:T(8,128)(2,1)}, u32[]{:S(2)}, u32[]{:S(2)}) collective-permute-start(bf16[56,896]{1,0:T(8,128)(2,1)S(1)} %bitcast.64), channel_id=1, source_target_pairs={{0,8},{8,16},{16,24},{24,32},{32,40},{40,48},{48,56},{56,0},{1,9},... | collective-permute-start | bytes 301064 | tf_op jit(solution)/shard_map/ppermute | solution.py:32
  25.8 3.2 %copy-start.7 = (bf16[1,4,3584]{2,1,0:T(4,128)(2,1)S(1)}, bf16[1,4,3584]{2,1,0:T(4,128)(2,1)}, u32[]{:S(2)}) copy-start(bf16[1,4,3584]{2,1,0:T(4,128)(2,1)} %param.21) | copy-start | bytes 86020
  25.8 3.2 %copy-start.9 = (bf16[1,3584,4]{1,2,0:T(4,128)(2,1)S(1)}, bf16[1,3584,4]{1,2,0:T(4,128)(2,1)}, u32[]{:S(2)}) copy-start(bf16[1,3584,4]{1,2,0:T(4,128)(2,1)} %param.18) | copy-start | bytes 86020
  44.7 3.6 %copy-start.8 = (bf16[56,896]{1,0:T(8,128)(2,1)}, bf16[56,896]{1,0:T(8,128)(2,1)S(1)}, u32[]{:S(2)}) copy-start(bf16[56,896]{1,0:T(8,128)(2,1)S(1)} %collective-permute-done.6.refs_4_) | copy-start | bytes 301060
  46.1 2.3 %copy-start.11 = (bf16[56,896]{1,0:T(8,128)(2,1)}, bf16[56,896]{1,0:T(8,128)(2,1)S(1)}, u32[]{:S(2)}) copy-start(bf16[56,896]{1,0:T(8,128)(2,1)S(1)} %collective-permute-done.4.refs_3_) | copy-start | bytes 301060
  50.4 36.1 %collective-permute-start.17 = (bf16[5,56,896]{2,1,0:T(8,128)(2,1)}, bf16[5,56,896]{2,1,0:T(8,128)(2,1)S(1)}, u32[]{:S(2)}, u32[]{:S(2)}) collective-permute-start(bf16[5,56,896]{2,1,0:T(8,128)(2,1)} %shard_map.143.refs_0_), channel_id=1, source_target_pairs={{0,64},{64,128},{128,192},{192,0},{1,65},{65,129},{129,193},{193,1... | collective-permute-start | bytes 1505288 | tf_op jit(solution)/shard_map/ppermute | solution.py:32
  52.7 10.9 %copy-start.10 = (f32[8,896]{1,0:T(8,128)}, f32[8,896]{1,0:T(8,128)S(1)}, u32[]{:S(2)}) copy-start(f32[8,896]{1,0:T(8,128)S(1)} %convert_reduce_fusion.refs_2_) | copy-start | bytes 86020
  52.7 7.6 %collective-permute-start.12 = (f32[8,896]{1,0:T(8,128)S(1)}, f32[8,896]{1,0:T(8,128)S(1)}, u32[]{:S(2)}, u32[]{:S(2)}) collective-permute-start(f32[8,896]{1,0:T(8,128)S(1)} %convert_reduce_fusion.refs_2_), channel_id=1, source_target_pairs={{0,4},{4,0},{1,5},{5,1},{2,6},{6,2},{3,7},{7,3},{8,12},{12,8},{9,1... | collective-permute-start | bytes 86024 | tf_op jit(solution)/shard_map/ppermute | solution.py:36
  54.8 32.7 %collective-permute-start.18 = (bf16[5,56,896]{2,1,0:T(8,128)(2,1)}, bf16[5,56,896]{2,1,0:T(8,128)(2,1)S(1)}, u32[]{:S(2)}, u32[]{:S(2)}) collective-permute-start(bf16[5,56,896]{2,1,0:T(8,128)(2,1)} %shard_map.143.refs_0_), channel_id=1, source_target_pairs={{0,192},{64,0},{128,64},{192,128},{1,193},{65,1},{129,65},{193,129... | collective-permute-start | bytes 1505288 | tf_op jit(solution)/shard_map/ppermute | solution.py:32
  57.1 12.6 %collective-permute-start.7 = (bf16[32,896]{1,0:T(8,128)(2,1)S(1)}, bf16[32,896]{1,0:T(8,128)(2,1)S(1)}, u32[]{:S(2)}, u32[]{:S(2)}) collective-permute-start(bf16[32,896]{1,0:T(8,128)(2,1)S(1)} %slice.75), channel_id=1, source_target_pairs={{0,48},{8,56},{16,0},{24,8},{32,16},{40,24},{48,32},{56,40},{1,49}... | collective-permute-start | bytes 172040 | tf_op jit(solution)/shard_map/ppermute | solution.py:32
  60.0 8.8 %collective-permute-start.5 = (bf16[24,896]{1,0:T(8,128)(2,1)S(1)}, bf16[24,896]{1,0:T(8,128)(2,1)S(1)}, u32[]{:S(2)}, u32[]{:S(2)}) collective-permute-start(bf16[24,896]{1,0:T(8,128)(2,1)S(1)} %slice.74), channel_id=1, source_target_pairs={{0,16},{8,24},{16,32},{24,40},{32,48},{40,56},{48,0},{56,8},{1,17}... | collective-permute-start | bytes 129032 | tf_op jit(solution)/shard_map/ppermute | solution.py:32
  60.3 3.3 %copy-start.24 = (f32[8,896]{1,0:T(8,128)}, f32[8,896]{1,0:T(8,128)S(1)}, u32[]{:S(2)}) copy-start(f32[8,896]{1,0:T(8,128)S(1)} %collective-permute-done.12.refs_3_) | copy-start | bytes 86020
  60.3 20.3 %collective-permute-start.3 = (bf16[56,896]{1,0:T(8,128)(2,1)}, bf16[56,896]{1,0:T(8,128)(2,1)S(1)}, u32[]{:S(2)}, u32[]{:S(2)}) collective-permute-start(bf16[56,896]{1,0:T(8,128)(2,1)} %collective-permute-done.2.refs_2_), channel_id=1, source_target_pairs={{0,48},{8,56},{16,0},{24,8},{32,16},{40,24},{48,32},{56,40},{1,49}... | collective-permute-start | bytes 301064 | tf_op jit(solution)/shard_map/ppermute | solution.py:32
  68.9 11.8 %copy-start.23 = (bf16[24,896]{1,0:T(8,128)(2,1)}, bf16[24,896]{1,0:T(8,128)(2,1)S(1)}, u32[]{:S(2)}) copy-start(bf16[24,896]{1,0:T(8,128)(2,1)S(1)} %collective-permute-done.5.refs_2_) | copy-start | bytes 129028
  68.9 11.7 %collective-permute-start.1 = (bf16[56,896]{1,0:T(8,128)(2,1)}, bf16[56,896]{1,0:T(8,128)(2,1)S(1)}, u32[]{:S(2)}, u32[]{:S(2)}) collective-permute-start(bf16[56,896]{1,0:T(8,128)(2,1)} %collective-permute-done.refs_1_), channel_id=1, source_target_pairs={{0,16},{8,24},{16,32},{24,40},{32,48},{40,56},{48,0},{56,8},{1,17}... | collective-permute-start | bytes 301064 | tf_op jit(solution)/shard_map/ppermute | solution.py:32
  69.8 10.9 %copy-start.22 = (bf16[32,896]{1,0:T(8,128)(2,1)}, bf16[32,896]{1,0:T(8,128)(2,1)S(1)}, u32[]{:S(2)}) copy-start(bf16[32,896]{1,0:T(8,128)(2,1)S(1)} %collective-permute-done.7.refs_3_) | copy-start | bytes 172036
  69.8 34.7 %collective-permute-start.13 = (bf16[272,896]{1,0:T(8,128)(2,1)}, bf16[272,896]{1,0:T(8,128)(2,1)}, u32[]{:S(2)}, u32[]{:S(2)}) collective-permute-start(bf16[272,896]{1,0:T(8,128)(2,1)} %shard_map.141.refs_5_), channel_id=1, source_target_pairs={{0,4},{4,0},{1,5},{5,1},{2,6},{6,2},{3,7},{7,3},{8,12},{12,8},{9,1... | collective-permute-start | bytes 1462280 | tf_op jit(solution)/shard_map/ppermute | solution.py:36
  73.2 57.7 %all-to-all-start.1 = ((bf16[64,4,640]{2,1,0:T(4,128)(2,1)}), bf16[64,4,640]{2,1,0:T(4,128)(2,1)S(1)}, u32[]{:S(2)}, u32[]{:S(2)}) async-start(bf16[64,4,640]{2,1,0:T(4,128)(2,1)} %concatenate.24), calls=%async_computation.1 | async-start | bytes 655360 | tf_op jit(solution)/shard_map/all_to_all | solution.py:351
  83.6 11.8 %collective-permute-start.9 = (bf16[3,56,896]{2,1,0:T(8,128)(2,1)}, bf16[3,56,896]{2,1,0:T(8,128)(2,1)S(1)}, u32[]{:S(2)}, u32[]{:S(2)}) collective-permute-start(bf16[3,56,896]{2,1,0:T(8,128)(2,1)} %shard_map.140.refs_0_), channel_id=1, source_target_pairs={{0,192},{64,0},{128,64},{192,128},{1,193},{65,1},{129,65},{193,129... | collective-permute-start | bytes 903176 | tf_op jit(solution)/shard_map/ppermute | solution.py:32
  86.5 11.8 %collective-permute-start.8 = (bf16[3,56,896]{2,1,0:T(8,128)(2,1)}, bf16[3,56,896]{2,1,0:T(8,128)(2,1)}, u32[]{:S(2)}, u32[]{:S(2)}) collective-permute-start(bf16[3,56,896]{2,1,0:T(8,128)(2,1)} %shard_map.140.refs_0_), channel_id=1, source_target_pairs={{0,64},{64,128},{128,192},{192,0},{1,65},{65,129},{129,193},{193,1... | collective-permute-start | bytes 903176 | tf_op jit(solution)/shard_map/ppermute | solution.py:32
  86.5 18.0 %copy-start.3 = (bf16[5,56,896]{2,1,0:T(8,128)(2,1)}, bf16[5,56,896]{2,1,0:T(8,128)(2,1)S(1)}, u32[]{:S(2)}) copy-start(bf16[5,56,896]{2,1,0:T(8,128)(2,1)S(1)} %collective-permute-done.17.refs_1_) | copy-start | bytes 1505284
  86.5 17.9 %collective-permute-start.19 = (bf16[3,56,896]{2,1,0:T(8,128)(2,1)S(1)}, bf16[3,56,896]{2,1,0:T(8,128)(2,1)}, u32[]{:S(2)}, u32[]{:S(2)}) collective-permute-start(bf16[3,56,896]{2,1,0:T(8,128)(2,1)S(1)} %slice.85), channel_id=1, source_target_pairs={{0,64},{64,128},{128,192},{192,0},{1,65},{65,129},{129,193},{193,1... | collective-permute-start | bytes 903176 | tf_op jit(solution)/shard_map/ppermute | solution.py:32
  87.5 17.0 %copy-start.5 = (bf16[5,56,896]{2,1,0:T(8,128)(2,1)}, bf16[5,56,896]{2,1,0:T(8,128)(2,1)S(1)}, u32[]{:S(2)}) copy-start(bf16[5,56,896]{2,1,0:T(8,128)(2,1)S(1)} %collective-permute-done.18.refs_2_) | copy-start | bytes 1505284
  87.5 12.2 %collective-permute-start.20 = (bf16[2,56,896]{2,1,0:T(8,128)(2,1)S(1)}, bf16[2,56,896]{2,1,0:T(8,128)(2,1)}, u32[]{:S(2)}, u32[]{:S(2)}) collective-permute-start(bf16[2,56,896]{2,1,0:T(8,128)(2,1)S(1)} %slice.86), channel_id=1, source_target_pairs={{0,192},{64,0},{128,64},{192,128},{1,193},{65,1},{129,65},{193,129... | collective-permute-start | bytes 602120 | tf_op jit(solution)/shard_map/ppermute | solution.py:32
  95.4 14.0 %copy-start.4 = (bf16[3,56,896]{2,1,0:T(8,128)(2,1)}, bf16[3,56,896]{2,1,0:T(8,128)(2,1)S(1)}, u32[]{:S(2)}) copy-start(bf16[3,56,896]{2,1,0:T(8,128)(2,1)S(1)} %collective-permute-done.9.refs_2_) | copy-start | bytes 903172
  95.4 19.7 %collective-permute-start.11 = (bf16[2,56,896]{2,1,0:T(8,128)(2,1)S(1)}, bf16[2,56,896]{2,1,0:T(8,128)(2,1)}, u32[]{:S(2)}, u32[]{:S(2)}) collective-permute-start(bf16[2,56,896]{2,1,0:T(8,128)(2,1)S(1)} %slice.77), channel_id=1, source_target_pairs={{0,192},{64,0},{128,64},{192,128},{1,193},{65,1},{129,65},{193,129... | collective-permute-start | bytes 602120 | tf_op jit(solution)/shard_map/ppermute | solution.py:32
  99.1 16.0 %collective-permute-start.10 = (bf16[1,56,896]{2,1,0:T(8,128)(2,1)S(1)}, bf16[1,56,896]{2,1,0:T(8,128)(2,1)S(1)}, u32[]{:S(2)}, u32[]{:S(2)}) collective-permute-start(bf16[1,56,896]{2,1,0:T(8,128)(2,1)S(1)} %slice.76), channel_id=1, source_target_pairs={{0,64},{64,128},{128,192},{192,0},{1,65},{65,129},{129,193},{193,1... | collective-permute-start | bytes 301064 | tf_op jit(solution)/shard_map/ppermute | solution.py:32
  109.4 12.7 %collective-permute-start.21 = (bf16[37,8,512]{2,1,0:T(8,128)(2,1)}, bf16[37,8,512]{2,1,0:T(8,128)(2,1)S(1)}, u32[]{:S(2)}, u32[]{:S(2)}) collective-permute-start(bf16[37,8,512]{2,1,0:T(8,128)(2,1)} %get-tuple-element.26), channel_id=1, source_target_pairs={{0,2},{1,3},{2,0},{3,1},{4,6},{5,7},{6,4},{7,5},{8,10},{9,11},{10,... | collective-permute-start | bytes 909320 | tf_op jit(solution)/shard_map/ppermute | solution.py:32
  112.4 16.1 %collective-permute-start.22 = (bf16[37,8,512]{2,1,0:T(8,128)(2,1)}, bf16[37,8,512]{2,1,0:T(8,128)(2,1)S(1)}, u32[]{:S(2)}, u32[]{:S(2)}) collective-permute-start(bf16[37,8,512]{2,1,0:T(8,128)(2,1)} %get-tuple-element.27), channel_id=1, source_target_pairs={{0,1},{1,2},{2,3},{3,0},{4,5},{5,6},{6,7},{7,4},{8,9},{9,10},{10,1... | collective-permute-start | bytes 909320 | tf_op jit(solution)/shard_map/ppermute | solution.py:32
  112.8 19.8 %collective-permute-start.23 = (bf16[37,8,512]{2,1,0:T(8,128)(2,1)}, bf16[37,8,512]{2,1,0:T(8,128)(2,1)}, u32[]{:S(2)}, u32[]{:S(2)}) collective-permute-start(bf16[37,8,512]{2,1,0:T(8,128)(2,1)} %get-tuple-element.28), channel_id=1, source_target_pairs={{0,3},{1,0},{2,1},{3,2},{4,7},{5,4},{6,5},{7,6},{8,11},{9,8},{10,9... | collective-permute-start | bytes 909320 | tf_op jit(solution)/shard_map/ppermute | solution.py:32
  120.3 15.5 %collective-permute-start.14 = (bf16[23,8,512]{2,1,0:T(8,128)(2,1)}, bf16[23,8,512]{2,1,0:T(8,128)(2,1)S(1)}, u32[]{:S(2)}, u32[]{:S(2)}) collective-permute-start(bf16[23,8,512]{2,1,0:T(8,128)(2,1)} %get-tuple-element.20), channel_id=1, source_target_pairs={{0,2},{1,3},{2,0},{3,1},{4,6},{5,7},{6,4},{7,5},{8,10},{9,11},{10,... | collective-permute-start | bytes 565256 | tf_op jit(solution)/shard_map/ppermute | solution.py:32
  120.4 15.4 %collective-permute-start.15 = (bf16[23,8,512]{2,1,0:T(8,128)(2,1)}, bf16[23,8,512]{2,1,0:T(8,128)(2,1)S(1)}, u32[]{:S(2)}, u32[]{:S(2)}) collective-permute-start(bf16[23,8,512]{2,1,0:T(8,128)(2,1)} %get-tuple-element.21), channel_id=1, source_target_pairs={{0,1},{1,2},{2,3},{3,0},{4,5},{5,6},{6,7},{7,4},{8,9},{9,10},{10,1... | collective-permute-start | bytes 565256 | tf_op jit(solution)/shard_map/ppermute | solution.py:32
  122.0 13.8 %copy-start.2 = (bf16[32,8,896]{2,1,0:T(8,128)(2,1)}, bf16[32,8,896]{2,1,0:T(8,128)(2,1)S(1)}, u32[]{:S(2)}) copy-start(bf16[32,8,896]{2,1,0:T(8,128)(2,1)S(1)} %slice.72.refs_3_) | copy-start | bytes 1376260
  122.1 11.1 %copy-start.14 = (bf16[37,8,512]{2,1,0:T(8,128)(2,1)}, bf16[37,8,512]{2,1,0:T(8,128)(2,1)S(1)}, u32[]{:S(2)}) copy-start(bf16[37,8,512]{2,1,0:T(8,128)(2,1)S(1)} %collective-permute-done.21.refs_1_) | copy-start | bytes 909316
  122.1 13.8 %collective-permute-start.16 = (bf16[23,8,512]{2,1,0:T(8,128)(2,1)}, bf16[23,8,512]{2,1,0:T(8,128)(2,1)}, u32[]{:S(2)}, u32[]{:S(2)}) collective-permute-start(bf16[23,8,512]{2,1,0:T(8,128)(2,1)} %get-tuple-element.22), channel_id=1, source_target_pairs={{0,3},{1,0},{2,1},{3,2},{4,7},{5,4},{6,5},{7,6},{8,11},{9,8},{10,9... | collective-permute-start | bytes 565256 | tf_op jit(solution)/shard_map/ppermute | solution.py:32
  128.5 4.7 %copy-start.15 = (bf16[37,8,512]{2,1,0:T(8,128)(2,1)}, bf16[37,8,512]{2,1,0:T(8,128)(2,1)S(1)}, u32[]{:S(2)}) copy-start(bf16[37,8,512]{2,1,0:T(8,128)(2,1)S(1)} %collective-permute-done.22.refs_2_) | copy-start | bytes 909316
  128.5 35.1 %collective-permute-start.24 = (bf16[32,8,896]{2,1,0:T(8,128)(2,1)S(1)}, bf16[32,8,896]{2,1,0:T(8,128)(2,1)S(1)}, u32[]{:S(2)}, u32[]{:S(2)}) collective-permute-start(bf16[32,8,896]{2,1,0:T(8,128)(2,1)S(1)} %slice.72.refs_3_), channel_id=1, source_target_pairs={{0,4},{4,0},{1,5},{5,1},{2,6},{6,2},{3,7},{7,3},{8,12},{12,8},{9,1... | collective-permute-start | bytes 1376264 | tf_op jit(solution)/shard_map/ppermute | solution.py:36
  135.8 0.7 copy-start.17
  149.1 14.5 %all-to-all-start.3 = ((f32[32,1,512]{2,1,0:T(1,128)}), f32[32,1,512]{2,1,0:T(1,128)S(1)}, u32[]{:S(2)}, u32[]{:S(2)}) async-start(f32[32,1,512]{2,1,0:T(1,128)} %broadcast_in_dim.17), calls=%async_computation.3 | async-start | bytes 131072 | tf_op jit(solution)/shard_map/all_to_all | solution.py:370
  163.6 0.8 copy-start.13
  (5 other events, 3.2 us)

commit v2 on v1

--- a/solution.py
+++ b/solution.py
@@ -44,7 +44,7 @@
     return jnp.concatenate([c, c], axis=-1), jnp.concatenate([-s, s], axis=-1)
 
 
-def front_kernel(where_ref, tokens_ref, w_ref, left_ref, right_ref, o_ref, out_ref, pad_ref):
+def front_kernel(where_ref, tokens_ref, w_ref, left_ref, right_ref, o_ref, turn_ref, out_ref, pad_ref):
     p = where_ref[0]
     start = pl.multiple_of(jnp.minimum((56 * p) // 128 * 128, 3584 - 256), 128)
     at = pl.multiple_of(56 * p - start, 8)
@@ -61,6 +61,9 @@
     out_ref[:, :, 896:904] = low.reshape(32, 8, 8).astype(BF16)
     both = jnp.concatenate([right_ref[...].astype(F32), o_ref[...].astype(F32)], axis=0)
     out_ref[:, :, 1024:1920] = jnp.broadcast_to(both[None], (32, 8, 896)).astype(BF16)
+    turn = turn_ref[:, pl.ds(pl.multiple_of(896 * where_ref[2], 128), 896)].astype(F32)
+    turn = jnp.concatenate([turn[:, :448], turn[:, 448:]], axis=0) * jnp.where(where_ref[1] == 0, 0.5, -0.5)
+    out_ref[:, :, 1920:2368] = jnp.broadcast_to(turn[None], (32, 8, 448)).astype(BF16)
 
 
 def attention_kernel(heads, where_ref, recv_ref, base_ref, other_ref, keys_ref, values_ref, cos_ref, sin_ref, mixed_ref):
@@ -111,13 +114,13 @@
 def project_kernel(where_ref, *refs):
     pieces, (own_ref, other_ref), out_refs = refs[:5], refs[5:7], refs[7:11]
     w_ref, mixed_ref, hold_ref, sems = refs[11:]
-    groups = 7 * w_ref.shape[1]
+    groups = w_ref.shape[1] // 8
     copies = []
     for d, piece in enumerate(pieces):
-        place = w_ref.at[where_ref[1 + min(d, 3)]]
-        if d >= 3:
-            place = place.at[pl.ds(pieces[3].shape[0] * (d - 3), piece.shape[0])]
-        copies.append(pltpu.make_async_copy(piece, place, sems.at[d]))
+        first = pieces[3].shape[0] if d == 4 else 0
+        for e in range(piece.shape[0]):
+            place = w_ref.at[where_ref[1 + min(d, 3)], pl.ds(56 * (first + e), 56)]
+            copies.append(pltpu.make_async_copy(piece.at[e], place, sems.at[5 * d + e]))
     copies.append(pltpu.make_async_copy(own_ref, mixed_ref.at[0], sems.at[32]))
     copies.append(pltpu.make_async_copy(other_ref, mixed_ref.at[1], sems.at[33]))
     for copy in copies:
@@ -127,7 +130,7 @@
     sides = [pl.ds(pl.multiple_of(256 * a, 128), 256) for a in (where_ref[0], 1 - where_ref[0])]
     outs = []
     for j in range(4):
-        w = w_ref[j].astype(F32).reshape(8 * groups, 896).astype(BF16)
+        w = w_ref[j]
         for i, at in enumerate(sides):
             got = lax.dot_general(w, mixed_ref[i, 0:256, :], NT, preferred_element_type=F32)
             hold_ref[j, 0:groups, :, at] = got.reshape(groups, 8, 256).astype(BF16)
@@ -139,31 +142,49 @@
         copy.wait()
 
 
-def error_kernel(*refs):
-    recv_refs, (right_ref, target_ref, so_far_ref, err_ref) = refs[:4], refs[4:]
+def error_kernel(group, where_ref, *refs):
+    recv_refs, (own_ref, other_ref, target_ref, so_far_ref, err_ref) = refs[:4], refs[4:]
+    core, z = where_ref[0], where_ref[1]
     groups = recv_refs[0].shape[0] - 2
     feats = groups * 8
     total = low = 0.0
     for ref in recv_refs:
         total = total + ref[0:groups].astype(F32)
         low = low + ref[groups : groups + 2].astype(F32)
-    tile = (iota((8, 512), 0) == (iota((8, 512), 1) & 7)).astype(BF16)
-    target = lax.dot_general(target_ref[...], tile, TN, preferred_element_type=F32)
-    total = total.reshape(feats, 512) - target
+    total = total.reshape(feats, 512)
     low = low[0] + low[1]
     low = pltpu.roll(low, 4, 0) + low
+
+    def source(rows):
+        g = iota((rows, feats), 1)
+        at = g + 56 * core
+        for i, e in enumerate(group):
+            shift = 112 * lax.rem(z + 8 - e, 8) - 56 * i
+            at = at + jnp.where((g >= 56 * i) & (g < 56 * i + 56), shift, 0)
+        return at
+
+    wide = (iota((896, feats), 0) == source(896)).astype(BF16)
+    at = source(448)
+    half = (iota((448, feats), 0) == jnp.where(at >= 448, at - 448, at)).astype(BF16)
+    late = source(256) >= 448
+    tile = (iota((8, 512), 0) == (iota((8, 512), 1) & 7)).astype(BF16)
+    target = jnp.dot(target_ref[...], wide, preferred_element_type=F32).astype(BF16)
+    total = total - lax.dot_general(target, tile, TN, preferred_element_type=F32)
+    r, c = iota((256, 512), 0), iota((256, 512), 1)
+    same = (r >> 3) == ((c & 255) >> 3)
     low = jnp.broadcast_to(low[None], (32, 8, 512)).reshape(256, 512)
-    r, c = iota((256, 512), 0), iota((256, 512), 1)
-    mine = ((r >> 3) == ((c & 255) >> 3)) & (((r & 7) >> 2) == (c >> 8))
-    low = jnp.where(mine, low, 0.0)
-    right = right_ref[...]
-    for _ in range(3):
-        piece = low.astype(BF16)
-        total = total + lax.dot_general(right, piece, TN, preferred_element_type=F32)
-        low = low - piece.astype(F32)
+    for side, ref in ((core, own_ref), (1 - core, other_ref)):
+        right = ref[:, :, 896:1344].astype(F32).reshape(256, 448).astype(BF16)
+        right = jnp.dot(right, half, preferred_element_type=F32)
+        right = jnp.where(late == ((iota((256, feats), 0) & 7) >= 4), right, 0.0).astype(BF16)
+        rest = jnp.where(same & ((c >> 8) == side), low, 0.0)
+        for _ in range(3):
+            piece = rest.astype(BF16)
+            total = total + lax.dot_general(right, piece, TN, preferred_element_type=F32)
+            rest = rest - piece.astype(F32)
     err = jnp.sum((total * total).reshape(groups, 8, 512), axis=0)
     err = jnp.sum(err, axis=0, keepdims=True) + so_far_ref[0]
-    err_ref[...] = jnp.broadcast_to(err[None], (8, 1, 512))
+    err_ref[...] = jnp.broadcast_to(err[None], (4, 1, 512))
 
 
 def final_kernel(where_ref, err_ref, left_ref, own_ref, other_ref, query_ref, out_ref, fit_ref):
@@ -193,7 +214,7 @@
         for _ in range(3):
             parts.append(l.astype(BF16))
             l = l - parts[-1].astype(F32)
-        right = ref[...].astype(F32).reshape(256, 896).astype(BF16)
+        right = ref[:, :, 0:896].astype(F32).reshape(256, 896).astype(BF16)
         g = lax.dot_general(jnp.concatenate(parts, axis=1), right, TN, preferred_element_type=F32)
         total = total + g[0:128] + g[128:256] + g[256:384]
     query_ref[...] = total[0:56]
@@ -283,8 +304,8 @@
 
     sent = call(
         front_kernel,
-        shape((32, 8, 1920)),
-        (ints(p, odd), tokens, w_query, left_t, query_right_factors[0], o_left[0].T),
+        shape((32, 8, 2368)),
+        (ints(p, odd, y), tokens, w_query, left_t, query_right_factors[0], o_left[0].T, o_right[0]),
         smem=1,
         scratch=[pltpu.VMEM((256, feats), F32)],
     )
@@ -324,7 +345,7 @@
             (where, *pieces, mixed, mixed_b),
             smem=1,
             scratch=[
-                pltpu.VMEM((4, len(group), 56, feats), BF16),
+                pltpu.VMEM((4, 56 * len(group), feats), BF16),
                 pltpu.VMEM((2, 272, feats), BF16),
                 pltpu.VMEM((4, 7 * len(group) + 2, 8, 512), BF16),
                 pltpu.SemaphoreType.DMA((38,)),
@@ -337,37 +358,27 @@
     for out in outs:
         mets.append([out[0]] + [shift(out[s], "mp", 4, s) for s in (2, 1, 3)])
 
-    order = jnp.array([e for group in GROUPS for e in group])
-    which = (jnp.arange(8)[:, None] - order[None]) % 8
-    o_r = after(o_right[0], sent)
-    o_cut = lax.dynamic_slice(o_r, (0, feats * y), (RANK, feats)).reshape(RANK, 8, 2, 56) * half
-    one = (which[:, :, None] == jnp.arange(8)).astype(BF16)
-    o_cut = jnp.einsum("kiz,rzcf->kcrif", one, o_cut, preferred_element_type=F32).astype(BF16)
-    o_cut = jnp.broadcast_to(o_cut.reshape(1, 16, RANK, 448), (4, 16, RANK, 448)).reshape(64, RANK, 448)
     cut_q = jnp.moveaxis((after(left_t, sent) * twice).reshape(RANK, 64, 56), 1, 0)
-    cut_o = jnp.moveaxis((o_r * twice).reshape(RANK, 64, 56), 1, 0)
+    cut_o = jnp.moveaxis((after(o_right[0], sent) * twice).reshape(RANK, 64, 56), 1, 0)
     gap = jnp.zeros((64, RANK, 8), BF16)
-    late = jnp.concatenate([cut_q, gap, cut_o, gap, o_cut, jnp.zeros((64, RANK, 64), BF16)], axis=2)
+    late = jnp.concatenate([cut_q, gap, cut_o, gap], axis=2)
     late = lax.all_to_all(late, POP, 0, 0, tiled=True)
-    factors = after(recv, outs[0][0])[:, :, 1024:1920]
+    factors = after(recv, mixed)[:, :, 1024:2368]
     factors_b = swap(factors)
-    lefts = late[:, :, :128].reshape(32, 8, 128)
-    goal = lax.dynamic_slice(target, (8 * k, 0), (8, feats)).reshape(8, 8, 2, 56)
-    goal = jnp.where(c == 0, goal[:, :, 0], goal[:, :, 1])
-    here = (((z - order) % 8)[:, None] == jnp.arange(8)).astype(BF16)
-    goal = jnp.einsum("iz,tzf->tif", here, goal, preferred_element_type=F32).astype(BF16).reshape(8, 448)
-    err = jnp.zeros((8, 1, 512), F32)
-    start = 128
+    lefts = late.reshape(32, 8, 128)
+    goal = lax.dynamic_slice(target, (8 * k, 0), (8, feats))
+    err = jnp.zeros((4, 1, 512), F32)
     for group, met in zip(GROUPS, mets):
-        n = 56 * len(group)
-        right = late[:, :, start : start + n].reshape(256, n)
-        part = goal[:, start - 128 : start - 128 + n]
-        start += n
-        err = call(error_kernel, shape((8, 1, 512), F32), (*met, right, part, err))
-
-    err = lax.all_to_all(err, ("pop_2", "mp"), 0, 0, tiled=True)
+        err = call(
+            functools.partial(error_kernel, group),
+            shape((4, 1, 512), F32),
+            (ints(c, z), *met, factors, factors_b, goal, err if met is mets[0] else after(err, late)),
+            smem=1,
+        )
+
+    err = lax.all_to_all(err, "mp", 0, 0, tiled=True)
     err = jnp.sum(err, axis=0, keepdims=True)
-    err = lax.all_to_all(jnp.broadcast_to(err, (32, 1, 512)), CHIPS, 0, 0, tiled=True)
+    err = lax.all_to_all(jnp.broadcast_to(err, (64, 1, 512)), POP, 0, 0, tiled=True)
     grad_query, grad_out, fitness = call(
         final_kernel,
         [shape((56, feats), F32), shape((56, feats), F32), shape((1, 128), F32)],

time: 169 us -> 177 us (1.047)
  waiting for transfers between devices: 40 us -> 45.8 us
  Pallas kernels: 31 us -> 36.1 us
  starting transfers between devices: 61.6 us -> 66.5 us
  local copies, waits for them, and re-layouts: 15.8 us -> 11 us
  blocking collectives: 9.43 us -> 7.38 us
    all_to_all x1, starting transfers between devices: 5.67 us -> 11.8 us  [per_device(): lax.all_to_all(jnp.broadcast_to(err, (64, 1, 512)), POP, 0, 0, tiled=True)]
    pallas_call x9, Pallas kernels: 31 us -> 36.1 us  [call(): pl.pallas_call(kernel, out_shape=out, in_specs=[pl.BlockSpec(memory_space...]
    ppermute x22, waiting for transfers between devices: 32.4 us -> 36.1 us  [shift(): return lax.ppermute(x, axis, [(i, (i + step) % size) for i in range(size)])]
    all_to_all x1, waiting for transfers between devices: 7.55 us -> 9.7 us  [per_device(): lax.all_to_all(jnp.broadcast_to(err, (64, 1, 512)), POP, 0, 0, tiled=True)]
    all_to_all x1, blocking collectives: 9.43 us -> 7.38 us  [per_device(): err = lax.all_to_all(err, 'mp', 0, 0, tiled=True)]
    slice x6 -> x1, local copies, waits for them, and re-layouts: 3.18 us -> 1.16 us  [per_device(): factors = after(recv, mixed)[:, :, 1024:2368]]
    unnamed x50 -> x56, local copies, waits for them, and re-layouts: 3.48 us -> 3.7 us
  transfers between devices with their start and end apart: 28 -> 28, of which waited for: 9 -> 8; matrix products, arithmetic and copies ran while one was open for 12% -> 7% of each run, Pallas kernels for 14% -> 13%
where the time goes in v2:
time: 177 us; the launch traced here: 176 us
  starting transfers between devices  66.5 us (38%)
  waiting for transfers between devices  45.8 us (26%)
  Pallas kernels  36.1 us (20%)
  local copies, waits for them, and re-layouts  11 us (6%)
  blocking collectives  7.38 us (4%)
  other arithmetic  5.27 us (3%)
  between operations  2.17 us (1%)
  matrix products  1.87 us (1%)
    pallas_call x9, Pallas kernels, call(): pl.pallas_call(kernel, out_shape=out, in_specs=[pl.BlockSpec(memory_space...  36.1 us
    ppermute x22, waiting for transfers between devices, shift(): return lax.ppermute(x, axis, [(i, (i + step) % size) for i in range(size)])  36.1 us
    ppermute x22, starting transfers between devices, shift(): return lax.ppermute(x, axis, [(i, (i + step) % size) for i in range(size)])  31 us
    all_to_all x1, starting transfers between devices, per_device(): recv = lax.all_to_all(sent, CHIPS, 0, 0, tiled=True)  12.1 us
    all_to_all x1, starting transfers between devices, per_device(): lax.all_to_all(jnp.broadcast_to(err, (64, 1, 512)), POP, 0, 0, tiled=True)  11.8 us
    all_to_all x1, waiting for transfers between devices, per_device(): lax.all_to_all(jnp.broadcast_to(err, (64, 1, 512)), POP, 0, 0, tiled=True)  9.7 us
    all_to_all x1, starting transfers between devices, per_device(): late = lax.all_to_all(late, POP, 0, 0, tiled=True)  7.48 us
    all_to_all x1, blocking collectives, per_device(): err = lax.all_to_all(err, 'mp', 0, 0, tiled=True)  7.38 us
  transfers between devices with their start and end apart: 28, of which 8 were waited for; matrix products, arithmetic and copies ran while one was open for 7% of the time, Pallas kernels for 13%

profile of v2, /device:TPU:1, one launch (start us, length us, event | category | flops | bytes accessed | tf_op | source)
XLA Modules:
  0.0 176.1 jit_solution(3530628515350799947)
XLA Ops:
  2.0 4.1 %shard_map.130 = bf16[32,8,2368]{2,1,0:T(8,128)(2,1)} custom-call(s32[3]{0:T(128)} %pad_add_fusion.2.refs_0_, bf16[256,3584]{1,0:T(8,128)(2,1)} %refs_1_.1, bf16[56,896]{1,0:T(8,128)(2,1)} %refs_2_.1, bf16[4,3584]{1,0:T(4,128)(2,1)} %bitcast.37, bf16[4,896]{1,0:T(4,128)(2,1)} %bitcast.46, bf16[4,896]{1,0:T(4,128)(2,1)} %bitcast.47, bf16[4,3584]{1,0:T(4,128)(2,1)} %bitcast.39), custom_call_target="tpu_custom_call" | custom-call | flops 1000000000 | bytes 2000000 | tf_op jit(solution)/shard_map/pallas_call | solution.py:254
  6.2 12.1 %all-to-all-start = ((bf16[32,8,2368]{2,1,0:T(8,128)(2,1)}), bf16[32,8,2368]{2,1,0:T(8,128)(2,1)}, u32[]{:S(2)}, u32[]{:S(2)}) async-start(bf16[32,8,2368]{2,1,0:T(8,128)(2,1)} %shard_map.130), calls=%async_computation | async-start | bytes 2490368 | tf_op jit(solution)/shard_map/all_to_all | solution.py:312
  18.3 3.4 %collective-permute-start.6 = (bf16[56,896]{1,0:T(8,128)(2,1)S(1)}, bf16[56,896]{1,0:T(8,128)(2,1)S(1)}, u32[]{:S(2)}, u32[]{:S(2)}) collective-permute-start(bf16[56,896]{1,0:T(8,128)(2,1)S(1)} %bitcast.42), channel_id=1, source_target_pairs={{0,48},{8,56},{16,0},{24,8},{32,16},{40,24},{48,32},{56,40},{1,49}... | collective-permute-start | bytes 301064 | tf_op jit(solution)/shard_map/ppermute | solution.py:32
  21.7 2.7 %collective-permute-start.2 = (bf16[56,896]{1,0:T(8,128)(2,1)S(1)}, bf16[56,896]{1,0:T(8,128)(2,1)S(1)}, u32[]{:S(2)}, u32[]{:S(2)}) collective-permute-start(bf16[56,896]{1,0:T(8,128)(2,1)S(1)} %bitcast.44), channel_id=1, source_target_pairs={{0,56},{8,0},{16,8},{24,16},{32,24},{40,32},{48,40},{56,48},{1,57}... | collective-permute-start | bytes 301064 | tf_op jit(solution)/shard_map/ppermute | solution.py:32
  25.6 0.8 fusion.1.refs_4_
  26.4 1.2 convolution_convert_fusion.refs_5_
  27.7 24.4 %collective-permute-done.4.refs_3_ = bf16[56,896]{1,0:T(8,128)(2,1)S(1)} collective-permute-done((bf16[56,896]{1,0:T(8,128)(2,1)S(1)}, bf16[56,896]{1,0:T(8,128)(2,1)S(1)}, u32[]{:S(2)}, u32[]{:S(2)}) %collective-permute-start.4) | collective-permute-done | bytes 100384 | tf_op jit(solution)/shard_map/ppermute | solution.py:32
  52.1 0.8 collective-permute-done.2.refs_2_
  52.8 1.3 collective-permute-done.refs_1_
  54.1 2.0 %shard_map.134.refs_0_ = bf16[5,56,896]{2,1,0:T(8,128)(2,1)} custom-call(bf16[56,896]{1,0:T(8,128)(2,1)} %bitcast.41, bf16[56,896]{1,0:T(8,128)(2,1)} %collective-permute-done.refs_1_, bf16[56,896]{1,0:T(8,128)(2,1)} %copy-done.22, bf16[56,896]{1,0:T(8,128)(2,1)} %copy-done.13, bf16[56,896]{1,0:T(8,128)(2,1)} %copy-done.9), custom_call_target="tpu_custom_call" | custom-call | flops 1000000000 | bytes 2000000 | tf_op jit(solution)/shard_map/pallas_call | solution.py:254
  56.1 2.5 %collective-permute-start.19 = (bf16[5,56,896]{2,1,0:T(8,128)(2,1)}, bf16[5,56,896]{2,1,0:T(8,128)(2,1)S(1)}, u32[]{:S(2)}, u32[]{:S(2)}) collective-permute-start(bf16[5,56,896]{2,1,0:T(8,128)(2,1)} %shard_map.134.refs_0_), channel_id=1, source_target_pairs={{0,192},{64,0},{128,64},{192,128},{1,193},{65,1},{129,65},{193,129... | collective-permute-start | bytes 1505288 | tf_op jit(solution)/shard_map/ppermute | solution.py:32
  58.6 0.8 slice.47
  59.4 2.9 %collective-permute-start.7 = (bf16[32,896]{1,0:T(8,128)(2,1)S(1)}, bf16[32,896]{1,0:T(8,128)(2,1)S(1)}, u32[]{:S(2)}, u32[]{:S(2)}) collective-permute-start(bf16[32,896]{1,0:T(8,128)(2,1)S(1)} %slice.47), channel_id=1, source_target_pairs={{0,48},{8,56},{16,0},{24,8},{32,16},{40,24},{48,32},{56,40},{1,49}... | collective-permute-start | bytes 172040 | tf_op jit(solution)/shard_map/ppermute | solution.py:32
  62.3 1.7 collective-permute-start.3
  64.0 0.7 collective-permute-start.1
  64.8 3.5 %collective-permute-done.3.refs_1_ = bf16[56,896]{1,0:T(8,128)(2,1)S(1)} collective-permute-done((bf16[56,896]{1,0:T(8,128)(2,1)}, bf16[56,896]{1,0:T(8,128)(2,1)S(1)}, u32[]{:S(2)}, u32[]{:S(2)}) %collective-permute-start.3) | collective-permute-done | bytes 100384 | tf_op jit(solution)/shard_map/ppermute | solution.py:32
  68.3 2.6 %collective-permute-done.1.refs_0_ = bf16[56,896]{1,0:T(8,128)(2,1)S(1)} collective-permute-done((bf16[56,896]{1,0:T(8,128)(2,1)}, bf16[56,896]{1,0:T(8,128)(2,1)S(1)}, u32[]{:S(2)}, u32[]{:S(2)}) %collective-permute-start.1) | collective-permute-done | bytes 100384 | tf_op jit(solution)/shard_map/ppermute | solution.py:32
  71.5 1.7 shard_map.131.refs_0_
  73.3 2.8 %collective-permute-start.9 = (bf16[3,56,896]{2,1,0:T(8,128)(2,1)}, bf16[3,56,896]{2,1,0:T(8,128)(2,1)S(1)}, u32[]{:S(2)}, u32[]{:S(2)}) collective-permute-start(bf16[3,56,896]{2,1,0:T(8,128)(2,1)} %shard_map.131.refs_0_), channel_id=1, source_target_pairs={{0,192},{64,0},{128,64},{192,128},{1,193},{65,1},{129,65},{193,129... | collective-permute-start | bytes 903176 | tf_op jit(solution)/shard_map/ppermute | solution.py:32
  76.0 1.1 convert_reduce_fusion.refs_2_
  77.1 3.4 %collective-permute-start.12 = (f32[8,896]{1,0:T(8,128)S(1)}, f32[8,896]{1,0:T(8,128)S(1)}, u32[]{:S(2)}, u32[]{:S(2)}) collective-permute-start(f32[8,896]{1,0:T(8,128)S(1)} %convert_reduce_fusion.refs_2_), channel_id=1, source_target_pairs={{0,4},{4,0},{1,5},{5,1},{2,6},{6,2},{3,7},{7,3},{8,12},{12,8},{9,1... | collective-permute-start | bytes 86024 | tf_op jit(solution)/shard_map/ppermute | solution.py:36
  80.5 0.7 pad_maximum_fusion.1
  81.2 2.7 %collective-permute-start.21 = (bf16[2,56,896]{2,1,0:T(8,128)(2,1)S(1)}, bf16[2,56,896]{2,1,0:T(8,128)(2,1)}, u32[]{:S(2)}, u32[]{:S(2)}) collective-permute-start(bf16[2,56,896]{2,1,0:T(8,128)(2,1)S(1)} %slice.54), channel_id=1, source_target_pairs={{0,192},{64,0},{128,64},{192,128},{1,193},{65,1},{129,65},{193,129... | collective-permute-start | bytes 602120 | tf_op jit(solution)/shard_map/ppermute | solution.py:32
  84.7 5.4 %shard_map.132.refs_5_ = bf16[272,896]{1,0:T(8,128)(2,1)} custom-call(s32[1]{0:T(128)} %bitcast.18.refs_0_, bf16[32,8,2368]{2,1,0:T(8,128)(2,1)} %all-to-all-done.refs_1_, f32[8,896]{1,0:T(8,128)} %copy-done.12, f32[8,896]{1,0:T(8,128)} %copy-done.27, bf16[256,128]{1,0:T(8,128)(2,1)} %fusion.1.refs_4_, bf16[256,128]{1,0:T(8,128)(2,1)} %convolution_convert_fusion.refs_5_, ...), custom_call_target="tpu_custom_call" | custom-call | flops 1000000000 | bytes 2000000 | tf_op jit(solution)/shard_map/pallas_call | solution.py:254
  90.1 0.7 collective-permute-start.13
  90.8 1.2 slice.42.refs_5_.refs_3_
  93.2 3.0 %collective-permute-start.11 = (bf16[2,56,896]{2,1,0:T(8,128)(2,1)S(1)}, bf16[2,56,896]{2,1,0:T(8,128)(2,1)}, u32[]{:S(2)}, u32[]{:S(2)}) collective-permute-start(bf16[2,56,896]{2,1,0:T(8,128)(2,1)S(1)} %slice.49), channel_id=1, source_target_pairs={{0,192},{64,0},{128,64},{192,128},{1,193},{65,1},{129,65},{193,129... | collective-permute-start | bytes 602120 | tf_op jit(solution)/shard_map/ppermute | solution.py:32
  96.1 0.9 slice.48
  97.1 0.7 collective-permute-done.20.refs_3_
  97.8 0.8 copy-done.14
  98.6 5.1 %shard_map.135 = (bf16[37,8,512]{2,1,0:T(8,128)(2,1)}, bf16[37,8,512]{2,1,0:T(8,128)(2,1)}, bf16[37,8,512]{2,1,0:T(8,128)(2,1)}, bf16[37,8,512]{2,1,0:T(8,128)(2,1)}) custom-call(s32[5]{0:T(128)} %stack.59.where_ref, bf16[5,56,896]{2,1,0:T(8,128)(2,1)} %shard_map.134.refs_0_, bf16[5,56,896]{2,1,0:T(8,128)(2,1)} %copy-done.4, bf16[5,56,896]{2,1,0:T(8,128)(2,1)} %copy-done.7, ...), custom_call_target="tpu_custom_call" | custom-call | flops 1000000000 | bytes 2000000 | tf_op jit(solution)/shard_map/pallas_call | solution.py:254
  103.7 3.0 %collective-permute-start.22 = (bf16[37,8,512]{2,1,0:T(8,128)(2,1)}, bf16[37,8,512]{2,1,0:T(8,128)(2,1)S(1)}, u32[]{:S(2)}, u32[]{:S(2)}) collective-permute-start(bf16[37,8,512]{2,1,0:T(8,128)(2,1)} %get-tuple-element.26), channel_id=1, source_target_pairs={{0,2},{1,3},{2,0},{3,1},{4,6},{5,7},{6,4},{7,5},{8,10},{9,11},{10,... | collective-permute-start | bytes 909320 | tf_op jit(solution)/shard_map/ppermute | solution.py:32
  106.9 0.7 copy.26
  107.5 7.5 %all-to-all-start.1 = ((bf16[64,4,128]{2,1,0:T(4,128)(2,1)}), bf16[64,4,128]{2,1,0:T(4,128)(2,1)S(1)}, u32[]{:S(2)}, u32[]{:S(2)}) async-start(bf16[64,4,128]{2,1,0:T(4,128)(2,1)} %copy.26), calls=%async_computation.1 | async-start | bytes 131072 | tf_op jit(solution)/shard_map/all_to_all | solution.py:365
  115.5 2.3 %collective-permute-start.24 = (bf16[37,8,512]{2,1,0:T(8,128)(2,1)}, bf16[37,8,512]{2,1,0:T(8,128)(2,1)S(1)}, u32[]{:S(2)}, u32[]{:S(2)}) collective-permute-start(bf16[37,8,512]{2,1,0:T(8,128)(2,1)} %get-tuple-element.28), channel_id=1, source_target_pairs={{0,3},{1,0},{2,1},{3,2},{4,7},{5,4},{6,5},{7,6},{8,11},{9,8},{10,9... | collective-permute-start | bytes 909320 | tf_op jit(solution)/shard_map/ppermute | solution.py:32
  117.8 1.3 constant_dynamic-slice_fusion.refs_7_
  119.1 4.7 %shard_map.133 = (bf16[23,8,512]{2,1,0:T(8,128)(2,1)}, bf16[23,8,512]{2,1,0:T(8,128)(2,1)}, bf16[23,8,512]{2,1,0:T(8,128)(2,1)}, bf16[23,8,512]{2,1,0:T(8,128)(2,1)}) custom-call(s32[5]{0:T(128)} %stack.59.where_ref, bf16[3,56,896]{2,1,0:T(8,128)(2,1)} %shard_map.131.refs_0_, bf16[3,56,896]{2,1,0:T(8,128)(2,1)} %collective-permute-done.8.refs_1_, ...), custom_call_target="tpu_custom_call" | custom-call | flops 1000000000 | bytes 2000000 | tf_op jit(solution)/shard_map/pallas_call | solution.py:254
  124.5 2.2 %collective-permute-start.16 = (bf16[23,8,512]{2,1,0:T(8,128)(2,1)}, bf16[23,8,512]{2,1,0:T(8,128)(2,1)S(1)}, u32[]{:S(2)}, u32[]{:S(2)}) collective-permute-start(bf16[23,8,512]{2,1,0:T(8,128)(2,1)} %get-tuple-element.23), channel_id=1, source_target_pairs={{0,3},{1,0},{2,1},{3,2},{4,7},{5,4},{6,5},{7,6},{8,11},{9,8},{10,9... | collective-permute-start | bytes 565256 | tf_op jit(solution)/shard_map/ppermute | solution.py:32
  126.7 0.7 pad_add_fusion.1.refs_0_
  128.2 4.8 %shard_map.136.refs_8_ = f32[4,1,512]{2,1,0:T(1,128)} custom-call(s32[2]{0:T(128)} %pad_add_fusion.1.refs_0_, bf16[37,8,512]{2,1,0:T(8,128)(2,1)} %get-tuple-element.25.refs_1_, bf16[37,8,512]{2,1,0:T(8,128)(2,1)} %copy-done.15, bf16[37,8,512]{2,1,0:T(8,128)(2,1)} %copy-done.16, bf16[37,8,512]{2,1,0:T(8,128)(2,1)} %copy-done.17, ...), custom_call_target="tpu_custom_call" | custom-call | flops 1000000000 | bytes 2000000 | tf_op jit(solution)/shard_map/pallas_call | solution.py:254
  133.0 2.9 %collective-permute-done.15.refs_3_ = bf16[23,8,512]{2,1,0:T(8,128)(2,1)S(1)} collective-permute-done((bf16[23,8,512]{2,1,0:T(8,128)(2,1)}, bf16[23,8,512]{2,1,0:T(8,128)(2,1)S(1)}, u32[]{:S(2)}, u32[]{:S(2)}) %collective-permute-start.15) | collective-permute-done | bytes 188448 | tf_op jit(solution)/shard_map/ppermute | solution.py:32
  136.6 4.6 %shard_map.137 = f32[4,1,512]{2,1,0:T(1,128)} custom-call(s32[2]{0:T(128)} %pad_add_fusion.1.refs_0_, bf16[23,8,512]{2,1,0:T(8,128)(2,1)} %get-tuple-element.20.refs_1_, bf16[23,8,512]{2,1,0:T(8,128)(2,1)} %copy-done.18, bf16[23,8,512]{2,1,0:T(8,128)(2,1)} %copy-done.19, bf16[23,8,512]{2,1,0:T(8,128)(2,1)} %copy-done.20, bf16[32,8,1344]{2,1,0:T(8,128)(2,1)} %copy-done.3, ...), custom_call_target="tpu_custom_call" | custom-call | flops 1000000000 | bytes 2000000 | tf_op jit(solution)/shard_map/pallas_call | solution.py:254
  141.2 7.4 %all_to_all.20 = f32[4,1,512]{2,1,0:T(1,128)S(1)} all-to-all(f32[4,1,512]{2,1,0:T(1,128)} %shard_map.137), channel_id=1, replica_groups=mesh['pop_0'=4,'pop_1'=8,'pop_2'=2,'mp'=4] {'mp'}, dimensions={0} | all-to-all | bytes 16384 | tf_op jit(solution)/shard_map/all_to_all | solution.py:379
  148.6 0.7 broadcast_in_dim.8
  149.4 11.8 %all-to-all-start.3 = ((f32[64,1,512]{2,1,0:T(1,128)}), f32[64,1,512]{2,1,0:T(1,128)S(1)}, u32[]{:S(2)}, u32[]{:S(2)}) async-start(f32[64,1,512]{2,1,0:T(1,128)} %broadcast_in_dim.8), calls=%async_computation.3 | async-start | bytes 262144 | tf_op jit(solution)/shard_map/all_to_all | solution.py:381
  161.8 9.7 %all-to-all-done.3.refs_1_ = f32[64,1,512]{2,1,0:T(1,128)S(1)} async-done(((f32[64,1,512]{2,1,0:T(1,128)}), f32[64,1,512]{2,1,0:T(1,128)S(1)}, u32[]{:S(2)}, u32[]{:S(2)}) %all-to-all-start.3) | async-done | bytes 131104 | tf_op jit(solution)/shard_map/all_to_all | solution.py:381
  171.5 0.7 copy-done.6
  172.1 3.8 %shard_map.138 = (f32[56,896]{1,0:T(8,128)}, f32[56,896]{1,0:T(8,128)}, f32[1,128]{1,0:T(1,128)}) custom-call(s32[2]{0:T(128)} %pad_add_fusion.refs_0_, f32[64,1,512]{2,1,0:T(1,128)} %copy-done.6, bf16[32,8,128]{2,1,0:T(8,128)(2,1)} %bitcast.36, bf16[32,8,1344]{2,1,0:T(8,128)(2,1)} %copy-done.3, bf16[32,8,1344]{2,1,0:T(8,128)(2,1)} %collective-permute-done.17.refs_6_.refs_4_), custom_call_target="tpu_custom_call" | custom-call | flops 1000000000 | bytes 2000000 | tf_op jit(solution)/shard_map/pallas_call | solution.py:254
  (105 shorter events, 8.1 us)
Async XLA Ops:
  0.6 23.7 %copy-start = (bf16[3584,128]{1,0:T(8,128)(2,1)S(1)}, bf16[3584,128]{1,0:T(8,128)(2,1)}, u32[]{:S(2)}) copy-start(bf16[3584,128]{1,0:T(8,128)(2,1)} %param.14) | copy-start | bytes 2752516
  6.1 12.1 %copy-start.21 = (bf16[896,56]{0,1:T(8,128)(2,1)S(1)}, bf16[896,56]{0,1:T(8,128)(2,1)}, u32[]{:S(2)}) copy-start(bf16[896,56]{0,1:T(8,128)(2,1)} %param.16) | copy-start | bytes 301060
  6.2 18.2 %copy-start.1 = (bf16[256,3584]{1,0:T(8,128)(2,1)S(1)}, bf16[256,3584]{1,0:T(8,128)(2,1)}, u32[]{:S(2)}) copy-start(bf16[256,3584]{1,0:T(8,128)(2,1)} %refs_1_.1) | copy-start | bytes 5505028
  6.2 69.9 %all-to-all-start = ((bf16[32,8,2368]{2,1,0:T(8,128)(2,1)}), bf16[32,8,2368]{2,1,0:T(8,128)(2,1)}, u32[]{:S(2)}, u32[]{:S(2)}) async-start(bf16[32,8,2368]{2,1,0:T(8,128)(2,1)} %shard_map.130), calls=%async_computation | async-start | bytes 2490368 | tf_op jit(solution)/shard_map/all_to_all | solution.py:312
  18.3 33.8 %collective-permute-start.6 = (bf16[56,896]{1,0:T(8,128)(2,1)S(1)}, bf16[56,896]{1,0:T(8,128)(2,1)S(1)}, u32[]{:S(2)}, u32[]{:S(2)}) collective-permute-start(bf16[56,896]{1,0:T(8,128)(2,1)S(1)} %bitcast.42), channel_id=1, source_target_pairs={{0,48},{8,56},{16,0},{24,8},{32,16},{40,24},{48,32},{56,40},{1,49}... | collective-permute-start | bytes 301064 | tf_op jit(solution)/shard_map/ppermute | solution.py:32
  21.7 30.4 %collective-permute-start.4 = (bf16[56,896]{1,0:T(8,128)(2,1)S(1)}, bf16[56,896]{1,0:T(8,128)(2,1)S(1)}, u32[]{:S(2)}, u32[]{:S(2)}) collective-permute-start(bf16[56,896]{1,0:T(8,128)(2,1)S(1)} %bitcast.43), channel_id=1, source_target_pairs={{0,16},{8,24},{16,32},{24,40},{32,48},{40,56},{48,0},{56,8},{1,17}... | collective-permute-start | bytes 301064 | tf_op jit(solution)/shard_map/ppermute | solution.py:32
  21.7 31.2 %collective-permute-start.2 = (bf16[56,896]{1,0:T(8,128)(2,1)S(1)}, bf16[56,896]{1,0:T(8,128)(2,1)S(1)}, u32[]{:S(2)}, u32[]{:S(2)}) collective-permute-start(bf16[56,896]{1,0:T(8,128)(2,1)S(1)} %bitcast.44), channel_id=1, source_target_pairs={{0,56},{8,0},{16,8},{24,16},{32,24},{40,32},{48,40},{56,48},{1,57}... | collective-permute-start | bytes 301064 | tf_op jit(solution)/shard_map/ppermute | solution.py:32
  24.3 29.7 %collective-permute-start = (bf16[56,896]{1,0:T(8,128)(2,1)S(1)}, bf16[56,896]{1,0:T(8,128)(2,1)}, u32[]{:S(2)}, u32[]{:S(2)}) collective-permute-start(bf16[56,896]{1,0:T(8,128)(2,1)S(1)} %bitcast.45), channel_id=1, source_target_pairs={{0,8},{8,16},{16,24},{24,32},{32,40},{40,48},{48,56},{56,0},{1,9},... | collective-permute-start | bytes 301064 | tf_op jit(solution)/shard_map/ppermute | solution.py:32
  24.4 2.1 %copy-start.2 = (bf16[3584,128]{1,0:T(8,128)(2,1)S(1)}, bf16[3584,128]{1,0:T(8,128)(2,1)}, u32[]{:S(2)}) copy-start(bf16[3584,128]{1,0:T(8,128)(2,1)} %param.15) | copy-start | bytes 2752516
  52.0 2.0 %copy-start.13 = (bf16[56,896]{1,0:T(8,128)(2,1)}, bf16[56,896]{1,0:T(8,128)(2,1)S(1)}, u32[]{:S(2)}) copy-start(bf16[56,896]{1,0:T(8,128)(2,1)S(1)} %collective-permute-done.4.refs_3_) | copy-start | bytes 301060
  52.0 11.9 %collective-permute-start.5 = (bf16[24,896]{1,0:T(8,128)(2,1)S(1)}, bf16[24,896]{1,0:T(8,128)(2,1)S(1)}, u32[]{:S(2)}, u32[]{:S(2)}) collective-permute-start(bf16[24,896]{1,0:T(8,128)(2,1)S(1)} %slice.46), channel_id=1, source_target_pairs={{0,16},{8,24},{16,32},{24,40},{32,48},{40,56},{48,0},{56,8},{1,17}... | collective-permute-start | bytes 129032 | tf_op jit(solution)/shard_map/ppermute | solution.py:32
  52.1 2.0 %copy-start.9 = (bf16[56,896]{1,0:T(8,128)(2,1)}, bf16[56,896]{1,0:T(8,128)(2,1)S(1)}, u32[]{:S(2)}) copy-start(bf16[56,896]{1,0:T(8,128)(2,1)S(1)} %collective-permute-done.6.refs_4_) | copy-start | bytes 301060
  52.8 1.3 copy-start.22
  56.1 25.1 %collective-permute-start.19 = (bf16[5,56,896]{2,1,0:T(8,128)(2,1)}, bf16[5,56,896]{2,1,0:T(8,128)(2,1)S(1)}, u32[]{:S(2)}, u32[]{:S(2)}) collective-permute-start(bf16[5,56,896]{2,1,0:T(8,128)(2,1)} %shard_map.134.refs_0_), channel_id=1, source_target_pairs={{0,192},{64,0},{128,64},{192,128},{1,193},{65,1},{129,65},{193,129... | collective-permute-start | bytes 1505288 | tf_op jit(solution)/shard_map/ppermute | solution.py:32
  58.6 25.4 %collective-permute-start.18 = (bf16[5,56,896]{2,1,0:T(8,128)(2,1)}, bf16[5,56,896]{2,1,0:T(8,128)(2,1)S(1)}, u32[]{:S(2)}, u32[]{:S(2)}) collective-permute-start(bf16[5,56,896]{2,1,0:T(8,128)(2,1)} %shard_map.134.refs_0_), channel_id=1, source_target_pairs={{0,64},{64,128},{128,192},{192,0},{1,65},{65,129},{129,193},{193,1... | collective-permute-start | bytes 1505288 | tf_op jit(solution)/shard_map/ppermute | solution.py:32
  59.4 5.4 %collective-permute-start.7 = (bf16[32,896]{1,0:T(8,128)(2,1)S(1)}, bf16[32,896]{1,0:T(8,128)(2,1)S(1)}, u32[]{:S(2)}, u32[]{:S(2)}) collective-permute-start(bf16[32,896]{1,0:T(8,128)(2,1)S(1)} %slice.47), channel_id=1, source_target_pairs={{0,48},{8,56},{16,0},{24,8},{32,16},{40,24},{48,32},{56,40},{1,49}... | collective-permute-start | bytes 172040 | tf_op jit(solution)/shard_map/ppermute | solution.py:32
  62.3 6.0 %collective-permute-start.3 = (bf16[56,896]{1,0:T(8,128)(2,1)}, bf16[56,896]{1,0:T(8,128)(2,1)S(1)}, u32[]{:S(2)}, u32[]{:S(2)}) collective-permute-start(bf16[56,896]{1,0:T(8,128)(2,1)} %copy-done.22), channel_id=1, source_target_pairs={{0,48},{8,56},{16,0},{24,8},{32,16},{40,24},{48,32},{56,40},{1,49}... | collective-permute-start | bytes 301064 | tf_op jit(solution)/shard_map/ppermute | solution.py:32
  64.0 6.9 %copy-start.26 = (bf16[24,896]{1,0:T(8,128)(2,1)}, bf16[24,896]{1,0:T(8,128)(2,1)S(1)}, u32[]{:S(2)}) copy-start(bf16[24,896]{1,0:T(8,128)(2,1)S(1)} %collective-permute-done.5.refs_2_) | copy-start | bytes 129028
  64.0 6.9 %collective-permute-start.1 = (bf16[56,896]{1,0:T(8,128)(2,1)}, bf16[56,896]{1,0:T(8,128)(2,1)S(1)}, u32[]{:S(2)}, u32[]{:S(2)}) collective-permute-start(bf16[56,896]{1,0:T(8,128)(2,1)} %collective-permute-done.refs_1_), channel_id=1, source_target_pairs={{0,16},{8,24},{16,32},{24,40},{32,48},{40,56},{48,0},{56,8},{1,17}... | collective-permute-start | bytes 301064 | tf_op jit(solution)/shard_map/ppermute | solution.py:32
  64.8 6.1 %copy-start.25 = (bf16[32,896]{1,0:T(8,128)(2,1)}, bf16[32,896]{1,0:T(8,128)(2,1)S(1)}, u32[]{:S(2)}) copy-start(bf16[32,896]{1,0:T(8,128)(2,1)S(1)} %collective-permute-done.7.refs_3_) | copy-start | bytes 172036
  68.3 2.6 %copy-start.23 = (bf16[56,896]{1,0:T(8,128)(2,1)}, bf16[56,896]{1,0:T(8,128)(2,1)S(1)}, u32[]{:S(2)}) copy-start(bf16[56,896]{1,0:T(8,128)(2,1)S(1)} %collective-permute-done.3.refs_1_) | copy-start | bytes 301060
  73.3 18.7 %collective-permute-start.9 = (bf16[3,56,896]{2,1,0:T(8,128)(2,1)}, bf16[3,56,896]{2,1,0:T(8,128)(2,1)S(1)}, u32[]{:S(2)}, u32[]{:S(2)}) collective-permute-start(bf16[3,56,896]{2,1,0:T(8,128)(2,1)} %shard_map.131.refs_0_), channel_id=1, source_target_pairs={{0,192},{64,0},{128,64},{192,128},{1,193},{65,1},{129,65},{193,129... | collective-permute-start | bytes 903176 | tf_op jit(solution)/shard_map/ppermute | solution.py:32
  77.1 7.0 %copy-start.12 = (f32[8,896]{1,0:T(8,128)}, f32[8,896]{1,0:T(8,128)S(1)}, u32[]{:S(2)}) copy-start(f32[8,896]{1,0:T(8,128)S(1)} %convert_reduce_fusion.refs_2_) | copy-start | bytes 86020
  77.1 6.9 %collective-permute-start.12 = (f32[8,896]{1,0:T(8,128)S(1)}, f32[8,896]{1,0:T(8,128)S(1)}, u32[]{:S(2)}, u32[]{:S(2)}) collective-permute-start(f32[8,896]{1,0:T(8,128)S(1)} %convert_reduce_fusion.refs_2_), channel_id=1, source_target_pairs={{0,4},{4,0},{1,5},{5,1},{2,6},{6,2},{3,7},{7,3},{8,12},{12,8},{9,1... | collective-permute-start | bytes 86024 | tf_op jit(solution)/shard_map/ppermute | solution.py:36
  81.2 12.0 %collective-permute-start.8 = (bf16[3,56,896]{2,1,0:T(8,128)(2,1)}, bf16[3,56,896]{2,1,0:T(8,128)(2,1)}, u32[]{:S(2)}, u32[]{:S(2)}) collective-permute-start(bf16[3,56,896]{2,1,0:T(8,128)(2,1)} %shard_map.131.refs_0_), channel_id=1, source_target_pairs={{0,64},{64,128},{128,192},{192,0},{1,65},{65,129},{129,193},{193,1... | collective-permute-start | bytes 903176 | tf_op jit(solution)/shard_map/ppermute | solution.py:32
  81.2 8.9 %copy-start.7 = (bf16[5,56,896]{2,1,0:T(8,128)(2,1)}, bf16[5,56,896]{2,1,0:T(8,128)(2,1)S(1)}, u32[]{:S(2)}) copy-start(bf16[5,56,896]{2,1,0:T(8,128)(2,1)S(1)} %collective-permute-done.19.refs_2_) | copy-start | bytes 1505284
  81.2 15.8 %collective-permute-start.21 = (bf16[2,56,896]{2,1,0:T(8,128)(2,1)S(1)}, bf16[2,56,896]{2,1,0:T(8,128)(2,1)}, u32[]{:S(2)}, u32[]{:S(2)}) collective-permute-start(bf16[2,56,896]{2,1,0:T(8,128)(2,1)S(1)} %slice.54), channel_id=1, source_target_pairs={{0,192},{64,0},{128,64},{192,128},{1,193},{65,1},{129,65},{193,129... | collective-permute-start | bytes 602120 | tf_op jit(solution)/shard_map/ppermute | solution.py:32
  84.0 6.2 %copy-start.4 = (bf16[5,56,896]{2,1,0:T(8,128)(2,1)}, bf16[5,56,896]{2,1,0:T(8,128)(2,1)S(1)}, u32[]{:S(2)}) copy-start(bf16[5,56,896]{2,1,0:T(8,128)(2,1)S(1)} %collective-permute-done.18.refs_1_) | copy-start | bytes 1505284
  84.0 13.8 %collective-permute-start.20 = (bf16[3,56,896]{2,1,0:T(8,128)(2,1)S(1)}, bf16[3,56,896]{2,1,0:T(8,128)(2,1)}, u32[]{:S(2)}, u32[]{:S(2)}) collective-permute-start(bf16[3,56,896]{2,1,0:T(8,128)(2,1)S(1)} %slice.53), channel_id=1, source_target_pairs={{0,64},{64,128},{128,192},{192,0},{1,65},{65,129},{129,193},{193,1... | collective-permute-start | bytes 903176 | tf_op jit(solution)/shard_map/ppermute | solution.py:32
  84.7 7.4 %copy-start.10 = (bf16[1,3584,4]{1,2,0:T(4,128)(2,1)S(1)}, bf16[1,3584,4]{1,2,0:T(4,128)(2,1)}, u32[]{:S(2)}) copy-start(bf16[1,3584,4]{1,2,0:T(4,128)(2,1)} %param.17) | copy-start | bytes 86020
  84.7 7.4 %copy-start.11 = (bf16[1,4,3584]{2,1,0:T(4,128)(2,1)S(1)}, bf16[1,4,3584]{2,1,0:T(4,128)(2,1)}, u32[]{:S(2)}) copy-start(bf16[1,4,3584]{2,1,0:T(4,128)(2,1)} %param.20) | copy-start | bytes 86020
  90.1 7.7 %collective-permute-start.13 = (bf16[272,896]{1,0:T(8,128)(2,1)}, bf16[272,896]{1,0:T(8,128)(2,1)S(1)}, u32[]{:S(2)}, u32[]{:S(2)}) collective-permute-start(bf16[272,896]{1,0:T(8,128)(2,1)} %shard_map.132.refs_5_), channel_id=1, source_target_pairs={{0,4},{4,0},{1,5},{5,1},{2,6},{6,2},{3,7},{7,3},{8,12},{12,8},{9,1... | collective-permute-start | bytes 1462280 | tf_op jit(solution)/shard_map/ppermute | solution.py:36
  91.9 11.8 %copy-start.3 = (bf16[32,8,1344]{2,1,0:T(8,128)(2,1)}, bf16[32,8,1344]{2,1,0:T(8,128)(2,1)S(1)}, u32[]{:S(2)}) copy-start(bf16[32,8,1344]{2,1,0:T(8,128)(2,1)S(1)} %slice.42.refs_5_.refs_3_) | copy-start | bytes 2064388
  92.0 11.7 %copy-start.5 = (bf16[3,56,896]{2,1,0:T(8,128)(2,1)}, bf16[3,56,896]{2,1,0:T(8,128)(2,1)S(1)}, u32[]{:S(2)}) copy-start(bf16[3,56,896]{2,1,0:T(8,128)(2,1)S(1)} %collective-permute-done.9.refs_2_) | copy-start | bytes 903172
  92.0 31.9 %collective-permute-start.17 = (bf16[32,8,1344]{2,1,0:T(8,128)(2,1)S(1)}, bf16[32,8,1344]{2,1,0:T(8,128)(2,1)}, u32[]{:S(2)}, u32[]{:S(2)}) collective-permute-start(bf16[32,8,1344]{2,1,0:T(8,128)(2,1)S(1)} %slice.42.refs_5_.refs_3_), channel_id=1, source_target_pairs={{0,4},{4,0},{1,5},{5,1},{2,6},{6,2},{3,7},{7,3},{8,12},{12,8},{9,1... | collective-permute-start | bytes 2064392 | tf_op jit(solution)/shard_map/ppermute | solution.py:36
  93.2 25.9 %collective-permute-start.11 = (bf16[2,56,896]{2,1,0:T(8,128)(2,1)S(1)}, bf16[2,56,896]{2,1,0:T(8,128)(2,1)}, u32[]{:S(2)}, u32[]{:S(2)}) collective-permute-start(bf16[2,56,896]{2,1,0:T(8,128)(2,1)S(1)} %slice.49), channel_id=1, source_target_pairs={{0,192},{64,0},{128,64},{192,128},{1,193},{65,1},{129,65},{193,129... | collective-permute-start | bytes 602120 | tf_op jit(solution)/shard_map/ppermute | solution.py:32
  97.1 18.5 %collective-permute-start.10 = (bf16[1,56,896]{2,1,0:T(8,128)(2,1)S(1)}, bf16[1,56,896]{2,1,0:T(8,128)(2,1)}, u32[]{:S(2)}, u32[]{:S(2)}) collective-permute-start(bf16[1,56,896]{2,1,0:T(8,128)(2,1)S(1)} %slice.48), channel_id=1, source_target_pairs={{0,64},{64,128},{128,192},{192,0},{1,65},{65,129},{129,193},{193,1... | collective-permute-start | bytes 301064 | tf_op jit(solution)/shard_map/ppermute | solution.py:32
  103.7 20.8 %collective-permute-start.22 = (bf16[37,8,512]{2,1,0:T(8,128)(2,1)}, bf16[37,8,512]{2,1,0:T(8,128)(2,1)S(1)}, u32[]{:S(2)}, u32[]{:S(2)}) collective-permute-start(bf16[37,8,512]{2,1,0:T(8,128)(2,1)} %get-tuple-element.26), channel_id=1, source_target_pairs={{0,2},{1,3},{2,0},{3,1},{4,6},{5,7},{6,4},{7,5},{8,10},{9,11},{10,... | collective-permute-start | bytes 909320 | tf_op jit(solution)/shard_map/ppermute | solution.py:32
  107.5 25.4 %all-to-all-start.1 = ((bf16[64,4,128]{2,1,0:T(4,128)(2,1)}), bf16[64,4,128]{2,1,0:T(4,128)(2,1)S(1)}, u32[]{:S(2)}, u32[]{:S(2)}) async-start(bf16[64,4,128]{2,1,0:T(4,128)(2,1)} %copy.26), calls=%async_computation.1 | async-start | bytes 131072 | tf_op jit(solution)/shard_map/all_to_all | solution.py:365
  115.0 12.3 %collective-permute-start.23 = (bf16[37,8,512]{2,1,0:T(8,128)(2,1)}, bf16[37,8,512]{2,1,0:T(8,128)(2,1)S(1)}, u32[]{:S(2)}, u32[]{:S(2)}) collective-permute-start(bf16[37,8,512]{2,1,0:T(8,128)(2,1)} %get-tuple-element.27), channel_id=1, source_target_pairs={{0,1},{1,2},{2,3},{3,0},{4,5},{5,6},{6,7},{7,4},{8,9},{9,10},{10,1... | collective-permute-start | bytes 909320 | tf_op jit(solution)/shard_map/ppermute | solution.py:32
  115.5 11.8 %collective-permute-start.24 = (bf16[37,8,512]{2,1,0:T(8,128)(2,1)}, bf16[37,8,512]{2,1,0:T(8,128)(2,1)S(1)}, u32[]{:S(2)}, u32[]{:S(2)}) collective-permute-start(bf16[37,8,512]{2,1,0:T(8,128)(2,1)} %get-tuple-element.28), channel_id=1, source_target_pairs={{0,3},{1,0},{2,1},{3,2},{4,7},{5,4},{6,5},{7,6},{8,11},{9,8},{10,9... | collective-permute-start | bytes 909320 | tf_op jit(solution)/shard_map/ppermute | solution.py:32
  123.8 9.2 %collective-permute-start.14 = (bf16[23,8,512]{2,1,0:T(8,128)(2,1)}, bf16[23,8,512]{2,1,0:T(8,128)(2,1)S(1)}, u32[]{:S(2)}, u32[]{:S(2)}) collective-permute-start(bf16[23,8,512]{2,1,0:T(8,128)(2,1)} %get-tuple-element.21), channel_id=1, source_target_pairs={{0,2},{1,3},{2,0},{3,1},{4,6},{5,7},{6,4},{7,5},{8,10},{9,11},{10,... | collective-permute-start | bytes 565256 | tf_op jit(solution)/shard_map/ppermute | solution.py:32
  123.9 12.0 %collective-permute-start.15 = (bf16[23,8,512]{2,1,0:T(8,128)(2,1)}, bf16[23,8,512]{2,1,0:T(8,128)(2,1)S(1)}, u32[]{:S(2)}, u32[]{:S(2)}) collective-permute-start(bf16[23,8,512]{2,1,0:T(8,128)(2,1)} %get-tuple-element.22), channel_id=1, source_target_pairs={{0,1},{1,2},{2,3},{3,0},{4,5},{5,6},{6,7},{7,4},{8,9},{9,10},{10,1... | collective-permute-start | bytes 565256 | tf_op jit(solution)/shard_map/ppermute | solution.py:32
  124.5 3.5 %copy-start.15 = (bf16[37,8,512]{2,1,0:T(8,128)(2,1)}, bf16[37,8,512]{2,1,0:T(8,128)(2,1)S(1)}, u32[]{:S(2)}) copy-start(bf16[37,8,512]{2,1,0:T(8,128)(2,1)S(1)} %collective-permute-done.22.refs_2_) | copy-start | bytes 909316
  124.5 11.4 %collective-permute-start.16 = (bf16[23,8,512]{2,1,0:T(8,128)(2,1)}, bf16[23,8,512]{2,1,0:T(8,128)(2,1)S(1)}, u32[]{:S(2)}, u32[]{:S(2)}) collective-permute-start(bf16[23,8,512]{2,1,0:T(8,128)(2,1)} %get-tuple-element.23), channel_id=1, source_target_pairs={{0,3},{1,0},{2,1},{3,2},{4,7},{5,4},{6,5},{7,6},{8,11},{9,8},{10,9... | collective-permute-start | bytes 565256 | tf_op jit(solution)/shard_map/ppermute | solution.py:32
  133.0 8.2 %copy-start.8 = (bf16[64,4,128]{2,1,0:T(4,128)(2,1)}, bf16[64,4,128]{2,1,0:T(4,128)(2,1)S(1)}, u32[]{:S(2)}) copy-start(bf16[64,4,128]{2,1,0:T(4,128)(2,1)S(1)} %all-to-all-done.1) | copy-start | bytes 196612
  133.0 2.9 %copy-start.18 = (bf16[23,8,512]{2,1,0:T(8,128)(2,1)}, bf16[23,8,512]{2,1,0:T(8,128)(2,1)S(1)}, u32[]{:S(2)}) copy-start(bf16[23,8,512]{2,1,0:T(8,128)(2,1)S(1)} %collective-permute-done.14.refs_2_) | copy-start | bytes 565252
  149.4 22.1 %all-to-all-start.3 = ((f32[64,1,512]{2,1,0:T(1,128)}), f32[64,1,512]{2,1,0:T(1,128)S(1)}, u32[]{:S(2)}, u32[]{:S(2)}) async-start(f32[64,1,512]{2,1,0:T(1,128)} %broadcast_in_dim.8), calls=%async_computation.3 | async-start | bytes 262144 | tf_op jit(solution)/shard_map/all_to_all | solution.py:381
  (8 other events, 5.7 us)

commit v3 on v1

--- a/solution.py
+++ b/solution.py
@@ -100,46 +100,48 @@
 
 def stack_kernel(*refs):
     *ins, out_ref = refs
-    for e in range(out_ref.shape[0] - 1):
-        out_ref[e] = ins[e][...]
-    at = 0
-    for ref in ins[out_ref.shape[0] - 1 :]:
-        out_ref[out_ref.shape[0] - 1, at : at + ref.shape[0]] = ref[...]
-        at += ref.shape[0]
+    for e, ref in enumerate(ins):
+        out_ref[e] = ref[...]
 
 
 def project_kernel(where_ref, *refs):
     pieces, (own_ref, other_ref), out_refs = refs[:5], refs[5:7], refs[7:11]
-    w_ref, mixed_ref, hold_ref, sems = refs[11:]
+    w_ref, mixed_ref, low_ref, hold_ref, sems = refs[11:]
     groups = 7 * w_ref.shape[1]
+    core = where_ref[0]
     copies = []
+    for i, (ref, side) in enumerate(((own_ref, core), (other_ref, 1 - core))):
+        at = pl.ds(pl.multiple_of(256 * side, 256), 256)
+        copies.append(pltpu.make_async_copy(ref.at[pl.ds(0, 256)], mixed_ref.at[at], sems.at[i]))
+        copies.append(pltpu.make_async_copy(ref.at[pl.ds(256, 16)], low_ref.at[side], sems.at[2 + i]))
+    loads = []
     for d, piece in enumerate(pieces):
-        place = w_ref.at[where_ref[1 + min(d, 3)]]
+        place = w_ref.at[min(d, 3)]
         if d >= 3:
             place = place.at[pl.ds(pieces[3].shape[0] * (d - 3), piece.shape[0])]
-        copies.append(pltpu.make_async_copy(piece, place, sems.at[d]))
-    copies.append(pltpu.make_async_copy(own_ref, mixed_ref.at[0], sems.at[32]))
-    copies.append(pltpu.make_async_copy(other_ref, mixed_ref.at[1], sems.at[33]))
-    for copy in copies:
+        loads.append(pltpu.make_async_copy(piece, place, sems.at[4 + d]))
+    for copy in copies + loads:
         copy.start()
     for copy in copies:
         copy.wait()
-    sides = [pl.ds(pl.multiple_of(256 * a, 128), 256) for a in (where_ref[0], 1 - where_ref[0])]
-    outs = []
-    for j in range(4):
-        w = w_ref[j].astype(F32).reshape(8 * groups, 896).astype(BF16)
-        for i, at in enumerate(sides):
-            got = lax.dot_general(w, mixed_ref[i, 0:256, :], NT, preferred_element_type=F32)
-            hold_ref[j, 0:groups, :, at] = got.reshape(groups, 8, 256).astype(BF16)
-            low = mixed_ref[i, 256:272, 0:256].astype(F32).reshape(2, 8, 256)
-            hold_ref[j, groups : groups + 2, :, at] = low.astype(BF16)
-        outs.append(pltpu.make_async_copy(hold_ref.at[j], out_refs[j], sems.at[34 + j]))
-        outs[-1].start()
+    low = [low_ref[i, :, 0:256].astype(F32).reshape(2, 8, 256) for i in range(2)]
+    low = jnp.concatenate(low, axis=2).astype(BF16)
+    for d in range(4):
+        for copy in loads[d : d + 1] if d < 3 else loads[3:]:
+            copy.wait()
+        w = w_ref[d].astype(F32).reshape(8 * groups, 896).astype(BF16)
+        got = lax.dot_general(w, mixed_ref[...], NT, preferred_element_type=F32)
+        at = where_ref[1 + d]
+        hold_ref[at, 0:groups] = got.reshape(groups, 8, 512).astype(BF16)
+        hold_ref[at, groups : groups + 2] = low
+    outs = [pltpu.make_async_copy(hold_ref.at[j], out_refs[j], sems.at[9 + j]) for j in range(4)]
+    for copy in outs:
+        copy.start()
     for copy in outs:
         copy.wait()
 
 
-def error_kernel(*refs):
+def error_kernel(core_ref, *refs):
     recv_refs, (right_ref, target_ref, so_far_ref, err_ref) = refs[:4], refs[4:]
     groups = recv_refs[0].shape[0] - 2
     feats = groups * 8
@@ -154,7 +156,7 @@
     low = pltpu.roll(low, 4, 0) + low
     low = jnp.broadcast_to(low[None], (32, 8, 512)).reshape(256, 512)
     r, c = iota((256, 512), 0), iota((256, 512), 1)
-    mine = ((r >> 3) == ((c & 255) >> 3)) & (((r & 7) >> 2) == (c >> 8))
+    mine = ((r >> 3) == ((c & 255) >> 3)) & (((r & 7) >> 2) == ((c >> 8) ^ core_ref[0]))
     low = jnp.where(mine, low, 0.0)
     right = right_ref[...]
     for _ in range(3):
@@ -163,7 +165,7 @@
         low = low - piece.astype(F32)
     err = jnp.sum((total * total).reshape(groups, 8, 512), axis=0)
     err = jnp.sum(err, axis=0, keepdims=True) + so_far_ref[0]
-    err_ref[...] = jnp.broadcast_to(err[None], (8, 1, 512))
+    err_ref[...] = jnp.broadcast_to(err[None], (4, 1, 512))
 
 
 def final_kernel(where_ref, err_ref, left_ref, own_ref, other_ref, query_ref, out_ref, fit_ref):
@@ -172,19 +174,19 @@
     at = iota((256, 512), 1)
     row = iota((256, 512), 0)
     member = ((at & 255) >> 3) * 2 + (at >> 8)
-    err = jnp.where(member == (row >> 2), jnp.broadcast_to(err, (256, 512)), 0.0)
+    mine = 2 * (row >> 3) + (((row & 7) >> 2) ^ core)
+    err = jnp.where(member == mine, jnp.broadcast_to(err, (256, 512)), 0.0)
     fit = -(jnp.sum(err, axis=1, keepdims=True) / (256 * D))
     mean = jnp.sum(fit, axis=0, keepdims=True) / 256
     away = fit - mean
     spread = jnp.sum(away * away, axis=0, keepdims=True) / 256
     weight = away / jnp.sqrt(spread + spread_floor)
-    me = iota((256, 128), 0) == 4 * (2 * chip + core)
+    me = iota((256, 128), 0) == 8 * chip
     fit_ref[...] = jnp.sum(jnp.where(me, jnp.broadcast_to(fit, (256, 128)), 0.0), axis=0, keepdims=True)
     left = left_ref[...].astype(F32).reshape(256, 128) * weight
     left = left.reshape(32, 8, 128)
     turned = pltpu.roll(left, 4, 1)
-    low = jnp.where(core == 0, left, turned)
-    high = jnp.where(core == 0, turned, left)
+    low, high = left, turned
     upper, narrow = iota((32, 8, 128), 1) < 4, iota((32, 8, 128), 2) < 64
     total = 0.0
     for ref, a, b in ((own_ref, low, high), (other_ref, high, low)):
@@ -291,10 +293,8 @@
     recv = lax.all_to_all(sent, CHIPS, 0, 0, tiled=True)
 
     w_t, parts = after(w_out.T, sent), []
-    z1, z7, z2, z6 = [shift(w_t, "pop_1", 8, e) for e in (1, 7, 2, 6)]
-    z3, z5 = shift(z1, "pop_1", 8, 2), shift(z7, "pop_1", 8, 6)
-    z4 = [shift(z2[:24], "pop_1", 8, 2), shift(z6[24:], "pop_1", 8, 6)]
-    for i, ins in enumerate(([w_t, z1, z7, z2, z6], [z3, z5, *z4])):
+    z1, z7, z2, z6, z3, z5, z4 = [shift(w_t, "pop_1", 8, e) for e in (1, 7, 2, 6, 3, 5, 4)]
+    for i, ins in enumerate(([w_t, z1, z7, z2, z6], [z3, z5, z4])):
         n, via = len(GROUPS[i]), VIA_UP[i]
         own = call(stack_kernel, shape((n, 56, feats)), ins)
         up, down = shift(own, "pop_0", 4, 1), shift(own, "pop_0", 4, 3)
@@ -325,9 +325,10 @@
             smem=1,
             scratch=[
                 pltpu.VMEM((4, len(group), 56, feats), BF16),
-                pltpu.VMEM((2, 272, feats), BF16),
+                pltpu.VMEM((512, feats), BF16),
+                pltpu.VMEM((2, 16, feats), BF16),
                 pltpu.VMEM((4, 7 * len(group) + 2, 8, 512), BF16),
-                pltpu.SemaphoreType.DMA((38,)),
+                pltpu.SemaphoreType.DMA((13,)),
             ],
             load=False,
         )
@@ -343,31 +344,38 @@
     o_cut = lax.dynamic_slice(o_r, (0, feats * y), (RANK, feats)).reshape(RANK, 8, 2, 56) * half
     one = (which[:, :, None] == jnp.arange(8)).astype(BF16)
     o_cut = jnp.einsum("kiz,rzcf->kcrif", one, o_cut, preferred_element_type=F32).astype(BF16)
-    o_cut = jnp.broadcast_to(o_cut.reshape(1, 16, RANK, 448), (4, 16, RANK, 448)).reshape(64, RANK, 448)
-    cut_q = jnp.moveaxis((after(left_t, sent) * twice).reshape(RANK, 64, 56), 1, 0)
-    cut_o = jnp.moveaxis((o_r * twice).reshape(RANK, 64, 56), 1, 0)
-    gap = jnp.zeros((64, RANK, 8), BF16)
-    late = jnp.concatenate([cut_q, gap, cut_o, gap, o_cut, jnp.zeros((64, RANK, 64), BF16)], axis=2)
-    late = lax.all_to_all(late, POP, 0, 0, tiled=True)
+    o_cut = jnp.where(c == 0, o_cut, o_cut[:, ::-1]).reshape(1, 8, 8, 448)
+    o_cut = jnp.broadcast_to(o_cut, (4, 8, 8, 448)).reshape(32, 8, 448)
+
+    def cut(a):
+        a = jnp.moveaxis((a * twice).reshape(RANK, 32, 2, 56), 0, 2)
+        return jnp.where(c == 0, a, a[:, ::-1]).reshape(32, 8, 56)
+
+    gap = jnp.zeros((32, 8, 8), BF16)
+    late = [cut(after(left_t, sent)), gap, cut(o_r), gap, o_cut, jnp.zeros((32, 8, 64), BF16)]
+    late = jnp.concatenate(late, axis=2)
+    late = lax.all_to_all(late, CHIPS, 0, 0, tiled=True)
+    late_b = swap(late[:, 4:])
+    late = jnp.concatenate([late[:, :4], late_b], axis=1)
     factors = after(recv, outs[0][0])[:, :, 1024:1920]
     factors_b = swap(factors)
-    lefts = late[:, :, :128].reshape(32, 8, 128)
+    lefts = late[:, :, :128]
     goal = lax.dynamic_slice(target, (8 * k, 0), (8, feats)).reshape(8, 8, 2, 56)
     goal = jnp.where(c == 0, goal[:, :, 0], goal[:, :, 1])
     here = (((z - order) % 8)[:, None] == jnp.arange(8)).astype(BF16)
     goal = jnp.einsum("iz,tzf->tif", here, goal, preferred_element_type=F32).astype(BF16).reshape(8, 448)
-    err = jnp.zeros((8, 1, 512), F32)
+    err = jnp.zeros((4, 1, 512), F32)
     start = 128
     for group, met in zip(GROUPS, mets):
         n = 56 * len(group)
         right = late[:, :, start : start + n].reshape(256, n)
         part = goal[:, start - 128 : start - 128 + n]
         start += n
-        err = call(error_kernel, shape((8, 1, 512), F32), (*met, right, part, err))
-
-    err = lax.all_to_all(err, ("pop_2", "mp"), 0, 0, tiled=True)
+        err = call(error_kernel, shape((4, 1, 512), F32), (ints(c), *met, right, part, err), smem=1)
+
+    err = lax.all_to_all(err, "mp", 0, 0, tiled=True)
     err = jnp.sum(err, axis=0, keepdims=True)
-    err = lax.all_to_all(jnp.broadcast_to(err, (32, 1, 512)), CHIPS, 0, 0, tiled=True)
+    err = lax.all_to_all(jnp.broadcast_to(err, (64, 1, 512)), POP, 0, 0, tiled=True)
     grad_query, grad_out, fitness = call(
         final_kernel,
         [shape((56, feats), F32), shape((56, feats), F32), shape((1, 128), F32)],

time: 169 us -> 167 us (0.988)
  starting transfers between devices: 61.6 us -> 81 us
  waiting for transfers between devices: 40 us -> 21.8 us
  local copies, waits for them, and re-layouts: 15.8 us -> 12.2 us
  other arithmetic: 4.62 us -> 6.97 us
  blocking collectives: 9.43 us -> 7.39 us
    ppermute x22 -> x21, waiting for transfers between devices: 32.4 us -> 11 us  [shift(): return lax.ppermute(x, axis, [(i, (i + step) % size) for i in range(size)])]
    all_to_all x2, starting transfers between devices: 13.1 us -> 21.8 us  [the longest x1 13.2 us: per_device(): lax.all_to_all(jnp.broadcast_to(err, (64, 1, 512)), POP, 0, 0, tiled=True)]
    ppermute x22 -> x21, starting transfers between devices: 32.5 us -> 40.2 us  [shift(): return lax.ppermute(x, axis, [(i, (i + step) % size) for i in range(size)])]
    ppermute x3 -> x4, starting transfers between devices: 3.9 us -> 10.8 us  [swap(): return lax.ppermute(x, 'pop_2', [(0, 1), (1, 0)])]
    all_to_all x1, starting transfers between devices: 12.1 us -> 8.16 us  [per_device(): recv = lax.all_to_all(sent, CHIPS, 0, 0, tiled=True)]
    slice x5 -> x1, local copies, waits for them, and re-layouts: 2.47 us -> 0.11 us  [per_device(): late_b = swap(late[:, 4:])]
    all_to_all x1, blocking collectives: 9.43 us -> 7.39 us  [per_device(): err = lax.all_to_all(err, 'mp', 0, 0, tiled=True)]
    all_to_all x1, waiting for transfers between devices: 0.01 us -> 1.7 us  [per_device(): recv = lax.all_to_all(sent, CHIPS, 0, 0, tiled=True)]
  transfers between devices with their start and end apart: 28 -> 28, of which waited for: 9 -> 5; matrix products, arithmetic and copies ran while one was open for 12% -> 11% of each run, Pallas kernels for 14% -> 14%
where the time goes in v3:
time: 167 us; the launch traced here: 166 us
  starting transfers between devices  81 us (49%)
  Pallas kernels  31.7 us (19%)
  waiting for transfers between devices  21.8 us (13%)
  local copies, waits for them, and re-layouts  12.2 us (7%)
  blocking collectives  7.39 us (4%)
  other arithmetic  6.97 us (4%)
  matrix products  2.3 us (1%)
  between operations  2.19 us (1%)
    ppermute x21, starting transfers between devices, shift(): return lax.ppermute(x, axis, [(i, (i + step) % size) for i in range(size)])  40.2 us
    pallas_call x9, Pallas kernels, call(): pl.pallas_call(kernel, out_shape=out, in_specs=[pl.BlockSpec(memory_space...  31.7 us
    all_to_all x1, starting transfers between devices, per_device(): lax.all_to_all(jnp.broadcast_to(err, (64, 1, 512)), POP, 0, 0, tiled=True)  13.2 us
    ppermute x21, waiting for transfers between devices, shift(): return lax.ppermute(x, axis, [(i, (i + step) % size) for i in range(size)])  11 us
    ppermute x4, starting transfers between devices, swap(): return lax.ppermute(x, 'pop_2', [(0, 1), (1, 0)])  10.8 us
    all_to_all x1, waiting for transfers between devices, per_device(): lax.all_to_all(jnp.broadcast_to(err, (64, 1, 512)), POP, 0, 0, tiled=True)  9.02 us
    all_to_all x1, starting transfers between devices, per_device(): late = lax.all_to_all(late, CHIPS, 0, 0, tiled=True)  8.69 us
    all_to_all x1, starting transfers between devices, per_device(): recv = lax.all_to_all(sent, CHIPS, 0, 0, tiled=True)  8.16 us
  transfers between devices with their start and end apart: 28, of which 5 were waited for; matrix products, arithmetic and copies ran while one was open for 11% of the time, Pallas kernels for 14%

profile of v3, /device:TPU:1, one launch (start us, length us, event | category | flops | bytes accessed | tf_op | source)
XLA Modules:
  0.0 165.6 jit_solution(12321762804553519576)
XLA Ops:
  2.0 4.2 %shard_map.139 = bf16[32,8,1920]{2,1,0:T(8,128)(2,1)} custom-call(s32[2]{0:T(128)} %pad_add_fusion.1.refs_0_, bf16[256,3584]{1,0:T(8,128)(2,1)} %refs_1_.1, bf16[56,896]{1,0:T(8,128)(2,1)} %refs_2_.1, bf16[4,3584]{1,0:T(4,128)(2,1)} %bitcast.68, bf16[4,896]{1,0:T(4,128)(2,1)} %bitcast.78, bf16[4,896]{1,0:T(4,128)(2,1)} %bitcast.79), custom_call_target="tpu_custom_call" | custom-call | flops 1000000000 | bytes 2000000 | tf_op jit(solution)/shard_map/pallas_call | solution.py:235
  6.2 2.5 %collective-permute-start.13 = (bf16[56,896]{1,0:T(8,128)(2,1)S(1)}, bf16[56,896]{1,0:T(8,128)(2,1)}, u32[]{:S(2)}, u32[]{:S(2)}) collective-permute-start(bf16[56,896]{1,0:T(8,128)(2,1)S(1)} %bitcast.71), channel_id=1, source_target_pairs={{0,8},{8,16},{16,24},{24,32},{32,40},{40,48},{48,56},{56,0},{1,9},... | collective-permute-start | bytes 301064 | tf_op jit(solution)/shard_map/ppermute | solution.py:32
  8.8 4.0 %collective-permute-start.14 = (bf16[56,896]{1,0:T(8,128)(2,1)S(1)}, bf16[56,896]{1,0:T(8,128)(2,1)}, u32[]{:S(2)}, u32[]{:S(2)}) collective-permute-start(bf16[56,896]{1,0:T(8,128)(2,1)S(1)} %bitcast.72), channel_id=1, source_target_pairs={{0,56},{8,0},{16,8},{24,16},{32,24},{40,32},{48,40},{56,48},{1,57}... | collective-permute-start | bytes 301064 | tf_op jit(solution)/shard_map/ppermute | solution.py:32
  12.8 3.6 %collective-permute-start.16 = (bf16[56,896]{1,0:T(8,128)(2,1)S(1)}, bf16[56,896]{1,0:T(8,128)(2,1)}, u32[]{:S(2)}, u32[]{:S(2)}) collective-permute-start(bf16[56,896]{1,0:T(8,128)(2,1)S(1)} %bitcast.74), channel_id=1, source_target_pairs={{0,48},{8,56},{16,0},{24,8},{32,16},{40,24},{48,32},{56,40},{1,49}... | collective-permute-start | bytes 301064 | tf_op jit(solution)/shard_map/ppermute | solution.py:32
  16.4 8.2 %all-to-all-start = ((bf16[32,8,1920]{2,1,0:T(8,128)(2,1)}), bf16[32,8,1920]{2,1,0:T(8,128)(2,1)}, u32[]{:S(2)}, u32[]{:S(2)}) async-start(bf16[32,8,1920]{2,1,0:T(8,128)(2,1)} %shard_map.139), calls=%async_computation | async-start | bytes 1966080 | tf_op jit(solution)/shard_map/all_to_all | solution.py:293
  24.6 3.0 %collective-permute-start = (bf16[56,896]{1,0:T(8,128)(2,1)S(1)}, bf16[56,896]{1,0:T(8,128)(2,1)S(1)}, u32[]{:S(2)}, u32[]{:S(2)}) collective-permute-start(bf16[56,896]{1,0:T(8,128)(2,1)S(1)} %bitcast.75), channel_id=1, source_target_pairs={{0,24},{8,32},{16,40},{24,48},{32,56},{40,0},{48,8},{56,16},{1,25}... | collective-permute-start | bytes 301064 | tf_op jit(solution)/shard_map/ppermute | solution.py:32
  28.8 0.7 constant_dynamic-slice_fusion
  29.6 0.9 concatenate.27
  32.0 0.8 fusion.7.refs_4_
  32.8 1.2 convolution_convert_fusion.1.refs_5_
  34.7 1.5 collective-permute-start.1
  36.2 5.1 %collective-permute-start.2 = (bf16[56,896]{1,0:T(8,128)(2,1)S(1)}, bf16[56,896]{1,0:T(8,128)(2,1)S(1)}, u32[]{:S(2)}, u32[]{:S(2)}) collective-permute-start(bf16[56,896]{1,0:T(8,128)(2,1)S(1)} %bitcast.77), channel_id=1, source_target_pairs={{0,32},{8,40},{16,48},{24,56},{32,0},{40,8},{48,16},{56,24},{1,33}... | collective-permute-start | bytes 301064 | tf_op jit(solution)/shard_map/ppermute | solution.py:32
  41.3 2.0 %shard_map.143.refs_0_ = bf16[5,56,896]{2,1,0:T(8,128)(2,1)} custom-call(bf16[56,896]{1,0:T(8,128)(2,1)} %bitcast.70, bf16[56,896]{1,0:T(8,128)(2,1)} %collective-permute-done.13.refs_1_, bf16[56,896]{1,0:T(8,128)(2,1)} %collective-permute-done.14.refs_2_, bf16[56,896]{1,0:T(8,128)(2,1)} %collective-permute-done.15.refs_3_, ...), custom_call_target="tpu_custom_call" | custom-call | flops 1000000000 | bytes 2000000 | tf_op jit(solution)/shard_map/pallas_call | solution.py:235
  43.3 1.3 collective-permute-start.17
  44.5 1.5 collective-permute-start.18
  46.0 1.7 %all-to-all-done.refs_1_ = bf16[32,8,1920]{2,1,0:T(8,128)(2,1)} async-done(((bf16[32,8,1920]{2,1,0:T(8,128)(2,1)}), bf16[32,8,1920]{2,1,0:T(8,128)(2,1)}, u32[]{:S(2)}, u32[]{:S(2)}) %all-to-all-start) | async-done | bytes 983072 | tf_op jit(solution)/shard_map/all_to_all | solution.py:293
  47.7 8.7 %all-to-all-start.1 = ((bf16[32,8,640]{2,1,0:T(8,128)(2,1)}), bf16[32,8,640]{2,1,0:T(8,128)(2,1)S(1)}, u32[]{:S(2)}, u32[]{:S(2)}) async-start(bf16[32,8,640]{2,1,0:T(8,128)(2,1)} %concatenate.27), calls=%async_computation.1 | async-start | bytes 655360 | tf_op jit(solution)/shard_map/all_to_all | solution.py:357
  56.4 1.1 convert_reduce_fusion.refs_2_
  57.5 7.6 %collective-permute-start.7 = (f32[8,896]{1,0:T(8,128)S(1)}, f32[8,896]{1,0:T(8,128)S(1)}, u32[]{:S(2)}, u32[]{:S(2)}) collective-permute-start(f32[8,896]{1,0:T(8,128)S(1)} %convert_reduce_fusion.refs_2_), channel_id=1, source_target_pairs={{0,4},{4,0},{1,5},{5,1},{2,6},{6,2},{3,7},{7,3},{8,12},{12,8},{9,1... | collective-permute-start | bytes 86024 | tf_op jit(solution)/shard_map/ppermute | solution.py:36
  66.5 1.8 %shard_map.140.refs_0_ = bf16[3,56,896]{2,1,0:T(8,128)(2,1)} custom-call(bf16[56,896]{1,0:T(8,128)(2,1)} %copy-done.18, bf16[56,896]{1,0:T(8,128)(2,1)} %copy-done.19, bf16[56,896]{1,0:T(8,128)(2,1)} %copy-done.20), custom_call_target="tpu_custom_call" | custom-call | flops 1000000000 | bytes 2000000 | tf_op jit(solution)/shard_map/pallas_call | solution.py:235
  68.2 2.8 %collective-permute-start.4 = (bf16[3,56,896]{2,1,0:T(8,128)(2,1)}, bf16[3,56,896]{2,1,0:T(8,128)(2,1)S(1)}, u32[]{:S(2)}, u32[]{:S(2)}) collective-permute-start(bf16[3,56,896]{2,1,0:T(8,128)(2,1)} %shard_map.140.refs_0_), channel_id=1, source_target_pairs={{0,192},{64,0},{128,64},{192,128},{1,193},{65,1},{129,65},{193,129... | collective-permute-start | bytes 903176 | tf_op jit(solution)/shard_map/ppermute | solution.py:32
  71.7 5.2 %shard_map.141.refs_5_ = bf16[272,896]{1,0:T(8,128)(2,1)} custom-call(s32[1]{0:T(128)} %bitcast.15.refs_0_, bf16[32,8,1920]{2,1,0:T(8,128)(2,1)} %all-to-all-done.refs_1_, f32[8,896]{1,0:T(8,128)} %copy-done.9, f32[8,896]{1,0:T(8,128)} %copy-done.22, bf16[256,128]{1,0:T(8,128)(2,1)} %fusion.7.refs_4_, bf16[256,128]{1,0:T(8,128)(2,1)} %convolution_convert_fusion.1.refs_5_, ...), custom_call_target="tpu_custom_call" | custom-call | flops 1000000000 | bytes 2000000 | tf_op jit(solution)/shard_map/pallas_call | solution.py:235
  78.4 3.1 %collective-permute-start.6 = (bf16[2,56,896]{2,1,0:T(8,128)(2,1)S(1)}, bf16[2,56,896]{2,1,0:T(8,128)(2,1)}, u32[]{:S(2)}, u32[]{:S(2)}) collective-permute-start(bf16[2,56,896]{2,1,0:T(8,128)(2,1)S(1)} %slice.75), channel_id=1, source_target_pairs={{0,192},{64,0},{128,64},{192,128},{1,193},{65,1},{129,65},{193,129... | collective-permute-start | bytes 602120 | tf_op jit(solution)/shard_map/ppermute | solution.py:32
  81.5 0.9 slice.87
  82.5 1.0 collective-permute-start.20
  83.6 5.8 %collective-permute-done.20.refs_4_ = bf16[2,56,896]{2,1,0:T(8,128)(2,1)} collective-permute-done((bf16[2,56,896]{2,1,0:T(8,128)(2,1)S(1)}, bf16[2,56,896]{2,1,0:T(8,128)(2,1)}, u32[]{:S(2)}, u32[]{:S(2)}) %collective-permute-start.20) | collective-permute-done | bytes 200736 | tf_op jit(solution)/shard_map/ppermute | solution.py:32
  89.4 1.6 collective-permute-start.12
  91.7 5.2 %shard_map.144 = (bf16[37,8,512]{2,1,0:T(8,128)(2,1)}, bf16[37,8,512]{2,1,0:T(8,128)(2,1)}, bf16[37,8,512]{2,1,0:T(8,128)(2,1)}, bf16[37,8,512]{2,1,0:T(8,128)(2,1)}) custom-call(s32[5]{0:T(128)} %stack.46.where_ref, bf16[5,56,896]{2,1,0:T(8,128)(2,1)} %shard_map.143.refs_0_, bf16[5,56,896]{2,1,0:T(8,128)(2,1)} %copy-done.4, ...), custom_call_target="tpu_custom_call" | custom-call | flops 1000000000 | bytes 2000000 | tf_op jit(solution)/shard_map/pallas_call | solution.py:235
  96.9 3.0 %collective-permute-start.21 = (bf16[37,8,512]{2,1,0:T(8,128)(2,1)}, bf16[37,8,512]{2,1,0:T(8,128)(2,1)S(1)}, u32[]{:S(2)}, u32[]{:S(2)}) collective-permute-start(bf16[37,8,512]{2,1,0:T(8,128)(2,1)} %get-tuple-element.26), channel_id=1, source_target_pairs={{0,2},{1,3},{2,0},{3,1},{4,6},{5,7},{6,4},{7,5},{8,10},{9,11},{10,... | collective-permute-start | bytes 909320 | tf_op jit(solution)/shard_map/ppermute | solution.py:32
  101.9 0.9 slice.74
  102.8 1.3 collective-permute-start.5
  104.0 2.3 %collective-permute-start.23 = (bf16[37,8,512]{2,1,0:T(8,128)(2,1)}, bf16[37,8,512]{2,1,0:T(8,128)(2,1)}, u32[]{:S(2)}, u32[]{:S(2)}) collective-permute-start(bf16[37,8,512]{2,1,0:T(8,128)(2,1)} %get-tuple-element.28), channel_id=1, source_target_pairs={{0,3},{1,0},{2,1},{3,2},{4,7},{5,4},{6,5},{7,6},{8,11},{9,8},{10,9... | collective-permute-start | bytes 909320 | tf_op jit(solution)/shard_map/ppermute | solution.py:32
  106.3 0.8 fusion.3.refs_5_
  107.1 1.1 slice.72.refs_3_
  108.2 0.9 collective-permute-done.5.refs_3_
  109.0 1.1 collective-permute-start.24
  110.2 4.8 %shard_map.142 = (bf16[23,8,512]{2,1,0:T(8,128)(2,1)}, bf16[23,8,512]{2,1,0:T(8,128)(2,1)}, bf16[23,8,512]{2,1,0:T(8,128)(2,1)}, bf16[23,8,512]{2,1,0:T(8,128)(2,1)}) custom-call(s32[5]{0:T(128)} %stack.46.where_ref, bf16[3,56,896]{2,1,0:T(8,128)(2,1)} %shard_map.140.refs_0_, bf16[3,56,896]{2,1,0:T(8,128)(2,1)} %collective-permute-done.3.refs_1_, ...), custom_call_target="tpu_custom_call" | custom-call | flops 1000000000 | bytes 2000000 | tf_op jit(solution)/shard_map/pallas_call | solution.py:235
  115.1 2.6 %collective-permute-start.11 = (bf16[23,8,512]{2,1,0:T(8,128)(2,1)}, bf16[23,8,512]{2,1,0:T(8,128)(2,1)S(1)}, u32[]{:S(2)}, u32[]{:S(2)}) collective-permute-start(bf16[23,8,512]{2,1,0:T(8,128)(2,1)} %get-tuple-element.22), channel_id=1, source_target_pairs={{0,3},{1,0},{2,1},{3,2},{4,7},{5,4},{6,5},{7,6},{8,11},{9,8},{10,9... | collective-permute-start | bytes 565256 | tf_op jit(solution)/shard_map/ppermute | solution.py:32
  117.7 0.9 collective-permute-start.9
  118.6 0.8 fusion.5.refs_5_
  120.1 2.6 %shard_map.145.refs_7_ = f32[4,1,512]{2,1,0:T(1,128)} custom-call(s32[1]{0:T(128)} %bitcast.refs_0_, bf16[37,8,512]{2,1,0:T(8,128)(2,1)} %get-tuple-element.25.refs_1_, bf16[37,8,512]{2,1,0:T(8,128)(2,1)} %copy-done.12, bf16[37,8,512]{2,1,0:T(8,128)(2,1)} %copy-done.13, bf16[37,8,512]{2,1,0:T(8,128)(2,1)} %collective-permute-done.23.refs_4_, ...), custom_call_target="tpu_custom_call" | custom-call | flops 1000000000 | bytes 2000000 | tf_op jit(solution)/shard_map/pallas_call | solution.py:235
  122.7 4.3 %collective-permute-done.9.refs_2_ = bf16[23,8,512]{2,1,0:T(8,128)(2,1)} collective-permute-done((bf16[23,8,512]{2,1,0:T(8,128)(2,1)}, bf16[23,8,512]{2,1,0:T(8,128)(2,1)}, u32[]{:S(2)}, u32[]{:S(2)}) %collective-permute-start.9) | collective-permute-done | bytes 188448 | tf_op jit(solution)/shard_map/ppermute | solution.py:32
  127.1 2.4 %shard_map.146 = f32[4,1,512]{2,1,0:T(1,128)} custom-call(s32[1]{0:T(128)} %bitcast.refs_0_, bf16[23,8,512]{2,1,0:T(8,128)(2,1)} %get-tuple-element.19.refs_1_, bf16[23,8,512]{2,1,0:T(8,128)(2,1)} %collective-permute-done.9.refs_2_, bf16[23,8,512]{2,1,0:T(8,128)(2,1)} %copy-done.15, bf16[23,8,512]{2,1,0:T(8,128)(2,1)} %copy-done.16, ...), custom_call_target="tpu_custom_call" | custom-call | flops 1000000000 | bytes 2000000 | tf_op jit(solution)/shard_map/pallas_call | solution.py:235
  129.5 7.4 %all_to_all.20 = f32[4,1,512]{2,1,0:T(1,128)S(1)} all-to-all(f32[4,1,512]{2,1,0:T(1,128)} %shard_map.146), channel_id=1, replica_groups=mesh['pop_0'=4,'pop_1'=8,'pop_2'=2,'mp'=4] {'mp'}, dimensions={0} | all-to-all | bytes 16384 | tf_op jit(solution)/shard_map/all_to_all | solution.py:376
  136.9 0.7 broadcast_in_dim.17
  137.6 13.2 %all-to-all-start.3 = ((f32[64,1,512]{2,1,0:T(1,128)}), f32[64,1,512]{2,1,0:T(1,128)S(1)}, u32[]{:S(2)}, u32[]{:S(2)}) async-start(f32[64,1,512]{2,1,0:T(1,128)} %broadcast_in_dim.17), calls=%async_computation.3 | async-start | bytes 262144 | tf_op jit(solution)/shard_map/all_to_all | solution.py:378
  152.1 9.0 %all-to-all-done.3.refs_1_ = f32[64,1,512]{2,1,0:T(1,128)S(1)} async-done(((f32[64,1,512]{2,1,0:T(1,128)}), f32[64,1,512]{2,1,0:T(1,128)S(1)}, u32[]{:S(2)}, u32[]{:S(2)}) %all-to-all-start.3) | async-done | bytes 131104 | tf_op jit(solution)/shard_map/all_to_all | solution.py:378
  161.8 3.6 %shard_map.147 = (f32[56,896]{1,0:T(8,128)}, f32[56,896]{1,0:T(8,128)}, f32[1,128]{1,0:T(1,128)}) custom-call(s32[2]{0:T(128)} %pad_add_fusion.refs_0_, f32[64,1,512]{2,1,0:T(1,128)} %copy-done.6, bf16[32,8,128]{2,1,0:T(8,128)(2,1)} %pad_maximum_fusion.refs_2_, bf16[32,8,896]{2,1,0:T(8,128)(2,1)} %copy-done.3, bf16[32,8,896]{2,1,0:T(8,128)(2,1)} %copy-done.11), custom_call_target="tpu_custom_call" | custom-call | flops 1000000000 | bytes 2000000 | tf_op jit(solution)/shard_map/pallas_call | solution.py:235
  (115 shorter events, 12.7 us)
Async XLA Ops:
  0.6 30.0 %copy-start = (bf16[3584,128]{1,0:T(8,128)(2,1)S(1)}, bf16[3584,128]{1,0:T(8,128)(2,1)}, u32[]{:S(2)}) copy-start(bf16[3584,128]{1,0:T(8,128)(2,1)} %param.15) | copy-start | bytes 2752516
  2.0 4.2 %copy-start.17 = (bf16[896,56]{0,1:T(8,128)(2,1)S(1)}, bf16[896,56]{0,1:T(8,128)(2,1)}, u32[]{:S(2)}) copy-start(bf16[896,56]{0,1:T(8,128)(2,1)} %param.17) | copy-start | bytes 301060
  6.2 21.4 %copy-start.7 = (bf16[1,4,3584]{2,1,0:T(4,128)(2,1)S(1)}, bf16[1,4,3584]{2,1,0:T(4,128)(2,1)}, u32[]{:S(2)}) copy-start(bf16[1,4,3584]{2,1,0:T(4,128)(2,1)} %param.21) | copy-start | bytes 86020
  6.2 21.4 %copy-start.8 = (bf16[1,3584,4]{1,2,0:T(4,128)(2,1)S(1)}, bf16[1,3584,4]{1,2,0:T(4,128)(2,1)}, u32[]{:S(2)}) copy-start(bf16[1,3584,4]{1,2,0:T(4,128)(2,1)} %param.18) | copy-start | bytes 86020
  6.2 22.1 %copy-start.10 = (s32[8]{0:T(128)S(1)}, s32[8]{0:T(128)}, u32[]{:S(2)}) copy-start(s32[8]{0:T(128)} %constant.113) | copy-start | bytes 100
  6.2 28.4 %collective-permute-start.13 = (bf16[56,896]{1,0:T(8,128)(2,1)S(1)}, bf16[56,896]{1,0:T(8,128)(2,1)}, u32[]{:S(2)}, u32[]{:S(2)}) collective-permute-start(bf16[56,896]{1,0:T(8,128)(2,1)S(1)} %bitcast.71), channel_id=1, source_target_pairs={{0,8},{8,16},{16,24},{24,32},{32,40},{40,48},{48,56},{56,0},{1,9},... | collective-permute-start | bytes 301064 | tf_op jit(solution)/shard_map/ppermute | solution.py:32
  8.8 27.4 %collective-permute-start.14 = (bf16[56,896]{1,0:T(8,128)(2,1)S(1)}, bf16[56,896]{1,0:T(8,128)(2,1)}, u32[]{:S(2)}, u32[]{:S(2)}) collective-permute-start(bf16[56,896]{1,0:T(8,128)(2,1)S(1)} %bitcast.72), channel_id=1, source_target_pairs={{0,56},{8,0},{16,8},{24,16},{32,24},{40,32},{48,40},{56,48},{1,57}... | collective-permute-start | bytes 301064 | tf_op jit(solution)/shard_map/ppermute | solution.py:32
  12.8 28.5 %collective-permute-start.15 = (bf16[56,896]{1,0:T(8,128)(2,1)S(1)}, bf16[56,896]{1,0:T(8,128)(2,1)}, u32[]{:S(2)}, u32[]{:S(2)}) collective-permute-start(bf16[56,896]{1,0:T(8,128)(2,1)S(1)} %bitcast.73), channel_id=1, source_target_pairs={{0,16},{8,24},{16,32},{24,40},{32,48},{40,56},{48,0},{56,8},{1,17}... | collective-permute-start | bytes 301064 | tf_op jit(solution)/shard_map/ppermute | solution.py:32
  12.8 28.5 %collective-permute-start.16 = (bf16[56,896]{1,0:T(8,128)(2,1)S(1)}, bf16[56,896]{1,0:T(8,128)(2,1)}, u32[]{:S(2)}, u32[]{:S(2)}) collective-permute-start(bf16[56,896]{1,0:T(8,128)(2,1)S(1)} %bitcast.74), channel_id=1, source_target_pairs={{0,48},{8,56},{16,0},{24,8},{32,16},{40,24},{48,32},{56,40},{1,49}... | collective-permute-start | bytes 301064 | tf_op jit(solution)/shard_map/ppermute | solution.py:32
  16.4 31.3 %all-to-all-start = ((bf16[32,8,1920]{2,1,0:T(8,128)(2,1)}), bf16[32,8,1920]{2,1,0:T(8,128)(2,1)}, u32[]{:S(2)}, u32[]{:S(2)}) async-start(bf16[32,8,1920]{2,1,0:T(8,128)(2,1)} %shard_map.139), calls=%async_computation | async-start | bytes 1966080 | tf_op jit(solution)/shard_map/all_to_all | solution.py:293
  24.5 6.1 %copy-start.1 = (bf16[256,3584]{1,0:T(8,128)(2,1)S(1)}, bf16[256,3584]{1,0:T(8,128)(2,1)}, u32[]{:S(2)}) copy-start(bf16[256,3584]{1,0:T(8,128)(2,1)} %refs_1_.1) | copy-start | bytes 5505028
  24.6 33.0 %collective-permute-start = (bf16[56,896]{1,0:T(8,128)(2,1)S(1)}, bf16[56,896]{1,0:T(8,128)(2,1)S(1)}, u32[]{:S(2)}, u32[]{:S(2)}) collective-permute-start(bf16[56,896]{1,0:T(8,128)(2,1)S(1)} %bitcast.75), channel_id=1, source_target_pairs={{0,24},{8,32},{16,40},{24,48},{32,56},{40,0},{48,8},{56,16},{1,25}... | collective-permute-start | bytes 301064 | tf_op jit(solution)/shard_map/ppermute | solution.py:32
  30.7 2.1 %copy-start.2 = (bf16[3584,128]{1,0:T(8,128)(2,1)S(1)}, bf16[3584,128]{1,0:T(8,128)(2,1)}, u32[]{:S(2)}) copy-start(bf16[3584,128]{1,0:T(8,128)(2,1)} %param.16) | copy-start | bytes 2752516
  34.7 30.5 %collective-permute-start.1 = (bf16[56,896]{1,0:T(8,128)(2,1)S(1)}, bf16[56,896]{1,0:T(8,128)(2,1)S(1)}, u32[]{:S(2)}, u32[]{:S(2)}) collective-permute-start(bf16[56,896]{1,0:T(8,128)(2,1)S(1)} %bitcast.76), channel_id=1, source_target_pairs={{0,40},{8,48},{16,56},{24,0},{32,8},{40,16},{48,24},{56,32},{1,41}... | collective-permute-start | bytes 301064 | tf_op jit(solution)/shard_map/ppermute | solution.py:32
  36.2 29.0 %collective-permute-start.2 = (bf16[56,896]{1,0:T(8,128)(2,1)S(1)}, bf16[56,896]{1,0:T(8,128)(2,1)S(1)}, u32[]{:S(2)}, u32[]{:S(2)}) collective-permute-start(bf16[56,896]{1,0:T(8,128)(2,1)S(1)} %bitcast.77), channel_id=1, source_target_pairs={{0,32},{8,40},{16,48},{24,56},{32,0},{40,8},{48,16},{56,24},{1,33}... | collective-permute-start | bytes 301064 | tf_op jit(solution)/shard_map/ppermute | solution.py:32
  43.3 34.1 %collective-permute-start.17 = (bf16[5,56,896]{2,1,0:T(8,128)(2,1)}, bf16[5,56,896]{2,1,0:T(8,128)(2,1)S(1)}, u32[]{:S(2)}, u32[]{:S(2)}) collective-permute-start(bf16[5,56,896]{2,1,0:T(8,128)(2,1)} %shard_map.143.refs_0_), channel_id=1, source_target_pairs={{0,64},{64,128},{128,192},{192,0},{1,65},{65,129},{129,193},{193,1... | collective-permute-start | bytes 1505288 | tf_op jit(solution)/shard_map/ppermute | solution.py:32
  44.5 37.0 %collective-permute-start.18 = (bf16[5,56,896]{2,1,0:T(8,128)(2,1)}, bf16[5,56,896]{2,1,0:T(8,128)(2,1)}, u32[]{:S(2)}, u32[]{:S(2)}) collective-permute-start(bf16[5,56,896]{2,1,0:T(8,128)(2,1)} %shard_map.143.refs_0_), channel_id=1, source_target_pairs={{0,192},{64,0},{128,64},{192,128},{1,193},{65,1},{129,65},{193,129... | collective-permute-start | bytes 1505288 | tf_op jit(solution)/shard_map/ppermute | solution.py:32
  47.7 35.8 %all-to-all-start.1 = ((bf16[32,8,640]{2,1,0:T(8,128)(2,1)}), bf16[32,8,640]{2,1,0:T(8,128)(2,1)S(1)}, u32[]{:S(2)}, u32[]{:S(2)}) async-start(bf16[32,8,640]{2,1,0:T(8,128)(2,1)} %concatenate.27), calls=%async_computation.1 | async-start | bytes 655360 | tf_op jit(solution)/shard_map/all_to_all | solution.py:357
  57.5 10.7 %copy-start.9 = (f32[8,896]{1,0:T(8,128)}, f32[8,896]{1,0:T(8,128)S(1)}, u32[]{:S(2)}) copy-start(f32[8,896]{1,0:T(8,128)S(1)} %convert_reduce_fusion.refs_2_) | copy-start | bytes 86020
  57.5 7.6 %copy-start.18 = (bf16[56,896]{1,0:T(8,128)(2,1)}, bf16[56,896]{1,0:T(8,128)(2,1)S(1)}, u32[]{:S(2)}) copy-start(bf16[56,896]{1,0:T(8,128)(2,1)S(1)} %collective-permute-done.refs_0_) | copy-start | bytes 301060
  57.5 13.5 %collective-permute-start.7 = (f32[8,896]{1,0:T(8,128)S(1)}, f32[8,896]{1,0:T(8,128)S(1)}, u32[]{:S(2)}, u32[]{:S(2)}) collective-permute-start(f32[8,896]{1,0:T(8,128)S(1)} %convert_reduce_fusion.refs_2_), channel_id=1, source_target_pairs={{0,4},{4,0},{1,5},{5,1},{2,6},{6,2},{3,7},{7,3},{8,12},{12,8},{9,1... | collective-permute-start | bytes 86024 | tf_op jit(solution)/shard_map/ppermute | solution.py:36
  68.2 10.2 %collective-permute-start.4 = (bf16[3,56,896]{2,1,0:T(8,128)(2,1)}, bf16[3,56,896]{2,1,0:T(8,128)(2,1)S(1)}, u32[]{:S(2)}, u32[]{:S(2)}) collective-permute-start(bf16[3,56,896]{2,1,0:T(8,128)(2,1)} %shard_map.140.refs_0_), channel_id=1, source_target_pairs={{0,192},{64,0},{128,64},{192,128},{1,193},{65,1},{129,65},{193,129... | collective-permute-start | bytes 903176 | tf_op jit(solution)/shard_map/ppermute | solution.py:32
  77.0 14.1 %collective-permute-start.8 = (bf16[272,896]{1,0:T(8,128)(2,1)}, bf16[272,896]{1,0:T(8,128)(2,1)}, u32[]{:S(2)}, u32[]{:S(2)}) collective-permute-start(bf16[272,896]{1,0:T(8,128)(2,1)} %shard_map.141.refs_5_), channel_id=1, source_target_pairs={{0,4},{4,0},{1,5},{5,1},{2,6},{6,2},{3,7},{7,3},{8,12},{12,8},{9,1... | collective-permute-start | bytes 1462280 | tf_op jit(solution)/shard_map/ppermute | solution.py:36
  77.4 13.6 %copy-start.4 = (bf16[5,56,896]{2,1,0:T(8,128)(2,1)}, bf16[5,56,896]{2,1,0:T(8,128)(2,1)S(1)}, u32[]{:S(2)}) copy-start(bf16[5,56,896]{2,1,0:T(8,128)(2,1)S(1)} %collective-permute-done.17.refs_1_) | copy-start | bytes 1505284
  77.5 13.6 %collective-permute-start.19 = (bf16[3,56,896]{2,1,0:T(8,128)(2,1)S(1)}, bf16[3,56,896]{2,1,0:T(8,128)(2,1)S(1)}, u32[]{:S(2)}, u32[]{:S(2)}) collective-permute-start(bf16[3,56,896]{2,1,0:T(8,128)(2,1)S(1)} %slice.86), channel_id=1, source_target_pairs={{0,64},{64,128},{128,192},{192,0},{1,65},{65,129},{129,193},{193,1... | collective-permute-start | bytes 903176 | tf_op jit(solution)/shard_map/ppermute | solution.py:32
  78.3 23.6 %collective-permute-start.3 = (bf16[3,56,896]{2,1,0:T(8,128)(2,1)}, bf16[3,56,896]{2,1,0:T(8,128)(2,1)}, u32[]{:S(2)}, u32[]{:S(2)}) collective-permute-start(bf16[3,56,896]{2,1,0:T(8,128)(2,1)} %shard_map.140.refs_0_), channel_id=1, source_target_pairs={{0,64},{64,128},{128,192},{192,0},{1,65},{65,129},{129,193},{193,1... | collective-permute-start | bytes 903176 | tf_op jit(solution)/shard_map/ppermute | solution.py:32
  78.4 18.5 %copy-start.5 = (bf16[3,56,896]{2,1,0:T(8,128)(2,1)}, bf16[3,56,896]{2,1,0:T(8,128)(2,1)S(1)}, u32[]{:S(2)}) copy-start(bf16[3,56,896]{2,1,0:T(8,128)(2,1)S(1)} %collective-permute-done.4.refs_2_) | copy-start | bytes 903172
  78.4 31.7 %collective-permute-start.6 = (bf16[2,56,896]{2,1,0:T(8,128)(2,1)S(1)}, bf16[2,56,896]{2,1,0:T(8,128)(2,1)}, u32[]{:S(2)}, u32[]{:S(2)}) collective-permute-start(bf16[2,56,896]{2,1,0:T(8,128)(2,1)S(1)} %slice.75), channel_id=1, source_target_pairs={{0,192},{64,0},{128,64},{192,128},{1,193},{65,1},{129,65},{193,129... | collective-permute-start | bytes 602120 | tf_op jit(solution)/shard_map/ppermute | solution.py:32
  82.5 6.9 %collective-permute-start.20 = (bf16[2,56,896]{2,1,0:T(8,128)(2,1)S(1)}, bf16[2,56,896]{2,1,0:T(8,128)(2,1)}, u32[]{:S(2)}, u32[]{:S(2)}) collective-permute-start(bf16[2,56,896]{2,1,0:T(8,128)(2,1)S(1)} %slice.87), channel_id=1, source_target_pairs={{0,192},{64,0},{128,64},{192,128},{1,193},{65,1},{129,65},{193,129... | collective-permute-start | bytes 602120 | tf_op jit(solution)/shard_map/ppermute | solution.py:32
  89.4 14.7 %collective-permute-start.12 = (bf16[32,4,640]{2,1,0:T(4,128)(2,1)S(1)}, bf16[32,4,640]{2,1,0:T(4,128)(2,1)S(1)}, u32[]{:S(2)}, u32[]{:S(2)}) collective-permute-start(bf16[32,4,640]{2,1,0:T(4,128)(2,1)S(1)} %get-tuple-element.33), channel_id=1, source_target_pairs={{0,4},{4,0},{1,5},{5,1},{2,6},{6,2},{3,7},{7,3},{8,12},{12,8},{9,1... | collective-permute-start | bytes 491528 | tf_op jit(solution)/shard_map/ppermute | solution.py:36
  91.0 0.7 copy-start.14
  96.9 18.1 %collective-permute-start.21 = (bf16[37,8,512]{2,1,0:T(8,128)(2,1)}, bf16[37,8,512]{2,1,0:T(8,128)(2,1)S(1)}, u32[]{:S(2)}, u32[]{:S(2)}) collective-permute-start(bf16[37,8,512]{2,1,0:T(8,128)(2,1)} %get-tuple-element.26), channel_id=1, source_target_pairs={{0,2},{1,3},{2,0},{3,1},{4,6},{5,7},{6,4},{7,5},{8,10},{9,11},{10,... | collective-permute-start | bytes 909320 | tf_op jit(solution)/shard_map/ppermute | solution.py:32
  99.9 17.8 %collective-permute-start.22 = (bf16[37,8,512]{2,1,0:T(8,128)(2,1)}, bf16[37,8,512]{2,1,0:T(8,128)(2,1)S(1)}, u32[]{:S(2)}, u32[]{:S(2)}) collective-permute-start(bf16[37,8,512]{2,1,0:T(8,128)(2,1)} %get-tuple-element.27), channel_id=1, source_target_pairs={{0,1},{1,2},{2,3},{3,0},{4,5},{5,6},{6,7},{7,4},{8,9},{9,10},{10,1... | collective-permute-start | bytes 909320 | tf_op jit(solution)/shard_map/ppermute | solution.py:32
  102.8 6.2 %collective-permute-start.5 = (bf16[1,56,896]{2,1,0:T(8,128)(2,1)S(1)}, bf16[1,56,896]{2,1,0:T(8,128)(2,1)S(1)}, u32[]{:S(2)}, u32[]{:S(2)}) collective-permute-start(bf16[1,56,896]{2,1,0:T(8,128)(2,1)S(1)} %slice.74), channel_id=1, source_target_pairs={{0,64},{64,128},{128,192},{192,0},{1,65},{65,129},{129,193},{193,1... | collective-permute-start | bytes 301064 | tf_op jit(solution)/shard_map/ppermute | solution.py:32
  104.0 15.4 %collective-permute-start.23 = (bf16[37,8,512]{2,1,0:T(8,128)(2,1)}, bf16[37,8,512]{2,1,0:T(8,128)(2,1)}, u32[]{:S(2)}, u32[]{:S(2)}) collective-permute-start(bf16[37,8,512]{2,1,0:T(8,128)(2,1)} %get-tuple-element.28), channel_id=1, source_target_pairs={{0,3},{1,0},{2,1},{3,2},{4,7},{5,4},{6,5},{7,6},{8,11},{9,8},{10,9... | collective-permute-start | bytes 909320 | tf_op jit(solution)/shard_map/ppermute | solution.py:32
  108.2 6.8 %copy-start.3 = (bf16[32,8,896]{2,1,0:T(8,128)(2,1)}, bf16[32,8,896]{2,1,0:T(8,128)(2,1)S(1)}, u32[]{:S(2)}) copy-start(bf16[32,8,896]{2,1,0:T(8,128)(2,1)S(1)} %slice.72.refs_3_) | copy-start | bytes 1376260
  109.0 1.1 copy-start.21
  109.0 43.1 %collective-permute-start.24 = (bf16[32,8,896]{2,1,0:T(8,128)(2,1)S(1)}, bf16[32,8,896]{2,1,0:T(8,128)(2,1)S(1)}, u32[]{:S(2)}, u32[]{:S(2)}) collective-permute-start(bf16[32,8,896]{2,1,0:T(8,128)(2,1)S(1)} %slice.72.refs_3_), channel_id=1, source_target_pairs={{0,4},{4,0},{1,5},{5,1},{2,6},{6,2},{3,7},{7,3},{8,12},{12,8},{9,1... | collective-permute-start | bytes 1376264 | tf_op jit(solution)/shard_map/ppermute | solution.py:36
  115.0 7.7 %collective-permute-start.10 = (bf16[23,8,512]{2,1,0:T(8,128)(2,1)}, bf16[23,8,512]{2,1,0:T(8,128)(2,1)S(1)}, u32[]{:S(2)}, u32[]{:S(2)}) collective-permute-start(bf16[23,8,512]{2,1,0:T(8,128)(2,1)} %get-tuple-element.21), channel_id=1, source_target_pairs={{0,1},{1,2},{2,3},{3,0},{4,5},{5,6},{6,7},{7,4},{8,9},{9,10},{10,1... | collective-permute-start | bytes 565256 | tf_op jit(solution)/shard_map/ppermute | solution.py:32
  115.1 5.0 %copy-start.12 = (bf16[37,8,512]{2,1,0:T(8,128)(2,1)}, bf16[37,8,512]{2,1,0:T(8,128)(2,1)S(1)}, u32[]{:S(2)}) copy-start(bf16[37,8,512]{2,1,0:T(8,128)(2,1)S(1)} %collective-permute-done.21.refs_2_) | copy-start | bytes 909316
  115.1 7.6 %collective-permute-start.11 = (bf16[23,8,512]{2,1,0:T(8,128)(2,1)}, bf16[23,8,512]{2,1,0:T(8,128)(2,1)S(1)}, u32[]{:S(2)}, u32[]{:S(2)}) collective-permute-start(bf16[23,8,512]{2,1,0:T(8,128)(2,1)} %get-tuple-element.22), channel_id=1, source_target_pairs={{0,3},{1,0},{2,1},{3,2},{4,7},{5,4},{6,5},{7,6},{8,11},{9,8},{10,9... | collective-permute-start | bytes 565256 | tf_op jit(solution)/shard_map/ppermute | solution.py:32
  117.7 2.3 %copy-start.13 = (bf16[37,8,512]{2,1,0:T(8,128)(2,1)}, bf16[37,8,512]{2,1,0:T(8,128)(2,1)S(1)}, u32[]{:S(2)}) copy-start(bf16[37,8,512]{2,1,0:T(8,128)(2,1)S(1)} %collective-permute-done.22.refs_3_) | copy-start | bytes 909316
  117.7 9.3 %collective-permute-start.9 = (bf16[23,8,512]{2,1,0:T(8,128)(2,1)}, bf16[23,8,512]{2,1,0:T(8,128)(2,1)}, u32[]{:S(2)}, u32[]{:S(2)}) collective-permute-start(bf16[23,8,512]{2,1,0:T(8,128)(2,1)} %get-tuple-element.20), channel_id=1, source_target_pairs={{0,2},{1,3},{2,0},{3,1},{4,6},{5,7},{6,4},{7,5},{8,10},{9,11},{10,... | collective-permute-start | bytes 565256 | tf_op jit(solution)/shard_map/ppermute | solution.py:32
  122.7 4.4 %copy-start.15 = (bf16[23,8,512]{2,1,0:T(8,128)(2,1)}, bf16[23,8,512]{2,1,0:T(8,128)(2,1)S(1)}, u32[]{:S(2)}) copy-start(bf16[23,8,512]{2,1,0:T(8,128)(2,1)S(1)} %collective-permute-done.10.refs_3_) | copy-start | bytes 565252
  122.7 4.4 %copy-start.16 = (bf16[23,8,512]{2,1,0:T(8,128)(2,1)}, bf16[23,8,512]{2,1,0:T(8,128)(2,1)S(1)}, u32[]{:S(2)}) copy-start(bf16[23,8,512]{2,1,0:T(8,128)(2,1)S(1)} %collective-permute-done.11.refs_4_) | copy-start | bytes 565252
  137.6 23.5 %all-to-all-start.3 = ((f32[64,1,512]{2,1,0:T(1,128)}), f32[64,1,512]{2,1,0:T(1,128)S(1)}, u32[]{:S(2)}, u32[]{:S(2)}) async-start(f32[64,1,512]{2,1,0:T(1,128)} %broadcast_in_dim.17), calls=%async_computation.3 | async-start | bytes 262144 | tf_op jit(solution)/shard_map/all_to_all | solution.py:378
  152.1 9.0 %copy-start.11 = (bf16[32,8,896]{2,1,0:T(8,128)(2,1)}, bf16[32,8,896]{2,1,0:T(8,128)(2,1)S(1)}, u32[]{:S(2)}) copy-start(bf16[32,8,896]{2,1,0:T(8,128)(2,1)S(1)} %collective-permute-done.24.refs_4_) | copy-start | bytes 1376260
  161.1 0.7 copy-start.6
  (3 other events, 1.9 us)

commit v4 on v3

--- a/solution.py
+++ b/solution.py
@@ -104,9 +104,10 @@
         out_ref[e] = ref[...]
 
 
-def project_kernel(where_ref, *refs):
-    pieces, (own_ref, other_ref), out_refs = refs[:5], refs[5:7], refs[7:11]
-    w_ref, mixed_ref, low_ref, hold_ref, sems = refs[11:]
+def project_kernel(plan, where_ref, *refs):
+    n = sum(len(of) for of in plan)
+    pieces, (own_ref, other_ref), out_refs = list(refs[:n]), refs[n : n + 2], refs[n + 2 : n + 6]
+    w_ref, mixed_ref, low_ref, hold_ref, sems = refs[n + 6 :]
     groups = 7 * w_ref.shape[1]
     core = where_ref[0]
     copies = []
@@ -114,27 +115,30 @@
         at = pl.ds(pl.multiple_of(256 * side, 256), 256)
         copies.append(pltpu.make_async_copy(ref.at[pl.ds(0, 256)], mixed_ref.at[at], sems.at[i]))
         copies.append(pltpu.make_async_copy(ref.at[pl.ds(256, 16)], low_ref.at[side], sems.at[2 + i]))
-    loads = []
-    for d, piece in enumerate(pieces):
-        place = w_ref.at[min(d, 3)]
-        if d >= 3:
-            place = place.at[pl.ds(pieces[3].shape[0] * (d - 3), piece.shape[0])]
-        loads.append(pltpu.make_async_copy(piece, place, sems.at[4 + d]))
-    for copy in copies + loads:
-        copy.start()
+    loads, used = [], 4
+    for d, of in enumerate(plan):
+        at, group = 0, []
+        for count in of:
+            place = w_ref.at[d, pl.ds(at, count)]
+            group.append(pltpu.make_async_copy(pieces.pop(0), place, sems.at[used]))
+            at, used = at + count, used + 1
+        loads.append(group)
+    for group in [copies] + loads:
+        for copy in group:
+            copy.start()
     for copy in copies:
         copy.wait()
     low = [low_ref[i, :, 0:256].astype(F32).reshape(2, 8, 256) for i in range(2)]
     low = jnp.concatenate(low, axis=2).astype(BF16)
     for d in range(4):
-        for copy in loads[d : d + 1] if d < 3 else loads[3:]:
+        for copy in loads[d]:
             copy.wait()
         w = w_ref[d].astype(F32).reshape(8 * groups, 896).astype(BF16)
         got = lax.dot_general(w, mixed_ref[...], NT, preferred_element_type=F32)
         at = where_ref[1 + d]
         hold_ref[at, 0:groups] = got.reshape(groups, 8, 512).astype(BF16)
         hold_ref[at, groups : groups + 2] = low
-    outs = [pltpu.make_async_copy(hold_ref.at[j], out_refs[j], sems.at[9 + j]) for j in range(4)]
+    outs = [pltpu.make_async_copy(hold_ref.at[j], out_refs[j], sems.at[used + j]) for j in range(4)]
     for copy in outs:
         copy.start()
     for copy in outs:
@@ -255,7 +259,7 @@
 
 
 GROUPS = ((0, 1, 7, 2, 6), (3, 5, 4))
-VIA_UP = (3, 1)
+VIA_UP = (2, 1)
 
 
 def per_device(
@@ -294,12 +298,16 @@
 
     w_t, parts = after(w_out.T, sent), []
     z1, z7, z2, z6, z3, z5, z4 = [shift(w_t, "pop_1", 8, e) for e in (1, 7, 2, 6, 3, 5, 4)]
-    for i, ins in enumerate(([w_t, z1, z7, z2, z6], [z3, z5, z4])):
-        n, via = len(GROUPS[i]), VIA_UP[i]
+    o1, o3, o2 = [shift(w_t, "pop_0", 4, d)[None] for d in (1, 3, 2)]
+    for i, ins in enumerate(([z1, z7, z2, z6], [z3, z5, z4])):
+        n, via = len(ins), VIA_UP[i]
         own = call(stack_kernel, shape((n, 56, feats)), ins)
         up, down = shift(own, "pop_0", 4, 1), shift(own, "pop_0", 4, 3)
         far = [shift(up[:via], "pop_0", 4, 1), shift(down[via:], "pop_0", 4, 3)]
-        parts.append([own, up, down, *far])
+        if i == 0:
+            parts.append([[w_t[None], own], [o1, up], [o3, down], [o2, *far]])
+        else:
+            parts.append([[own], [up], [down], far])
     where = ints(c, *[(x + d - y) % 4 for d in (0, -1, 1, 2)])
 
     cos_all, sin_all = tables(jnp.arange(tok, dtype=F32), HEAD_DIM)
@@ -317,23 +325,24 @@
     )
     mixed_b = swap(mixed)
 
-    outs = [
-        call(
-            project_kernel,
-            [shape((7 * len(group) + 2, 8, 512))] * 4,
-            (where, *pieces, mixed, mixed_b),
-            smem=1,
-            scratch=[
-                pltpu.VMEM((4, len(group), 56, feats), BF16),
-                pltpu.VMEM((512, feats), BF16),
-                pltpu.VMEM((2, 16, feats), BF16),
-                pltpu.VMEM((4, 7 * len(group) + 2, 8, 512), BF16),
-                pltpu.SemaphoreType.DMA((13,)),
-            ],
-            load=False,
+    outs = []
+    for group, pieces in zip(GROUPS, parts):
+        outs.append(
+            call(
+                functools.partial(project_kernel, [[a.shape[0] for a in of] for of in pieces]),
+                [shape((7 * len(group) + 2, 8, 512))] * 4,
+                (where, *sum(pieces, []), mixed, mixed_b),
+                smem=1,
+                scratch=[
+                    pltpu.VMEM((4, len(group), 56, feats), BF16),
+                    pltpu.VMEM((512, feats), BF16),
+                    pltpu.VMEM((2, 16, feats), BF16),
+                    pltpu.VMEM((4, 7 * len(group) + 2, 8, 512), BF16),
+                    pltpu.SemaphoreType.DMA((17,)),
+                ],
+                load=False,
+            )
         )
-        for group, pieces in zip(GROUPS, parts)
-    ]
     mets = []
     for out in outs:
         mets.append([out[0]] + [shift(out[s], "mp", 4, s) for s in (2, 1, 3)])

time: 167 us -> 168 us (level)
  starting transfers between devices: 81 us -> 86.1 us
  local copies, waits for them, and re-layouts: 12.2 us -> 9.94 us
    ppermute x4, starting transfers between devices: 10.8 us -> 17.5 us  [swap(): return lax.ppermute(x, 'pop_2', [(0, 1), (1, 0)])]
    all_to_all x1, starting transfers between devices: 13.2 us -> 11.2 us  [per_device(): lax.all_to_all(jnp.broadcast_to(err, (64, 1, 512)), POP, 0, 0, tiled=True)]
    ppermute x21 -> x24, waiting for transfers between devices: 11 us -> 9.62 us  [shift(): return lax.ppermute(x, axis, [(i, (i + step) % size) for i in range(size)])]
    ppermute x21 -> x24, starting transfers between devices: 40.2 us -> 40.6 us  [shift(): return lax.ppermute(x, axis, [(i, (i + step) % size) for i in range(size)])]
  transfers between devices with their start and end apart: 28 -> 31, of which waited for: 5 -> 7; matrix products, arithmetic and copies ran while one was open for 11% -> 10% of each run, Pallas kernels for 14% -> 14%
where the time goes in v4:
time: 168 us; the launch traced here: 167 us
  starting transfers between devices  86.1 us (51%)
  Pallas kernels  31.6 us (19%)
  waiting for transfers between devices  20.8 us (12%)
  local copies, waits for them, and re-layouts  9.94 us (6%)
  blocking collectives  7.4 us (4%)
  other arithmetic  6.88 us (4%)
  matrix products  2.32 us (1%)
  between operations  2.24 us (1%)
    ppermute x24, starting transfers between devices, shift(): return lax.ppermute(x, axis, [(i, (i + step) % size) for i in range(size)])  40.6 us
    pallas_call x9, Pallas kernels, call(): pl.pallas_call(kernel, out_shape=out, in_specs=[pl.BlockSpec(memory_space...  31.6 us
    ppermute x4, starting transfers between devices, swap(): return lax.ppermute(x, 'pop_2', [(0, 1), (1, 0)])  17.5 us
    all_to_all x1, starting transfers between devices, per_device(): lax.all_to_all(jnp.broadcast_to(err, (64, 1, 512)), POP, 0, 0, tiled=True)  11.2 us
    ppermute x24, waiting for transfers between devices, shift(): return lax.ppermute(x, axis, [(i, (i + step) % size) for i in range(size)])  9.62 us
    all_to_all x1, waiting for transfers between devices, per_device(): lax.all_to_all(jnp.broadcast_to(err, (64, 1, 512)), POP, 0, 0, tiled=True)  9.08 us
    all_to_all x1, starting transfers between devices, per_device(): late = lax.all_to_all(late, CHIPS, 0, 0, tiled=True)  8.69 us
    all_to_all x1, starting transfers between devices, per_device(): recv = lax.all_to_all(sent, CHIPS, 0, 0, tiled=True)  8.15 us
  transfers between devices with their start and end apart: 31, of which 7 were waited for; matrix products, arithmetic and copies ran while one was open for 10% of the time, Pallas kernels for 14%

profile of v4, /device:TPU:1, one launch (start us, length us, event | category | flops | bytes accessed | tf_op | source)
XLA Modules:
  0.0 167.3 jit_solution(2683594644115451582)
XLA Ops:
  2.0 4.0 %shard_map.139 = bf16[32,8,1920]{2,1,0:T(8,128)(2,1)} custom-call(s32[2]{0:T(128)} %pad_add_fusion.1.refs_0_, bf16[256,3584]{1,0:T(8,128)(2,1)} %refs_1_.1, bf16[56,896]{1,0:T(8,128)(2,1)} %refs_2_.1, bf16[4,3584]{1,0:T(4,128)(2,1)} %bitcast.72, bf16[4,896]{1,0:T(4,128)(2,1)} %bitcast.74, bf16[4,896]{1,0:T(4,128)(2,1)} %bitcast.75), custom_call_target="tpu_custom_call" | custom-call | flops 1000000000 | bytes 2000000 | tf_op jit(solution)/shard_map/pallas_call | solution.py:239
  6.1 2.5 %collective-permute-start.13 = (bf16[56,896]{1,0:T(8,128)(2,1)}, bf16[56,896]{1,0:T(8,128)(2,1)S(1)}, u32[]{:S(2)}, u32[]{:S(2)}) collective-permute-start(bf16[56,896]{1,0:T(8,128)(2,1)} %bitcast.6), channel_id=1, source_target_pairs={{0,8},{8,16},{16,24},{24,32},{32,40},{40,48},{48,56},{56,0},{1,9},... | collective-permute-start | bytes 301064 | tf_op jit(solution)/shard_map/ppermute | solution.py:32
  8.6 4.0 %collective-permute-start.14 = (bf16[56,896]{1,0:T(8,128)(2,1)}, bf16[56,896]{1,0:T(8,128)(2,1)}, u32[]{:S(2)}, u32[]{:S(2)}) collective-permute-start(bf16[56,896]{1,0:T(8,128)(2,1)} %bitcast.6), channel_id=1, source_target_pairs={{0,56},{8,0},{16,8},{24,16},{32,24},{40,32},{48,40},{56,48},{1,57}... | collective-permute-start | bytes 301064 | tf_op jit(solution)/shard_map/ppermute | solution.py:32
  12.6 3.6 %collective-permute-start.16 = (bf16[56,896]{1,0:T(8,128)(2,1)}, bf16[56,896]{1,0:T(8,128)(2,1)}, u32[]{:S(2)}, u32[]{:S(2)}) collective-permute-start(bf16[56,896]{1,0:T(8,128)(2,1)} %bitcast.6), channel_id=1, source_target_pairs={{0,48},{8,56},{16,0},{24,8},{32,16},{40,24},{48,32},{56,40},{1,49}... | collective-permute-start | bytes 301064 | tf_op jit(solution)/shard_map/ppermute | solution.py:32
  16.2 8.2 %all-to-all-start = ((bf16[32,8,1920]{2,1,0:T(8,128)(2,1)}), bf16[32,8,1920]{2,1,0:T(8,128)(2,1)}, u32[]{:S(2)}, u32[]{:S(2)}) async-start(bf16[32,8,1920]{2,1,0:T(8,128)(2,1)} %shard_map.139), calls=%async_computation | async-start | bytes 1966080 | tf_op jit(solution)/shard_map/all_to_all | solution.py:297
  24.4 1.2 collective-permute-start.17
  27.7 0.9 concatenate.27
  30.0 0.8 fusion.7.refs_4_
  30.8 1.3 convolution_convert_fusion.1.refs_5_
  32.7 3.0 %collective-permute-start = (bf16[56,896]{1,0:T(8,128)(2,1)}, bf16[56,896]{1,0:T(8,128)(2,1)S(1)}, u32[]{:S(2)}, u32[]{:S(2)}) collective-permute-start(bf16[56,896]{1,0:T(8,128)(2,1)} %bitcast.6), channel_id=1, source_target_pairs={{0,24},{8,32},{16,40},{24,48},{32,56},{40,0},{48,8},{56,16},{1,25}... | collective-permute-start | bytes 301064 | tf_op jit(solution)/shard_map/ppermute | solution.py:32
  35.7 1.5 collective-permute-start.1
  37.2 5.1 %collective-permute-start.2 = (bf16[56,896]{1,0:T(8,128)(2,1)}, bf16[56,896]{1,0:T(8,128)(2,1)S(1)}, u32[]{:S(2)}, u32[]{:S(2)}) collective-permute-start(bf16[56,896]{1,0:T(8,128)(2,1)} %bitcast.6), channel_id=1, source_target_pairs={{0,32},{8,40},{16,48},{24,56},{32,0},{40,8},{48,16},{56,24},{1,33}... | collective-permute-start | bytes 301064 | tf_op jit(solution)/shard_map/ppermute | solution.py:32
  42.3 1.9 %shard_map.143.refs_1_ = bf16[4,56,896]{2,1,0:T(8,128)(2,1)} custom-call(bf16[56,896]{1,0:T(8,128)(2,1)} %copy-done.18, bf16[56,896]{1,0:T(8,128)(2,1)} %collective-permute-done.14.refs_1_, bf16[56,896]{1,0:T(8,128)(2,1)} %collective-permute-done.15.refs_2_, bf16[56,896]{1,0:T(8,128)(2,1)} %collective-permute-done.16.refs_3_), custom_call_target="tpu_custom_call" | custom-call | flops 1000000000 | bytes 2000000 | tf_op jit(solution)/shard_map/pallas_call | solution.py:239
  44.2 1.3 collective-permute-start.18
  45.5 2.1 %all-to-all-done.refs_1_ = bf16[32,8,1920]{2,1,0:T(8,128)(2,1)} async-done(((bf16[32,8,1920]{2,1,0:T(8,128)(2,1)}), bf16[32,8,1920]{2,1,0:T(8,128)(2,1)}, u32[]{:S(2)}, u32[]{:S(2)}) %all-to-all-start) | async-done | bytes 983072 | tf_op jit(solution)/shard_map/all_to_all | solution.py:297
  47.6 8.7 %all-to-all-start.1 = ((bf16[32,8,640]{2,1,0:T(8,128)(2,1)}), bf16[32,8,640]{2,1,0:T(8,128)(2,1)S(1)}, u32[]{:S(2)}, u32[]{:S(2)}) async-start(bf16[32,8,640]{2,1,0:T(8,128)(2,1)} %concatenate.27), calls=%async_computation.1 | async-start | bytes 655360 | tf_op jit(solution)/shard_map/all_to_all | solution.py:366
  56.3 1.1 convert_reduce_fusion.refs_2_
  57.4 2.7 %collective-permute-start.20 = (bf16[4,56,896]{2,1,0:T(8,128)(2,1)}, bf16[4,56,896]{2,1,0:T(8,128)(2,1)S(1)}, u32[]{:S(2)}, u32[]{:S(2)}) collective-permute-start(bf16[4,56,896]{2,1,0:T(8,128)(2,1)} %shard_map.143.refs_1_), channel_id=1, source_target_pairs={{0,192},{64,0},{128,64},{192,128},{1,193},{65,1},{129,65},{193,129... | collective-permute-start | bytes 1204232 | tf_op jit(solution)/shard_map/ppermute | solution.py:32
  60.1 7.9 %collective-permute-start.7 = (f32[8,896]{1,0:T(8,128)S(1)}, f32[8,896]{1,0:T(8,128)S(1)}, u32[]{:S(2)}, u32[]{:S(2)}) collective-permute-start(f32[8,896]{1,0:T(8,128)S(1)} %convert_reduce_fusion.refs_2_), channel_id=1, source_target_pairs={{0,4},{4,0},{1,5},{5,1},{2,6},{6,2},{3,7},{7,3},{8,12},{12,8},{9,1... | collective-permute-start | bytes 86024 | tf_op jit(solution)/shard_map/ppermute | solution.py:36
  68.7 1.8 %shard_map.140.refs_0_ = bf16[3,56,896]{2,1,0:T(8,128)(2,1)} custom-call(bf16[56,896]{1,0:T(8,128)(2,1)} %copy-done.19, bf16[56,896]{1,0:T(8,128)(2,1)} %copy-done.20, bf16[56,896]{1,0:T(8,128)(2,1)} %copy-done.21), custom_call_target="tpu_custom_call" | custom-call | flops 1000000000 | bytes 2000000 | tf_op jit(solution)/shard_map/pallas_call | solution.py:239
  71.7 5.3 %shard_map.141.refs_5_.refs_9_ = bf16[272,896]{1,0:T(8,128)(2,1)} custom-call(s32[1]{0:T(128)} %bitcast.15.refs_0_, bf16[32,8,1920]{2,1,0:T(8,128)(2,1)} %all-to-all-done.refs_1_, f32[8,896]{1,0:T(8,128)} %copy-done.10, f32[8,896]{1,0:T(8,128)} %copy-done.23, bf16[256,128]{1,0:T(8,128)(2,1)} %fusion.7.refs_4_, ...), custom_call_target="tpu_custom_call" | custom-call | flops 1000000000 | bytes 2000000 | tf_op jit(solution)/shard_map/pallas_call | solution.py:239
  77.0 1.0 collective-permute-start.8
  78.8 1.2 collective-permute-done.4.refs_2_
  79.9 1.8 %collective-permute-start.19 = (bf16[56,896]{1,0:T(8,128)(2,1)}, bf16[56,896]{1,0:T(8,128)(2,1)}, u32[]{:S(2)}, u32[]{:S(2)}) collective-permute-start(bf16[56,896]{1,0:T(8,128)(2,1)} %bitcast.6), channel_id=1, source_target_pairs={{0,192},{64,0},{128,64},{192,128},{1,193},{65,1},{129,65},{193,129... | collective-permute-start | bytes 301064 | tf_op jit(solution)/shard_map/ppermute | solution.py:32
  82.6 2.2 %collective-permute-start.23 = (bf16[2,56,896]{2,1,0:T(8,128)(2,1)S(1)}, bf16[2,56,896]{2,1,0:T(8,128)(2,1)}, u32[]{:S(2)}, u32[]{:S(2)}) collective-permute-start(bf16[2,56,896]{2,1,0:T(8,128)(2,1)S(1)} %slice.87), channel_id=1, source_target_pairs={{0,192},{64,0},{128,64},{192,128},{1,193},{65,1},{129,65},{193,129... | collective-permute-start | bytes 602120 | tf_op jit(solution)/shard_map/ppermute | solution.py:32
  85.0 2.3 %collective-permute-done.21 = bf16[56,896]{1,0:T(8,128)(2,1)} collective-permute-done((bf16[56,896]{1,0:T(8,128)(2,1)}, bf16[56,896]{1,0:T(8,128)(2,1)}, u32[]{:S(2)}, u32[]{:S(2)}) %collective-permute-start.21) | collective-permute-done | bytes 100384 | tf_op jit(solution)/shard_map/ppermute | solution.py:32
  87.8 1.0 collective-permute-done.22.refs_7_
  88.8 6.5 %collective-permute-start.12 = (bf16[32,4,640]{2,1,0:T(4,128)(2,1)S(1)}, bf16[32,4,640]{2,1,0:T(4,128)(2,1)S(1)}, u32[]{:S(2)}, u32[]{:S(2)}) collective-permute-start(bf16[32,4,640]{2,1,0:T(4,128)(2,1)S(1)} %get-tuple-element.33), channel_id=1, source_target_pairs={{0,4},{4,0},{1,5},{5,1},{2,6},{6,2},{3,7},{7,3},{8,12},{12,8},{9,1... | collective-permute-start | bytes 491528 | tf_op jit(solution)/shard_map/ppermute | solution.py:36
  95.4 5.2 %shard_map.144 = (bf16[37,8,512]{2,1,0:T(8,128)(2,1)}, bf16[37,8,512]{2,1,0:T(8,128)(2,1)}, bf16[37,8,512]{2,1,0:T(8,128)(2,1)}, bf16[37,8,512]{2,1,0:T(8,128)(2,1)}) custom-call(s32[5]{0:T(128)} %stack.46.where_ref, bf16[1,56,896]{2,1,0:T(8,128)(2,1)} %bitcast.30.refs_0_, bf16[4,56,896]{2,1,0:T(8,128)(2,1)} %shard_map.143.refs_1_, ...), custom_call_target="tpu_custom_call" | custom-call | flops 1000000000 | bytes 2000000 | tf_op jit(solution)/shard_map/pallas_call | solution.py:239
  100.6 3.0 %collective-permute-start.24 = (bf16[37,8,512]{2,1,0:T(8,128)(2,1)}, bf16[37,8,512]{2,1,0:T(8,128)(2,1)S(1)}, u32[]{:S(2)}, u32[]{:S(2)}) collective-permute-start(bf16[37,8,512]{2,1,0:T(8,128)(2,1)} %get-tuple-element.26), channel_id=1, source_target_pairs={{0,2},{1,3},{2,0},{3,1},{4,6},{5,7},{6,4},{7,5},{8,10},{9,11},{10,... | collective-permute-start | bytes 909320 | tf_op jit(solution)/shard_map/ppermute | solution.py:32
  105.5 0.9 slice.74
  106.7 2.4 %collective-permute-start.26 = (bf16[37,8,512]{2,1,0:T(8,128)(2,1)}, bf16[37,8,512]{2,1,0:T(8,128)(2,1)}, u32[]{:S(2)}, u32[]{:S(2)}) collective-permute-start(bf16[37,8,512]{2,1,0:T(8,128)(2,1)} %get-tuple-element.28), channel_id=1, source_target_pairs={{0,3},{1,0},{2,1},{3,2},{4,7},{5,4},{6,5},{7,6},{8,11},{9,8},{10,9... | collective-permute-start | bytes 909320 | tf_op jit(solution)/shard_map/ppermute | solution.py:32
  109.1 0.8 fusion.3.refs_5_
  109.9 1.1 slice.72.refs_3_
  110.9 0.8 collective-permute-done.5.refs_3_
  111.7 2.1 %collective-permute-start.27 = (bf16[32,8,896]{2,1,0:T(8,128)(2,1)S(1)}, bf16[32,8,896]{2,1,0:T(8,128)(2,1)S(1)}, u32[]{:S(2)}, u32[]{:S(2)}) collective-permute-start(bf16[32,8,896]{2,1,0:T(8,128)(2,1)S(1)} %slice.72.refs_3_), channel_id=1, source_target_pairs={{0,4},{4,0},{1,5},{5,1},{2,6},{6,2},{3,7},{7,3},{8,12},{12,8},{9,1... | collective-permute-start | bytes 1376264 | tf_op jit(solution)/shard_map/ppermute | solution.py:36
  113.8 4.8 %shard_map.142 = (bf16[23,8,512]{2,1,0:T(8,128)(2,1)}, bf16[23,8,512]{2,1,0:T(8,128)(2,1)}, bf16[23,8,512]{2,1,0:T(8,128)(2,1)}, bf16[23,8,512]{2,1,0:T(8,128)(2,1)}) custom-call(s32[5]{0:T(128)} %stack.46.where_ref, bf16[3,56,896]{2,1,0:T(8,128)(2,1)} %shard_map.140.refs_0_, bf16[3,56,896]{2,1,0:T(8,128)(2,1)} %collective-permute-done.3.refs_1_, ...), custom_call_target="tpu_custom_call" | custom-call | flops 1000000000 | bytes 2000000 | tf_op jit(solution)/shard_map/pallas_call | solution.py:239
  118.7 2.6 %collective-permute-start.11 = (bf16[23,8,512]{2,1,0:T(8,128)(2,1)}, bf16[23,8,512]{2,1,0:T(8,128)(2,1)S(1)}, u32[]{:S(2)}, u32[]{:S(2)}) collective-permute-start(bf16[23,8,512]{2,1,0:T(8,128)(2,1)} %get-tuple-element.22), channel_id=1, source_target_pairs={{0,3},{1,0},{2,1},{3,2},{4,7},{5,4},{6,5},{7,6},{8,11},{9,8},{10,9... | collective-permute-start | bytes 565256 | tf_op jit(solution)/shard_map/ppermute | solution.py:32
  121.4 0.9 collective-permute-start.9
  122.2 0.8 fusion.5.refs_5_
  123.7 2.6 %shard_map.145.refs_7_ = f32[4,1,512]{2,1,0:T(1,128)} custom-call(s32[1]{0:T(128)} %bitcast.refs_0_, bf16[37,8,512]{2,1,0:T(8,128)(2,1)} %get-tuple-element.25.refs_1_, bf16[37,8,512]{2,1,0:T(8,128)(2,1)} %copy-done.13, bf16[37,8,512]{2,1,0:T(8,128)(2,1)} %copy-done.14, bf16[37,8,512]{2,1,0:T(8,128)(2,1)} %collective-permute-done.26.refs_4_, ...), custom_call_target="tpu_custom_call" | custom-call | flops 1000000000 | bytes 2000000 | tf_op jit(solution)/shard_map/pallas_call | solution.py:239
  126.3 4.3 %collective-permute-done.9.refs_2_ = bf16[23,8,512]{2,1,0:T(8,128)(2,1)} collective-permute-done((bf16[23,8,512]{2,1,0:T(8,128)(2,1)}, bf16[23,8,512]{2,1,0:T(8,128)(2,1)}, u32[]{:S(2)}, u32[]{:S(2)}) %collective-permute-start.9) | collective-permute-done | bytes 188448 | tf_op jit(solution)/shard_map/ppermute | solution.py:32
  130.7 2.4 %shard_map.146 = f32[4,1,512]{2,1,0:T(1,128)} custom-call(s32[1]{0:T(128)} %bitcast.refs_0_, bf16[23,8,512]{2,1,0:T(8,128)(2,1)} %get-tuple-element.19.refs_1_, bf16[23,8,512]{2,1,0:T(8,128)(2,1)} %collective-permute-done.9.refs_2_, bf16[23,8,512]{2,1,0:T(8,128)(2,1)} %copy-done.16, bf16[23,8,512]{2,1,0:T(8,128)(2,1)} %copy-done.17, ...), custom_call_target="tpu_custom_call" | custom-call | flops 1000000000 | bytes 2000000 | tf_op jit(solution)/shard_map/pallas_call | solution.py:239
  133.1 7.4 %all_to_all.20 = f32[4,1,512]{2,1,0:T(1,128)S(1)} all-to-all(f32[4,1,512]{2,1,0:T(1,128)} %shard_map.146), channel_id=1, replica_groups=mesh['pop_0'=4,'pop_1'=8,'pop_2'=2,'mp'=4] {'mp'}, dimensions={0} | all-to-all | bytes 16384 | tf_op jit(solution)/shard_map/all_to_all | solution.py:385
  140.5 0.7 broadcast_in_dim.53
  141.2 11.2 %all-to-all-start.3 = ((f32[64,1,512]{2,1,0:T(1,128)}), f32[64,1,512]{2,1,0:T(1,128)S(1)}, u32[]{:S(2)}, u32[]{:S(2)}) async-start(f32[64,1,512]{2,1,0:T(1,128)} %broadcast_in_dim.53), calls=%async_computation.3 | async-start | bytes 262144 | tf_op jit(solution)/shard_map/all_to_all | solution.py:387
  153.7 9.1 %all-to-all-done.3.refs_1_ = f32[64,1,512]{2,1,0:T(1,128)S(1)} async-done(((f32[64,1,512]{2,1,0:T(1,128)}), f32[64,1,512]{2,1,0:T(1,128)S(1)}, u32[]{:S(2)}, u32[]{:S(2)}) %all-to-all-start.3) | async-done | bytes 131104 | tf_op jit(solution)/shard_map/all_to_all | solution.py:387
  163.4 3.6 %shard_map.147 = (f32[56,896]{1,0:T(8,128)}, f32[56,896]{1,0:T(8,128)}, f32[1,128]{1,0:T(1,128)}) custom-call(s32[2]{0:T(128)} %pad_add_fusion.refs_0_, f32[64,1,512]{2,1,0:T(1,128)} %copy-done.5, bf16[32,8,128]{2,1,0:T(8,128)(2,1)} %pad_maximum_fusion.refs_2_, bf16[32,8,896]{2,1,0:T(8,128)(2,1)} %copy-done.3, bf16[32,8,896]{2,1,0:T(8,128)(2,1)} %copy-done.12), custom_call_target="tpu_custom_call" | custom-call | flops 1000000000 | bytes 2000000 | tf_op jit(solution)/shard_map/pallas_call | solution.py:239
  (123 shorter events, 13.6 us)
Async XLA Ops:
  0.6 28.1 %copy-start = (bf16[3584,128]{1,0:T(8,128)(2,1)S(1)}, bf16[3584,128]{1,0:T(8,128)(2,1)}, u32[]{:S(2)}) copy-start(bf16[3584,128]{1,0:T(8,128)(2,1)} %param.15) | copy-start | bytes 2752516
  6.0 19.6 %copy-start.8 = (bf16[1,4,3584]{2,1,0:T(4,128)(2,1)S(1)}, bf16[1,4,3584]{2,1,0:T(4,128)(2,1)}, u32[]{:S(2)}) copy-start(bf16[1,4,3584]{2,1,0:T(4,128)(2,1)} %param.21) | copy-start | bytes 86020
  6.0 19.6 %copy-start.9 = (bf16[1,3584,4]{1,2,0:T(4,128)(2,1)S(1)}, bf16[1,3584,4]{1,2,0:T(4,128)(2,1)}, u32[]{:S(2)}) copy-start(bf16[1,3584,4]{1,2,0:T(4,128)(2,1)} %param.18) | copy-start | bytes 86020
  6.1 20.3 %copy-start.11 = (s32[8]{0:T(128)S(1)}, s32[8]{0:T(128)}, u32[]{:S(2)}) copy-start(s32[8]{0:T(128)} %constant.113) | copy-start | bytes 100
  6.1 26.7 %collective-permute-start.13 = (bf16[56,896]{1,0:T(8,128)(2,1)}, bf16[56,896]{1,0:T(8,128)(2,1)S(1)}, u32[]{:S(2)}, u32[]{:S(2)}) collective-permute-start(bf16[56,896]{1,0:T(8,128)(2,1)} %bitcast.6), channel_id=1, source_target_pairs={{0,8},{8,16},{16,24},{24,32},{32,40},{40,48},{48,56},{56,0},{1,9},... | collective-permute-start | bytes 301064 | tf_op jit(solution)/shard_map/ppermute | solution.py:32
  8.6 27.1 %collective-permute-start.14 = (bf16[56,896]{1,0:T(8,128)(2,1)}, bf16[56,896]{1,0:T(8,128)(2,1)}, u32[]{:S(2)}, u32[]{:S(2)}) collective-permute-start(bf16[56,896]{1,0:T(8,128)(2,1)} %bitcast.6), channel_id=1, source_target_pairs={{0,56},{8,0},{16,8},{24,16},{32,24},{40,32},{48,40},{56,48},{1,57}... | collective-permute-start | bytes 301064 | tf_op jit(solution)/shard_map/ppermute | solution.py:32
  12.6 24.6 %collective-permute-start.15 = (bf16[56,896]{1,0:T(8,128)(2,1)}, bf16[56,896]{1,0:T(8,128)(2,1)}, u32[]{:S(2)}, u32[]{:S(2)}) collective-permute-start(bf16[56,896]{1,0:T(8,128)(2,1)} %bitcast.6), channel_id=1, source_target_pairs={{0,16},{8,24},{16,32},{24,40},{32,48},{40,56},{48,0},{56,8},{1,17}... | collective-permute-start | bytes 301064 | tf_op jit(solution)/shard_map/ppermute | solution.py:32
  12.6 29.7 %collective-permute-start.16 = (bf16[56,896]{1,0:T(8,128)(2,1)}, bf16[56,896]{1,0:T(8,128)(2,1)}, u32[]{:S(2)}, u32[]{:S(2)}) collective-permute-start(bf16[56,896]{1,0:T(8,128)(2,1)} %bitcast.6), channel_id=1, source_target_pairs={{0,48},{8,56},{16,0},{24,8},{32,16},{40,24},{48,32},{56,40},{1,49}... | collective-permute-start | bytes 301064 | tf_op jit(solution)/shard_map/ppermute | solution.py:32
  16.2 31.3 %all-to-all-start = ((bf16[32,8,1920]{2,1,0:T(8,128)(2,1)}), bf16[32,8,1920]{2,1,0:T(8,128)(2,1)}, u32[]{:S(2)}, u32[]{:S(2)}) async-start(bf16[32,8,1920]{2,1,0:T(8,128)(2,1)} %shard_map.139), calls=%async_computation | async-start | bytes 1966080 | tf_op jit(solution)/shard_map/all_to_all | solution.py:297
  24.4 4.4 %copy-start.1 = (bf16[256,3584]{1,0:T(8,128)(2,1)S(1)}, bf16[256,3584]{1,0:T(8,128)(2,1)}, u32[]{:S(2)}) copy-start(bf16[256,3584]{1,0:T(8,128)(2,1)} %refs_1_.1) | copy-start | bytes 5505028
  24.4 58.2 %collective-permute-start.17 = (bf16[56,896]{1,0:T(8,128)(2,1)}, bf16[56,896]{1,0:T(8,128)(2,1)}, u32[]{:S(2)}, u32[]{:S(2)}) collective-permute-start(bf16[56,896]{1,0:T(8,128)(2,1)} %bitcast.6), channel_id=1, source_target_pairs={{0,64},{64,128},{128,192},{192,0},{1,65},{65,129},{129,193},{193,1... | collective-permute-start | bytes 301064 | tf_op jit(solution)/shard_map/ppermute | solution.py:32
  32.7 9.6 %copy-start.18 = (bf16[56,896]{1,0:T(8,128)(2,1)}, bf16[56,896]{1,0:T(8,128)(2,1)S(1)}, u32[]{:S(2)}) copy-start(bf16[56,896]{1,0:T(8,128)(2,1)S(1)} %collective-permute-done.13.refs_0_) | copy-start | bytes 301060
  32.7 24.6 %collective-permute-start = (bf16[56,896]{1,0:T(8,128)(2,1)}, bf16[56,896]{1,0:T(8,128)(2,1)S(1)}, u32[]{:S(2)}, u32[]{:S(2)}) collective-permute-start(bf16[56,896]{1,0:T(8,128)(2,1)} %bitcast.6), channel_id=1, source_target_pairs={{0,24},{8,32},{16,40},{24,48},{32,56},{40,0},{48,8},{56,16},{1,25}... | collective-permute-start | bytes 301064 | tf_op jit(solution)/shard_map/ppermute | solution.py:32
  35.7 24.4 %collective-permute-start.1 = (bf16[56,896]{1,0:T(8,128)(2,1)}, bf16[56,896]{1,0:T(8,128)(2,1)S(1)}, u32[]{:S(2)}, u32[]{:S(2)}) collective-permute-start(bf16[56,896]{1,0:T(8,128)(2,1)} %bitcast.6), channel_id=1, source_target_pairs={{0,40},{8,48},{16,56},{24,0},{32,8},{40,16},{48,24},{56,32},{1,41}... | collective-permute-start | bytes 301064 | tf_op jit(solution)/shard_map/ppermute | solution.py:32
  37.2 30.8 %collective-permute-start.2 = (bf16[56,896]{1,0:T(8,128)(2,1)}, bf16[56,896]{1,0:T(8,128)(2,1)S(1)}, u32[]{:S(2)}, u32[]{:S(2)}) collective-permute-start(bf16[56,896]{1,0:T(8,128)(2,1)} %bitcast.6), channel_id=1, source_target_pairs={{0,32},{8,40},{16,48},{24,56},{32,0},{40,8},{48,16},{56,24},{1,33}... | collective-permute-start | bytes 301064 | tf_op jit(solution)/shard_map/ppermute | solution.py:32
  44.2 37.5 %collective-permute-start.18 = (bf16[4,56,896]{2,1,0:T(8,128)(2,1)}, bf16[4,56,896]{2,1,0:T(8,128)(2,1)S(1)}, u32[]{:S(2)}, u32[]{:S(2)}) collective-permute-start(bf16[4,56,896]{2,1,0:T(8,128)(2,1)} %shard_map.143.refs_1_), channel_id=1, source_target_pairs={{0,64},{64,128},{128,192},{192,0},{1,65},{65,129},{129,193},{193,1... | collective-permute-start | bytes 1204232 | tf_op jit(solution)/shard_map/ppermute | solution.py:32
  47.6 37.2 %all-to-all-start.1 = ((bf16[32,8,640]{2,1,0:T(8,128)(2,1)}), bf16[32,8,640]{2,1,0:T(8,128)(2,1)S(1)}, u32[]{:S(2)}, u32[]{:S(2)}) async-start(bf16[32,8,640]{2,1,0:T(8,128)(2,1)} %concatenate.27), calls=%async_computation.1 | async-start | bytes 655360 | tf_op jit(solution)/shard_map/all_to_all | solution.py:366
  57.4 13.1 %copy-start.10 = (f32[8,896]{1,0:T(8,128)}, f32[8,896]{1,0:T(8,128)S(1)}, u32[]{:S(2)}) copy-start(f32[8,896]{1,0:T(8,128)S(1)} %convert_reduce_fusion.refs_2_) | copy-start | bytes 86020
  57.4 10.7 %copy-start.19 = (bf16[56,896]{1,0:T(8,128)(2,1)}, bf16[56,896]{1,0:T(8,128)(2,1)S(1)}, u32[]{:S(2)}) copy-start(bf16[56,896]{1,0:T(8,128)(2,1)S(1)} %collective-permute-done.refs_0_) | copy-start | bytes 301060
  57.4 24.5 %collective-permute-start.20 = (bf16[4,56,896]{2,1,0:T(8,128)(2,1)}, bf16[4,56,896]{2,1,0:T(8,128)(2,1)S(1)}, u32[]{:S(2)}, u32[]{:S(2)}) collective-permute-start(bf16[4,56,896]{2,1,0:T(8,128)(2,1)} %shard_map.143.refs_1_), channel_id=1, source_target_pairs={{0,192},{64,0},{128,64},{192,128},{1,193},{65,1},{129,65},{193,129... | collective-permute-start | bytes 1204232 | tf_op jit(solution)/shard_map/ppermute | solution.py:32
  60.1 7.9 %copy-start.20 = (bf16[56,896]{1,0:T(8,128)(2,1)}, bf16[56,896]{1,0:T(8,128)(2,1)S(1)}, u32[]{:S(2)}) copy-start(bf16[56,896]{1,0:T(8,128)(2,1)S(1)} %collective-permute-done.1.refs_1_) | copy-start | bytes 301060
  60.1 11.0 %collective-permute-start.7 = (f32[8,896]{1,0:T(8,128)S(1)}, f32[8,896]{1,0:T(8,128)S(1)}, u32[]{:S(2)}, u32[]{:S(2)}) collective-permute-start(f32[8,896]{1,0:T(8,128)S(1)} %convert_reduce_fusion.refs_2_), channel_id=1, source_target_pairs={{0,4},{4,0},{1,5},{5,1},{2,6},{6,2},{3,7},{7,3},{8,12},{12,8},{9,1... | collective-permute-start | bytes 86024 | tf_op jit(solution)/shard_map/ppermute | solution.py:36
  70.5 9.4 %collective-permute-start.4 = (bf16[3,56,896]{2,1,0:T(8,128)(2,1)}, bf16[3,56,896]{2,1,0:T(8,128)(2,1)S(1)}, u32[]{:S(2)}, u32[]{:S(2)}) collective-permute-start(bf16[3,56,896]{2,1,0:T(8,128)(2,1)} %shard_map.140.refs_0_), channel_id=1, source_target_pairs={{0,192},{64,0},{128,64},{192,128},{1,193},{65,1},{129,65},{193,129... | collective-permute-start | bytes 903176 | tf_op jit(solution)/shard_map/ppermute | solution.py:32
  77.0 18.3 %collective-permute-start.8 = (bf16[272,896]{1,0:T(8,128)(2,1)}, bf16[272,896]{1,0:T(8,128)(2,1)}, u32[]{:S(2)}, u32[]{:S(2)}) collective-permute-start(bf16[272,896]{1,0:T(8,128)(2,1)} %shard_map.141.refs_5_.refs_9_), channel_id=1, source_target_pairs={{0,4},{4,0},{1,5},{5,1},{2,6},{6,2},{3,7},{7,3},{8,12},{12,8},{9,1... | collective-permute-start | bytes 1462280 | tf_op jit(solution)/shard_map/ppermute | solution.py:36
  79.9 20.6 %copy-start.4 = (bf16[3,56,896]{2,1,0:T(8,128)(2,1)}, bf16[3,56,896]{2,1,0:T(8,128)(2,1)S(1)}, u32[]{:S(2)}) copy-start(bf16[3,56,896]{2,1,0:T(8,128)(2,1)S(1)} %collective-permute-done.4.refs_2_) | copy-start | bytes 903172
  79.9 4.9 %collective-permute-start.19 = (bf16[56,896]{1,0:T(8,128)(2,1)}, bf16[56,896]{1,0:T(8,128)(2,1)}, u32[]{:S(2)}, u32[]{:S(2)}) collective-permute-start(bf16[56,896]{1,0:T(8,128)(2,1)} %bitcast.6), channel_id=1, source_target_pairs={{0,192},{64,0},{128,64},{192,128},{1,193},{65,1},{129,65},{193,129... | collective-permute-start | bytes 301064 | tf_op jit(solution)/shard_map/ppermute | solution.py:32
  81.7 13.6 %copy-start.6 = (bf16[4,56,896]{2,1,0:T(8,128)(2,1)}, bf16[4,56,896]{2,1,0:T(8,128)(2,1)S(1)}, u32[]{:S(2)}) copy-start(bf16[4,56,896]{2,1,0:T(8,128)(2,1)S(1)} %collective-permute-done.18.refs_3_) | copy-start | bytes 1204228
  81.7 5.5 %collective-permute-start.21 = (bf16[56,896]{1,0:T(8,128)(2,1)}, bf16[56,896]{1,0:T(8,128)(2,1)}, u32[]{:S(2)}, u32[]{:S(2)}) collective-permute-start(bf16[56,896]{1,0:T(8,128)(2,1)} %bitcast.6), channel_id=1, source_target_pairs={{0,128},{64,192},{128,0},{192,64},{1,129},{65,193},{129,1},{193,65... | collective-permute-start | bytes 301064 | tf_op jit(solution)/shard_map/ppermute | solution.py:32
  81.9 13.4 %copy-start.7 = (bf16[4,56,896]{2,1,0:T(8,128)(2,1)}, bf16[4,56,896]{2,1,0:T(8,128)(2,1)S(1)}, u32[]{:S(2)}) copy-start(bf16[4,56,896]{2,1,0:T(8,128)(2,1)S(1)} %collective-permute-done.20.refs_5_) | copy-start | bytes 1204228
  81.9 6.9 %collective-permute-start.22 = (bf16[2,56,896]{2,1,0:T(8,128)(2,1)S(1)}, bf16[2,56,896]{2,1,0:T(8,128)(2,1)S(1)}, u32[]{:S(2)}, u32[]{:S(2)}) collective-permute-start(bf16[2,56,896]{2,1,0:T(8,128)(2,1)S(1)} %slice.86), channel_id=1, source_target_pairs={{0,64},{64,128},{128,192},{192,0},{1,65},{65,129},{129,193},{193,1... | collective-permute-start | bytes 602120 | tf_op jit(solution)/shard_map/ppermute | solution.py:32
  82.6 12.8 %collective-permute-start.23 = (bf16[2,56,896]{2,1,0:T(8,128)(2,1)S(1)}, bf16[2,56,896]{2,1,0:T(8,128)(2,1)}, u32[]{:S(2)}, u32[]{:S(2)}) collective-permute-start(bf16[2,56,896]{2,1,0:T(8,128)(2,1)S(1)} %slice.87), channel_id=1, source_target_pairs={{0,192},{64,0},{128,64},{192,128},{1,193},{65,1},{129,65},{193,129... | collective-permute-start | bytes 602120 | tf_op jit(solution)/shard_map/ppermute | solution.py:32
  84.9 20.6 %collective-permute-start.3 = (bf16[3,56,896]{2,1,0:T(8,128)(2,1)}, bf16[3,56,896]{2,1,0:T(8,128)(2,1)}, u32[]{:S(2)}, u32[]{:S(2)}) collective-permute-start(bf16[3,56,896]{2,1,0:T(8,128)(2,1)} %shard_map.140.refs_0_), channel_id=1, source_target_pairs={{0,64},{64,128},{128,192},{192,0},{1,65},{65,129},{129,193},{193,1... | collective-permute-start | bytes 903176 | tf_op jit(solution)/shard_map/ppermute | solution.py:32
  87.2 26.5 %collective-permute-start.6 = (bf16[2,56,896]{2,1,0:T(8,128)(2,1)S(1)}, bf16[2,56,896]{2,1,0:T(8,128)(2,1)}, u32[]{:S(2)}, u32[]{:S(2)}) collective-permute-start(bf16[2,56,896]{2,1,0:T(8,128)(2,1)S(1)} %slice.75), channel_id=1, source_target_pairs={{0,192},{64,0},{128,64},{192,128},{1,193},{65,1},{129,65},{193,129... | collective-permute-start | bytes 602120 | tf_op jit(solution)/shard_map/ppermute | solution.py:32
  88.8 6.5 %copy-start.15 = (bf16[2,56,896]{2,1,0:T(8,128)(2,1)}, bf16[2,56,896]{2,1,0:T(8,128)(2,1)S(1)}, u32[]{:S(2)}) copy-start(bf16[2,56,896]{2,1,0:T(8,128)(2,1)S(1)} %collective-permute-done.22.refs_7_) | copy-start | bytes 602116
  88.8 17.9 %collective-permute-start.12 = (bf16[32,4,640]{2,1,0:T(4,128)(2,1)S(1)}, bf16[32,4,640]{2,1,0:T(4,128)(2,1)S(1)}, u32[]{:S(2)}, u32[]{:S(2)}) collective-permute-start(bf16[32,4,640]{2,1,0:T(4,128)(2,1)S(1)} %get-tuple-element.33), channel_id=1, source_target_pairs={{0,4},{4,0},{1,5},{5,1},{2,6},{6,2},{3,7},{7,3},{8,12},{12,8},{9,1... | collective-permute-start | bytes 491528 | tf_op jit(solution)/shard_map/ppermute | solution.py:36
  100.6 18.1 %collective-permute-start.24 = (bf16[37,8,512]{2,1,0:T(8,128)(2,1)}, bf16[37,8,512]{2,1,0:T(8,128)(2,1)S(1)}, u32[]{:S(2)}, u32[]{:S(2)}) collective-permute-start(bf16[37,8,512]{2,1,0:T(8,128)(2,1)} %get-tuple-element.26), channel_id=1, source_target_pairs={{0,2},{1,3},{2,0},{3,1},{4,6},{5,7},{6,4},{7,5},{8,10},{9,11},{10,... | collective-permute-start | bytes 909320 | tf_op jit(solution)/shard_map/ppermute | solution.py:32
  103.6 17.8 %collective-permute-start.25 = (bf16[37,8,512]{2,1,0:T(8,128)(2,1)}, bf16[37,8,512]{2,1,0:T(8,128)(2,1)S(1)}, u32[]{:S(2)}, u32[]{:S(2)}) collective-permute-start(bf16[37,8,512]{2,1,0:T(8,128)(2,1)} %get-tuple-element.27), channel_id=1, source_target_pairs={{0,1},{1,2},{2,3},{3,0},{4,5},{5,6},{6,7},{7,4},{8,9},{9,10},{10,1... | collective-permute-start | bytes 909320 | tf_op jit(solution)/shard_map/ppermute | solution.py:32
  106.4 5.3 %collective-permute-start.5 = (bf16[1,56,896]{2,1,0:T(8,128)(2,1)S(1)}, bf16[1,56,896]{2,1,0:T(8,128)(2,1)S(1)}, u32[]{:S(2)}, u32[]{:S(2)}) collective-permute-start(bf16[1,56,896]{2,1,0:T(8,128)(2,1)S(1)} %slice.74), channel_id=1, source_target_pairs={{0,64},{64,128},{128,192},{192,0},{1,65},{65,129},{129,193},{193,1... | collective-permute-start | bytes 301064 | tf_op jit(solution)/shard_map/ppermute | solution.py:32
  106.7 16.3 %collective-permute-start.26 = (bf16[37,8,512]{2,1,0:T(8,128)(2,1)}, bf16[37,8,512]{2,1,0:T(8,128)(2,1)}, u32[]{:S(2)}, u32[]{:S(2)}) collective-permute-start(bf16[37,8,512]{2,1,0:T(8,128)(2,1)} %get-tuple-element.28), channel_id=1, source_target_pairs={{0,3},{1,0},{2,1},{3,2},{4,7},{5,4},{6,5},{7,6},{8,11},{9,8},{10,9... | collective-permute-start | bytes 909320 | tf_op jit(solution)/shard_map/ppermute | solution.py:32
  110.9 7.7 %copy-start.3 = (bf16[32,8,896]{2,1,0:T(8,128)(2,1)}, bf16[32,8,896]{2,1,0:T(8,128)(2,1)S(1)}, u32[]{:S(2)}) copy-start(bf16[32,8,896]{2,1,0:T(8,128)(2,1)S(1)} %slice.72.refs_3_) | copy-start | bytes 1376260
  111.7 42.0 %collective-permute-start.27 = (bf16[32,8,896]{2,1,0:T(8,128)(2,1)S(1)}, bf16[32,8,896]{2,1,0:T(8,128)(2,1)S(1)}, u32[]{:S(2)}, u32[]{:S(2)}) collective-permute-start(bf16[32,8,896]{2,1,0:T(8,128)(2,1)S(1)} %slice.72.refs_3_), channel_id=1, source_target_pairs={{0,4},{4,0},{1,5},{5,1},{2,6},{6,2},{3,7},{7,3},{8,12},{12,8},{9,1... | collective-permute-start | bytes 1376264 | tf_op jit(solution)/shard_map/ppermute | solution.py:36
  118.6 7.7 %collective-permute-start.10 = (bf16[23,8,512]{2,1,0:T(8,128)(2,1)}, bf16[23,8,512]{2,1,0:T(8,128)(2,1)S(1)}, u32[]{:S(2)}, u32[]{:S(2)}) collective-permute-start(bf16[23,8,512]{2,1,0:T(8,128)(2,1)} %get-tuple-element.21), channel_id=1, source_target_pairs={{0,1},{1,2},{2,3},{3,0},{4,5},{5,6},{6,7},{7,4},{8,9},{9,10},{10,1... | collective-permute-start | bytes 565256 | tf_op jit(solution)/shard_map/ppermute | solution.py:32
  118.7 5.0 %copy-start.13 = (bf16[37,8,512]{2,1,0:T(8,128)(2,1)}, bf16[37,8,512]{2,1,0:T(8,128)(2,1)S(1)}, u32[]{:S(2)}) copy-start(bf16[37,8,512]{2,1,0:T(8,128)(2,1)S(1)} %collective-permute-done.24.refs_2_) | copy-start | bytes 909316
  118.7 7.6 %collective-permute-start.11 = (bf16[23,8,512]{2,1,0:T(8,128)(2,1)}, bf16[23,8,512]{2,1,0:T(8,128)(2,1)S(1)}, u32[]{:S(2)}, u32[]{:S(2)}) collective-permute-start(bf16[23,8,512]{2,1,0:T(8,128)(2,1)} %get-tuple-element.22), channel_id=1, source_target_pairs={{0,3},{1,0},{2,1},{3,2},{4,7},{5,4},{6,5},{7,6},{8,11},{9,8},{10,9... | collective-permute-start | bytes 565256 | tf_op jit(solution)/shard_map/ppermute | solution.py:32
  121.4 9.3 %collective-permute-start.9 = (bf16[23,8,512]{2,1,0:T(8,128)(2,1)}, bf16[23,8,512]{2,1,0:T(8,128)(2,1)}, u32[]{:S(2)}, u32[]{:S(2)}) collective-permute-start(bf16[23,8,512]{2,1,0:T(8,128)(2,1)} %get-tuple-element.20), channel_id=1, source_target_pairs={{0,2},{1,3},{2,0},{3,1},{4,6},{5,7},{6,4},{7,5},{8,10},{9,11},{10,... | collective-permute-start | bytes 565256 | tf_op jit(solution)/shard_map/ppermute | solution.py:32
  126.3 4.4 %copy-start.16 = (bf16[23,8,512]{2,1,0:T(8,128)(2,1)}, bf16[23,8,512]{2,1,0:T(8,128)(2,1)S(1)}, u32[]{:S(2)}) copy-start(bf16[23,8,512]{2,1,0:T(8,128)(2,1)S(1)} %collective-permute-done.10.refs_3_) | copy-start | bytes 565252
  141.2 21.5 %all-to-all-start.3 = ((f32[64,1,512]{2,1,0:T(1,128)}), f32[64,1,512]{2,1,0:T(1,128)S(1)}, u32[]{:S(2)}, u32[]{:S(2)}) async-start(f32[64,1,512]{2,1,0:T(1,128)} %broadcast_in_dim.53), calls=%async_computation.3 | async-start | bytes 262144 | tf_op jit(solution)/shard_map/all_to_all | solution.py:387
  153.7 9.1 %copy-start.12 = (bf16[32,8,896]{2,1,0:T(8,128)(2,1)}, bf16[32,8,896]{2,1,0:T(8,128)(2,1)S(1)}, u32[]{:S(2)}) copy-start(bf16[32,8,896]{2,1,0:T(8,128)(2,1)S(1)} %collective-permute-done.27.refs_4_) | copy-start | bytes 1376260
  (7 other events, 12.7 us)

commit v5 on v4

--- a/solution.py
+++ b/solution.py
@@ -96,12 +96,6 @@
     hi = d.astype(BF16).astype(F32)
     mixed_ref[256:272, :] = jnp.zeros((16, 896), BF16)
     mixed_ref[256:272, 0:256] = jnp.concatenate([hi, d - hi], axis=0).astype(BF16)
-
-
-def stack_kernel(*refs):
-    *ins, out_ref = refs
-    for e, ref in enumerate(ins):
-        out_ref[e] = ref[...]
 
 
 def project_kernel(plan, where_ref, *refs):
@@ -169,7 +163,7 @@
         low = low - piece.astype(F32)
     err = jnp.sum((total * total).reshape(groups, 8, 512), axis=0)
     err = jnp.sum(err, axis=0, keepdims=True) + so_far_ref[0]
-    err_ref[...] = jnp.broadcast_to(err[None], (4, 1, 512))
+    err_ref[...] = jnp.broadcast_to(err[None], (32, 1, 512))
 
 
 def final_kernel(where_ref, err_ref, left_ref, own_ref, other_ref, query_ref, out_ref, fit_ref):
@@ -301,7 +295,7 @@
     o1, o3, o2 = [shift(w_t, "pop_0", 4, d)[None] for d in (1, 3, 2)]
     for i, ins in enumerate(([z1, z7, z2, z6], [z3, z5, z4])):
         n, via = len(ins), VIA_UP[i]
-        own = call(stack_kernel, shape((n, 56, feats)), ins)
+        own = jnp.stack(ins)
         up, down = shift(own, "pop_0", 4, 1), shift(own, "pop_0", 4, 3)
         far = [shift(up[:via], "pop_0", 4, 1), shift(down[via:], "pop_0", 4, 3)]
         if i == 0:
@@ -373,18 +367,18 @@
     goal = jnp.where(c == 0, goal[:, :, 0], goal[:, :, 1])
     here = (((z - order) % 8)[:, None] == jnp.arange(8)).astype(BF16)
     goal = jnp.einsum("iz,tzf->tif", here, goal, preferred_element_type=F32).astype(BF16).reshape(8, 448)
-    err = jnp.zeros((4, 1, 512), F32)
+    err = jnp.zeros((32, 1, 512), F32)
     start = 128
     for group, met in zip(GROUPS, mets):
         n = 56 * len(group)
         right = late[:, :, start : start + n].reshape(256, n)
         part = goal[:, start - 128 : start - 128 + n]
         start += n
-        err = call(error_kernel, shape((4, 1, 512), F32), (ints(c), *met, right, part, err), smem=1)
-
-    err = lax.all_to_all(err, "mp", 0, 0, tiled=True)
+        err = call(error_kernel, shape((32, 1, 512), F32), (ints(c), *met, right, part, err), smem=1)
+
+    err = lax.all_to_all(err, ("pop_0", "pop_2", "mp"), 0, 0, tiled=True)
     err = jnp.sum(err, axis=0, keepdims=True)
-    err = lax.all_to_all(jnp.broadcast_to(err, (64, 1, 512)), POP, 0, 0, tiled=True)
+    err = lax.all_to_all(jnp.broadcast_to(err, (8, 1, 512)), "pop_1", 0, 0, tiled=True)
     grad_query, grad_out, fitness = call(
         final_kernel,
         [shape((56, feats), F32), shape((56, feats), F32), shape((1, 128), F32)],

time: 168 us -> 166 us (0.988)
  blocking collectives: 7.4 us -> 0 us
  starting transfers between devices: 86.1 us -> 89.9 us
  Pallas kernels: 31.6 us -> 27.9 us
  waiting for transfers between devices: 20.8 us -> 23.8 us
    all_to_all x1 -> x0, blocking collectives: 7.4 us -> none  [per_device(): err = lax.all_to_all(err, 'mp', 0, 0, tiled=True)]
    pallas_call x9 -> x7, Pallas kernels: 31.6 us -> 27.9 us  [call(): pl.pallas_call(kernel, out_shape=out, in_specs=[pl.BlockSpec(memory_space...]
    all_to_all x1 -> x2, waiting for transfers between devices: 9.08 us -> 12.6 us  [the longest x1 6.65 us: per_device(): err = lax.all_to_all(err, ('pop_0', 'pop_2', 'mp'), 0, 0, tiled=True)]
    ppermute x24, starting transfers between devices: 40.6 us -> 42.4 us  [shift(): return lax.ppermute(x, axis, [(i, (i + step) % size) for i in range(size)])]
    all_to_all x1 -> x2, starting transfers between devices: 11.2 us -> 12.1 us  [the longest x1 6.33 us: per_device(): err = lax.all_to_all(err, ('pop_0', 'pop_2', 'mp'), 0, 0, tiled=True)]
  transfers between devices with their start and end apart: 31 -> 32, of which waited for: 7 -> 9; matrix products, arithmetic and copies ran while one was open for 10% -> 11% of each run, Pallas kernels for 14% -> 12%
where the time goes in v5:
time: 166 us; the launch traced here: 165 us
  starting transfers between devices  89.9 us (54%)
  Pallas kernels  27.9 us (17%)
  waiting for transfers between devices  23.8 us (14%)
  local copies, waits for them, and re-layouts  11 us (7%)
  other arithmetic  8.02 us (5%)
  matrix products  2.3 us (1%)
  between operations  2.2 us (1%)
    ppermute x24, starting transfers between devices, shift(): return lax.ppermute(x, axis, [(i, (i + step) % size) for i in range(size)])  42.4 us
    pallas_call x7, Pallas kernels, call(): pl.pallas_call(kernel, out_shape=out, in_specs=[pl.BlockSpec(memory_space...  27.9 us
    ppermute x4, starting transfers between devices, swap(): return lax.ppermute(x, 'pop_2', [(0, 1), (1, 0)])  18.5 us
    all_to_all x1, starting transfers between devices, per_device(): late = lax.all_to_all(late, CHIPS, 0, 0, tiled=True)  8.69 us
    all_to_all x1, starting transfers between devices, per_device(): recv = lax.all_to_all(sent, CHIPS, 0, 0, tiled=True)  8.15 us
    ppermute x24, waiting for transfers between devices, shift(): return lax.ppermute(x, axis, [(i, (i + step) % size) for i in range(size)])  8.04 us
    all_to_all x1, waiting for transfers between devices, per_device(): err = lax.all_to_all(err, ('pop_0', 'pop_2', 'mp'), 0, 0, tiled=True)  6.65 us
    all_to_all x1, starting transfers between devices, per_device(): err = lax.all_to_all(err, ('pop_0', 'pop_2', 'mp'), 0, 0, tiled=True)  6.33 us
  transfers between devices with their start and end apart: 32, of which 9 were waited for; matrix products, arithmetic and copies ran while one was open for 11% of the time, Pallas kernels for 12%

profile of v5, /device:TPU:1, one launch (start us, length us, event | category | flops | bytes accessed | tf_op | source)
XLA Modules:
  0.0 165.1 jit_solution(14139151706744129890)
XLA Ops:
  2.0 4.0 %shard_map.139 = bf16[32,8,1920]{2,1,0:T(8,128)(2,1)} custom-call(s32[2]{0:T(128)} %pad_add_fusion.1.refs_0_, bf16[256,3584]{1,0:T(8,128)(2,1)} %refs_1_.1, bf16[56,896]{1,0:T(8,128)(2,1)} %refs_2_.1, bf16[4,3584]{1,0:T(4,128)(2,1)} %bitcast.84, bf16[4,896]{1,0:T(4,128)(2,1)} %bitcast.87, bf16[4,896]{1,0:T(4,128)(2,1)} %bitcast.88), custom_call_target="tpu_custom_call" | custom-call | flops 1000000000 | bytes 2000000 | tf_op jit(solution)/shard_map/pallas_call | solution.py:233
  6.0 2.5 %collective-permute-start.13 = (bf16[56,896]{1,0:T(8,128)(2,1)}, bf16[56,896]{1,0:T(8,128)(2,1)S(1)}, u32[]{:S(2)}, u32[]{:S(2)}) collective-permute-start(bf16[56,896]{1,0:T(8,128)(2,1)} %bitcast.6), channel_id=1, source_target_pairs={{0,8},{8,16},{16,24},{24,32},{32,40},{40,48},{48,56},{56,0},{1,9},... | collective-permute-start | bytes 301064 | tf_op jit(solution)/shard_map/ppermute | solution.py:32
  8.6 4.0 %collective-permute-start.14 = (bf16[56,896]{1,0:T(8,128)(2,1)}, bf16[56,896]{1,0:T(8,128)(2,1)S(1)}, u32[]{:S(2)}, u32[]{:S(2)}) collective-permute-start(bf16[56,896]{1,0:T(8,128)(2,1)} %bitcast.6), channel_id=1, source_target_pairs={{0,56},{8,0},{16,8},{24,16},{32,24},{40,32},{48,40},{56,48},{1,57}... | collective-permute-start | bytes 301064 | tf_op jit(solution)/shard_map/ppermute | solution.py:32
  12.6 3.6 %collective-permute-start.16 = (bf16[56,896]{1,0:T(8,128)(2,1)}, bf16[56,896]{1,0:T(8,128)(2,1)}, u32[]{:S(2)}, u32[]{:S(2)}) collective-permute-start(bf16[56,896]{1,0:T(8,128)(2,1)} %bitcast.6), channel_id=1, source_target_pairs={{0,48},{8,56},{16,0},{24,8},{32,16},{40,24},{48,32},{56,40},{1,49}... | collective-permute-start | bytes 301064 | tf_op jit(solution)/shard_map/ppermute | solution.py:32
  16.2 8.2 %all-to-all-start = ((bf16[32,8,1920]{2,1,0:T(8,128)(2,1)}), bf16[32,8,1920]{2,1,0:T(8,128)(2,1)}, u32[]{:S(2)}, u32[]{:S(2)}) async-start(bf16[32,8,1920]{2,1,0:T(8,128)(2,1)} %shard_map.139), calls=%async_computation | async-start | bytes 1966080 | tf_op jit(solution)/shard_map/all_to_all | solution.py:291
  24.4 1.2 collective-permute-start.17
  27.7 0.9 concatenate.27
  30.0 0.8 fusion.7.refs_4_
  30.8 1.3 convolution_convert_fusion.1.refs_5_
  32.7 3.0 %collective-permute-start = (bf16[56,896]{1,0:T(8,128)(2,1)}, bf16[56,896]{1,0:T(8,128)(2,1)S(1)}, u32[]{:S(2)}, u32[]{:S(2)}) collective-permute-start(bf16[56,896]{1,0:T(8,128)(2,1)} %bitcast.6), channel_id=1, source_target_pairs={{0,24},{8,32},{16,40},{24,48},{32,56},{40,0},{48,8},{56,16},{1,25}... | collective-permute-start | bytes 301064 | tf_op jit(solution)/shard_map/ppermute | solution.py:32
  35.7 1.5 collective-permute-start.1
  37.2 5.1 %collective-permute-start.2 = (bf16[56,896]{1,0:T(8,128)(2,1)}, bf16[56,896]{1,0:T(8,128)(2,1)S(1)}, u32[]{:S(2)}, u32[]{:S(2)}) collective-permute-start(bf16[56,896]{1,0:T(8,128)(2,1)} %bitcast.6), channel_id=1, source_target_pairs={{0,32},{8,40},{16,48},{24,56},{32,0},{40,8},{48,16},{56,24},{1,33}... | collective-permute-start | bytes 301064 | tf_op jit(solution)/shard_map/ppermute | solution.py:32
  42.3 1.0 pad_maximum_fusion.refs_1_
  43.3 1.3 collective-permute-start.18
  44.6 3.0 %all-to-all-done.refs_1_ = bf16[32,8,1920]{2,1,0:T(8,128)(2,1)} async-done(((bf16[32,8,1920]{2,1,0:T(8,128)(2,1)}), bf16[32,8,1920]{2,1,0:T(8,128)(2,1)}, u32[]{:S(2)}, u32[]{:S(2)}) %all-to-all-start) | async-done | bytes 983072 | tf_op jit(solution)/shard_map/all_to_all | solution.py:291
  47.5 8.7 %all-to-all-start.1 = ((bf16[32,8,640]{2,1,0:T(8,128)(2,1)}), bf16[32,8,640]{2,1,0:T(8,128)(2,1)S(1)}, u32[]{:S(2)}, u32[]{:S(2)}) async-start(bf16[32,8,640]{2,1,0:T(8,128)(2,1)} %concatenate.27), calls=%async_computation.1 | async-start | bytes 655360 | tf_op jit(solution)/shard_map/all_to_all | solution.py:360
  56.2 1.1 convert_reduce_fusion.refs_2_
  57.4 2.7 %collective-permute-start.20 = (bf16[4,56,896]{2,1,0:T(8,128)(2,1)S(1)}, bf16[4,56,896]{2,1,0:T(8,128)(2,1)}, u32[]{:S(2)}, u32[]{:S(2)}) collective-permute-start(bf16[4,56,896]{2,1,0:T(8,128)(2,1)S(1)} %pad_maximum_fusion.refs_1_), channel_id=1, source_target_pairs={{0,192},{64,0},{128,64},{192,128},{1,193},{65,1},{129,65},{193,129... | collective-permute-start | bytes 1204232 | tf_op jit(solution)/shard_map/ppermute | solution.py:32
  60.1 7.9 %collective-permute-start.7 = (f32[8,896]{1,0:T(8,128)S(1)}, f32[8,896]{1,0:T(8,128)S(1)}, u32[]{:S(2)}, u32[]{:S(2)}) collective-permute-start(f32[8,896]{1,0:T(8,128)S(1)} %convert_reduce_fusion.refs_2_), channel_id=1, source_target_pairs={{0,4},{4,0},{1,5},{5,1},{2,6},{6,2},{3,7},{7,3},{8,12},{12,8},{9,1... | collective-permute-start | bytes 86024 | tf_op jit(solution)/shard_map/ppermute | solution.py:36
  69.5 5.3 %shard_map.140.refs_5_.refs_9_ = bf16[272,896]{1,0:T(8,128)(2,1)} custom-call(s32[1]{0:T(128)} %bitcast.18.refs_0_, bf16[32,8,1920]{2,1,0:T(8,128)(2,1)} %all-to-all-done.refs_1_, f32[8,896]{1,0:T(8,128)} %copy-done.10, f32[8,896]{1,0:T(8,128)} %copy-done.20, bf16[256,128]{1,0:T(8,128)(2,1)} %fusion.7.refs_4_, ...), custom_call_target="tpu_custom_call" | custom-call | flops 1000000000 | bytes 2000000 | tf_op jit(solution)/shard_map/pallas_call | solution.py:233
  76.0 1.9 %collective-permute-done.4.refs_2_ = bf16[3,56,896]{2,1,0:T(8,128)(2,1)S(1)} collective-permute-done((bf16[3,56,896]{2,1,0:T(8,128)(2,1)S(1)}, bf16[3,56,896]{2,1,0:T(8,128)(2,1)S(1)}, u32[]{:S(2)}, u32[]{:S(2)}) %collective-permute-start.4) | collective-permute-done | bytes 301088 | tf_op jit(solution)/shard_map/ppermute | solution.py:32
  78.0 1.9 %collective-permute-start.19 = (bf16[56,896]{1,0:T(8,128)(2,1)}, bf16[56,896]{1,0:T(8,128)(2,1)S(1)}, u32[]{:S(2)}, u32[]{:S(2)}) collective-permute-start(bf16[56,896]{1,0:T(8,128)(2,1)} %bitcast.6), channel_id=1, source_target_pairs={{0,192},{64,0},{128,64},{192,128},{1,193},{65,1},{129,65},{193,129... | collective-permute-start | bytes 301064 | tf_op jit(solution)/shard_map/ppermute | solution.py:32
  80.0 0.9 slice.86
  81.6 0.9 slice.87
  82.5 2.2 %collective-permute-start.23 = (bf16[2,56,896]{2,1,0:T(8,128)(2,1)S(1)}, bf16[2,56,896]{2,1,0:T(8,128)(2,1)}, u32[]{:S(2)}, u32[]{:S(2)}) collective-permute-start(bf16[2,56,896]{2,1,0:T(8,128)(2,1)S(1)} %slice.87), channel_id=1, source_target_pairs={{0,192},{64,0},{128,64},{192,128},{1,193},{65,1},{129,65},{193,129... | collective-permute-start | bytes 602120 | tf_op jit(solution)/shard_map/ppermute | solution.py:32
  85.3 2.3 %collective-permute-start.6 = (bf16[2,56,896]{2,1,0:T(8,128)(2,1)S(1)}, bf16[2,56,896]{2,1,0:T(8,128)(2,1)}, u32[]{:S(2)}, u32[]{:S(2)}) collective-permute-start(bf16[2,56,896]{2,1,0:T(8,128)(2,1)S(1)} %slice.75), channel_id=1, source_target_pairs={{0,192},{64,0},{128,64},{192,128},{1,193},{65,1},{129,65},{193,129... | collective-permute-start | bytes 602120 | tf_op jit(solution)/shard_map/ppermute | solution.py:32
  87.6 8.1 %collective-permute-start.12 = (bf16[32,4,640]{2,1,0:T(4,128)(2,1)S(1)}, bf16[32,4,640]{2,1,0:T(4,128)(2,1)S(1)}, u32[]{:S(2)}, u32[]{:S(2)}) collective-permute-start(bf16[32,4,640]{2,1,0:T(4,128)(2,1)S(1)} %get-tuple-element.33), channel_id=1, source_target_pairs={{0,4},{4,0},{1,5},{5,1},{2,6},{6,2},{3,7},{7,3},{8,12},{12,8},{9,1... | collective-permute-start | bytes 491528 | tf_op jit(solution)/shard_map/ppermute | solution.py:36
  95.7 5.2 %shard_map.142 = (bf16[37,8,512]{2,1,0:T(8,128)(2,1)}, bf16[37,8,512]{2,1,0:T(8,128)(2,1)}, bf16[37,8,512]{2,1,0:T(8,128)(2,1)}, bf16[37,8,512]{2,1,0:T(8,128)(2,1)}) custom-call(s32[5]{0:T(128)} %stack.73.where_ref, bf16[1,56,896]{2,1,0:T(8,128)(2,1)} %bitcast.33.refs_0_, bf16[4,56,896]{2,1,0:T(8,128)(2,1)} %copy-done.4, ...), custom_call_target="tpu_custom_call" | custom-call | flops 1000000000 | bytes 2000000 | tf_op jit(solution)/shard_map/pallas_call | solution.py:233
  100.9 3.0 %collective-permute-start.24 = (bf16[37,8,512]{2,1,0:T(8,128)(2,1)}, bf16[37,8,512]{2,1,0:T(8,128)(2,1)S(1)}, u32[]{:S(2)}, u32[]{:S(2)}) collective-permute-start(bf16[37,8,512]{2,1,0:T(8,128)(2,1)} %get-tuple-element.26), channel_id=1, source_target_pairs={{0,2},{1,3},{2,0},{3,1},{4,6},{5,7},{6,4},{7,5},{8,10},{9,11},{10,... | collective-permute-start | bytes 909320 | tf_op jit(solution)/shard_map/ppermute | solution.py:32
  106.2 2.4 %collective-permute-start.26 = (bf16[37,8,512]{2,1,0:T(8,128)(2,1)}, bf16[37,8,512]{2,1,0:T(8,128)(2,1)S(1)}, u32[]{:S(2)}, u32[]{:S(2)}) collective-permute-start(bf16[37,8,512]{2,1,0:T(8,128)(2,1)} %get-tuple-element.28), channel_id=1, source_target_pairs={{0,3},{1,0},{2,1},{3,2},{4,7},{5,4},{6,5},{7,6},{8,11},{9,8},{10,9... | collective-permute-start | bytes 909320 | tf_op jit(solution)/shard_map/ppermute | solution.py:32
  108.6 0.8 fusion.3.refs_5_
  109.4 1.1 slice.72.refs_3_
  110.4 0.9 collective-permute-done.5.refs_3_
  111.3 2.1 %collective-permute-start.27 = (bf16[32,8,896]{2,1,0:T(8,128)(2,1)S(1)}, bf16[32,8,896]{2,1,0:T(8,128)(2,1)S(1)}, u32[]{:S(2)}, u32[]{:S(2)}) collective-permute-start(bf16[32,8,896]{2,1,0:T(8,128)(2,1)S(1)} %slice.72.refs_3_), channel_id=1, source_target_pairs={{0,4},{4,0},{1,5},{5,1},{2,6},{6,2},{3,7},{7,3},{8,12},{12,8},{9,1... | collective-permute-start | bytes 1376264 | tf_op jit(solution)/shard_map/ppermute | solution.py:36
  113.4 4.8 %shard_map.141 = (bf16[23,8,512]{2,1,0:T(8,128)(2,1)}, bf16[23,8,512]{2,1,0:T(8,128)(2,1)}, bf16[23,8,512]{2,1,0:T(8,128)(2,1)}, bf16[23,8,512]{2,1,0:T(8,128)(2,1)}) custom-call(s32[5]{0:T(128)} %stack.73.where_ref, bf16[3,56,896]{2,1,0:T(8,128)(2,1)} %copy-done.5, bf16[3,56,896]{2,1,0:T(8,128)(2,1)} %copy-done.8, bf16[3,56,896]{2,1,0:T(8,128)(2,1)} %copy-done.6, ...), custom_call_target="tpu_custom_call" | custom-call | flops 1000000000 | bytes 2000000 | tf_op jit(solution)/shard_map/pallas_call | solution.py:233
  118.3 2.6 %collective-permute-start.11 = (bf16[23,8,512]{2,1,0:T(8,128)(2,1)}, bf16[23,8,512]{2,1,0:T(8,128)(2,1)S(1)}, u32[]{:S(2)}, u32[]{:S(2)}) collective-permute-start(bf16[23,8,512]{2,1,0:T(8,128)(2,1)} %get-tuple-element.22), channel_id=1, source_target_pairs={{0,3},{1,0},{2,1},{3,2},{4,7},{5,4},{6,5},{7,6},{8,11},{9,8},{10,9... | collective-permute-start | bytes 565256 | tf_op jit(solution)/shard_map/ppermute | solution.py:32
  121.0 0.9 collective-permute-start.9
  121.8 0.8 fusion.5.refs_5_
  123.4 2.6 %shard_map.143.refs_7_ = f32[32,1,512]{2,1,0:T(1,128)} custom-call(s32[1]{0:T(128)} %bitcast.refs_0_, bf16[37,8,512]{2,1,0:T(8,128)(2,1)} %get-tuple-element.25.refs_1_, bf16[37,8,512]{2,1,0:T(8,128)(2,1)} %copy-done.14, bf16[37,8,512]{2,1,0:T(8,128)(2,1)} %collective-permute-done.25.refs_3_, bf16[37,8,512]{2,1,0:T(8,128)(2,1)} %copy-done.15, ...), custom_call_target="tpu_custom_call" | custom-call | flops 1000000000 | bytes 2000000 | tf_op jit(solution)/shard_map/pallas_call | solution.py:233
  126.1 2.9 %collective-permute-done.11.refs_4_ = bf16[23,8,512]{2,1,0:T(8,128)(2,1)S(1)} collective-permute-done((bf16[23,8,512]{2,1,0:T(8,128)(2,1)}, bf16[23,8,512]{2,1,0:T(8,128)(2,1)S(1)}, u32[]{:S(2)}, u32[]{:S(2)}) %collective-permute-start.11) | collective-permute-done | bytes 188448 | tf_op jit(solution)/shard_map/ppermute | solution.py:32
  129.0 1.9 %collective-permute-done.9.refs_2_ = bf16[23,8,512]{2,1,0:T(8,128)(2,1)} collective-permute-done((bf16[23,8,512]{2,1,0:T(8,128)(2,1)}, bf16[23,8,512]{2,1,0:T(8,128)(2,1)}, u32[]{:S(2)}, u32[]{:S(2)}) %collective-permute-start.9) | collective-permute-done | bytes 188448 | tf_op jit(solution)/shard_map/ppermute | solution.py:32
  130.9 2.4 %shard_map.144 = f32[32,1,512]{2,1,0:T(1,128)} custom-call(s32[1]{0:T(128)} %bitcast.refs_0_, bf16[23,8,512]{2,1,0:T(8,128)(2,1)} %get-tuple-element.19.refs_1_, bf16[23,8,512]{2,1,0:T(8,128)(2,1)} %collective-permute-done.9.refs_2_, bf16[23,8,512]{2,1,0:T(8,128)(2,1)} %copy-done.17, bf16[23,8,512]{2,1,0:T(8,128)(2,1)} %copy-done.18, ...), custom_call_target="tpu_custom_call" | custom-call | flops 1000000000 | bytes 2000000 | tf_op jit(solution)/shard_map/pallas_call | solution.py:233
  133.3 6.3 %all-to-all-start.2 = ((f32[32,1,512]{2,1,0:T(1,128)}), f32[32,1,512]{2,1,0:T(1,128)S(1)}, u32[]{:S(2)}, u32[]{:S(2)}) async-start(f32[32,1,512]{2,1,0:T(1,128)} %shard_map.144), calls=%async_computation.2 | async-start | bytes 131072 | tf_op jit(solution)/shard_map/all_to_all | solution.py:379
  140.3 6.6 %all-to-all-done.2 = f32[32,1,512]{2,1,0:T(1,128)S(1)} async-done(((f32[32,1,512]{2,1,0:T(1,128)}), f32[32,1,512]{2,1,0:T(1,128)S(1)}, u32[]{:S(2)}, u32[]{:S(2)}) %all-to-all-start.2) | async-done | bytes 65568 | tf_op jit(solution)/shard_map/all_to_all | solution.py:379
  147.6 5.7 %all-to-all-start.3 = ((f32[8,1,512]{2,1,0:T(1,128)}), f32[8,1,512]{2,1,0:T(1,128)S(1)}, u32[]{:S(2)}, u32[]{:S(2)}) async-start(f32[8,1,512]{2,1,0:T(1,128)} %broadcast_in_dim.53), calls=%async_computation.3 | async-start | bytes 32768 | tf_op jit(solution)/shard_map/all_to_all | solution.py:381
  154.0 6.0 %all-to-all-done.3.refs_1_ = f32[8,1,512]{2,1,0:T(1,128)S(1)} async-done(((f32[8,1,512]{2,1,0:T(1,128)}), f32[8,1,512]{2,1,0:T(1,128)S(1)}, u32[]{:S(2)}, u32[]{:S(2)}) %all-to-all-start.3) | async-done | bytes 16416 | tf_op jit(solution)/shard_map/all_to_all | solution.py:381
  160.6 0.8 copy-done.13
  161.4 3.5 %shard_map.145 = (f32[56,896]{1,0:T(8,128)}, f32[56,896]{1,0:T(8,128)}, f32[1,128]{1,0:T(1,128)}) custom-call(s32[2]{0:T(128)} %pad_add_fusion.refs_0_, f32[8,1,512]{2,1,0:T(1,128)} %copy-done.11, bf16[32,8,128]{2,1,0:T(8,128)(2,1)} %pad_maximum_fusion.2.refs_2_, bf16[32,8,896]{2,1,0:T(8,128)(2,1)} %copy-done.3, bf16[32,8,896]{2,1,0:T(8,128)(2,1)} %copy-done.13), custom_call_target="tpu_custom_call" | custom-call | flops 1000000000 | bytes 2000000 | tf_op jit(solution)/shard_map/pallas_call | solution.py:233
  (118 shorter events, 14.2 us)
Async XLA Ops:
  0.6 28.1 %copy-start = (bf16[3584,128]{1,0:T(8,128)(2,1)S(1)}, bf16[3584,128]{1,0:T(8,128)(2,1)}, u32[]{:S(2)}) copy-start(bf16[3584,128]{1,0:T(8,128)(2,1)} %param.15) | copy-start | bytes 2752516
  6.0 19.6 %copy-start.7 = (bf16[1,4,3584]{2,1,0:T(4,128)(2,1)S(1)}, bf16[1,4,3584]{2,1,0:T(4,128)(2,1)}, u32[]{:S(2)}) copy-start(bf16[1,4,3584]{2,1,0:T(4,128)(2,1)} %param.21) | copy-start | bytes 86020
  6.0 19.6 %copy-start.9 = (bf16[1,3584,4]{1,2,0:T(4,128)(2,1)S(1)}, bf16[1,3584,4]{1,2,0:T(4,128)(2,1)}, u32[]{:S(2)}) copy-start(bf16[1,3584,4]{1,2,0:T(4,128)(2,1)} %param.18) | copy-start | bytes 86020
  6.0 20.3 %copy-start.12 = (s32[8]{0:T(128)S(1)}, s32[8]{0:T(128)}, u32[]{:S(2)}) copy-start(s32[8]{0:T(128)} %constant.113) | copy-start | bytes 100
  6.0 26.7 %collective-permute-start.13 = (bf16[56,896]{1,0:T(8,128)(2,1)}, bf16[56,896]{1,0:T(8,128)(2,1)S(1)}, u32[]{:S(2)}, u32[]{:S(2)}) collective-permute-start(bf16[56,896]{1,0:T(8,128)(2,1)} %bitcast.6), channel_id=1, source_target_pairs={{0,8},{8,16},{16,24},{24,32},{32,40},{40,48},{48,56},{56,0},{1,9},... | collective-permute-start | bytes 301064 | tf_op jit(solution)/shard_map/ppermute | solution.py:32
  8.6 27.1 %collective-permute-start.14 = (bf16[56,896]{1,0:T(8,128)(2,1)}, bf16[56,896]{1,0:T(8,128)(2,1)S(1)}, u32[]{:S(2)}, u32[]{:S(2)}) collective-permute-start(bf16[56,896]{1,0:T(8,128)(2,1)} %bitcast.6), channel_id=1, source_target_pairs={{0,56},{8,0},{16,8},{24,16},{32,24},{40,32},{48,40},{56,48},{1,57}... | collective-permute-start | bytes 301064 | tf_op jit(solution)/shard_map/ppermute | solution.py:32
  12.6 24.6 %collective-permute-start.15 = (bf16[56,896]{1,0:T(8,128)(2,1)}, bf16[56,896]{1,0:T(8,128)(2,1)}, u32[]{:S(2)}, u32[]{:S(2)}) collective-permute-start(bf16[56,896]{1,0:T(8,128)(2,1)} %bitcast.6), channel_id=1, source_target_pairs={{0,16},{8,24},{16,32},{24,40},{32,48},{40,56},{48,0},{56,8},{1,17}... | collective-permute-start | bytes 301064 | tf_op jit(solution)/shard_map/ppermute | solution.py:32
  12.6 29.7 %collective-permute-start.16 = (bf16[56,896]{1,0:T(8,128)(2,1)}, bf16[56,896]{1,0:T(8,128)(2,1)}, u32[]{:S(2)}, u32[]{:S(2)}) collective-permute-start(bf16[56,896]{1,0:T(8,128)(2,1)} %bitcast.6), channel_id=1, source_target_pairs={{0,48},{8,56},{16,0},{24,8},{32,16},{40,24},{48,32},{56,40},{1,49}... | collective-permute-start | bytes 301064 | tf_op jit(solution)/shard_map/ppermute | solution.py:32
  16.2 31.3 %all-to-all-start = ((bf16[32,8,1920]{2,1,0:T(8,128)(2,1)}), bf16[32,8,1920]{2,1,0:T(8,128)(2,1)}, u32[]{:S(2)}, u32[]{:S(2)}) async-start(bf16[32,8,1920]{2,1,0:T(8,128)(2,1)} %shard_map.139), calls=%async_computation | async-start | bytes 1966080 | tf_op jit(solution)/shard_map/all_to_all | solution.py:291
  24.4 4.3 %copy-start.1 = (bf16[256,3584]{1,0:T(8,128)(2,1)S(1)}, bf16[256,3584]{1,0:T(8,128)(2,1)}, u32[]{:S(2)}) copy-start(bf16[256,3584]{1,0:T(8,128)(2,1)} %refs_1_.1) | copy-start | bytes 5505028
  24.4 58.1 %collective-permute-start.17 = (bf16[56,896]{1,0:T(8,128)(2,1)}, bf16[56,896]{1,0:T(8,128)(2,1)}, u32[]{:S(2)}, u32[]{:S(2)}) collective-permute-start(bf16[56,896]{1,0:T(8,128)(2,1)} %bitcast.6), channel_id=1, source_target_pairs={{0,64},{64,128},{128,192},{192,0},{1,65},{65,129},{129,193},{193,1... | collective-permute-start | bytes 301064 | tf_op jit(solution)/shard_map/ppermute | solution.py:32
  28.7 2.1 %copy-start.2 = (bf16[3584,128]{1,0:T(8,128)(2,1)S(1)}, bf16[3584,128]{1,0:T(8,128)(2,1)}, u32[]{:S(2)}) copy-start(bf16[3584,128]{1,0:T(8,128)(2,1)} %param.16) | copy-start | bytes 2752516
  32.7 24.6 %collective-permute-start = (bf16[56,896]{1,0:T(8,128)(2,1)}, bf16[56,896]{1,0:T(8,128)(2,1)S(1)}, u32[]{:S(2)}, u32[]{:S(2)}) collective-permute-start(bf16[56,896]{1,0:T(8,128)(2,1)} %bitcast.6), channel_id=1, source_target_pairs={{0,24},{8,32},{16,40},{24,48},{32,56},{40,0},{48,8},{56,16},{1,25}... | collective-permute-start | bytes 301064 | tf_op jit(solution)/shard_map/ppermute | solution.py:32
  35.7 24.4 %collective-permute-start.1 = (bf16[56,896]{1,0:T(8,128)(2,1)}, bf16[56,896]{1,0:T(8,128)(2,1)S(1)}, u32[]{:S(2)}, u32[]{:S(2)}) collective-permute-start(bf16[56,896]{1,0:T(8,128)(2,1)} %bitcast.6), channel_id=1, source_target_pairs={{0,40},{8,48},{16,56},{24,0},{32,8},{40,16},{48,24},{56,32},{1,41}... | collective-permute-start | bytes 301064 | tf_op jit(solution)/shard_map/ppermute | solution.py:32
  37.2 30.8 %collective-permute-start.2 = (bf16[56,896]{1,0:T(8,128)(2,1)}, bf16[56,896]{1,0:T(8,128)(2,1)S(1)}, u32[]{:S(2)}, u32[]{:S(2)}) collective-permute-start(bf16[56,896]{1,0:T(8,128)(2,1)} %bitcast.6), channel_id=1, source_target_pairs={{0,32},{8,40},{16,48},{24,56},{32,0},{40,8},{48,16},{56,24},{1,33}... | collective-permute-start | bytes 301064 | tf_op jit(solution)/shard_map/ppermute | solution.py:32
  43.3 31.4 %copy-start.4 = (bf16[4,56,896]{2,1,0:T(8,128)(2,1)}, bf16[4,56,896]{2,1,0:T(8,128)(2,1)S(1)}, u32[]{:S(2)}) copy-start(bf16[4,56,896]{2,1,0:T(8,128)(2,1)S(1)} %pad_maximum_fusion.refs_1_) | copy-start | bytes 1204228
  43.3 36.5 %collective-permute-start.18 = (bf16[4,56,896]{2,1,0:T(8,128)(2,1)S(1)}, bf16[4,56,896]{2,1,0:T(8,128)(2,1)}, u32[]{:S(2)}, u32[]{:S(2)}) collective-permute-start(bf16[4,56,896]{2,1,0:T(8,128)(2,1)S(1)} %pad_maximum_fusion.refs_1_), channel_id=1, source_target_pairs={{0,64},{64,128},{128,192},{192,0},{1,65},{65,129},{129,193},{193,1... | collective-permute-start | bytes 1204232 | tf_op jit(solution)/shard_map/ppermute | solution.py:32
  47.5 37.2 %all-to-all-start.1 = ((bf16[32,8,640]{2,1,0:T(8,128)(2,1)}), bf16[32,8,640]{2,1,0:T(8,128)(2,1)S(1)}, u32[]{:S(2)}, u32[]{:S(2)}) async-start(bf16[32,8,640]{2,1,0:T(8,128)(2,1)} %concatenate.27), calls=%async_computation.1 | async-start | bytes 655360 | tf_op jit(solution)/shard_map/all_to_all | solution.py:360
  57.3 11.5 %copy-start.10 = (f32[8,896]{1,0:T(8,128)}, f32[8,896]{1,0:T(8,128)S(1)}, u32[]{:S(2)}) copy-start(f32[8,896]{1,0:T(8,128)S(1)} %convert_reduce_fusion.refs_2_) | copy-start | bytes 86020
  57.4 23.6 %collective-permute-start.20 = (bf16[4,56,896]{2,1,0:T(8,128)(2,1)S(1)}, bf16[4,56,896]{2,1,0:T(8,128)(2,1)}, u32[]{:S(2)}, u32[]{:S(2)}) collective-permute-start(bf16[4,56,896]{2,1,0:T(8,128)(2,1)S(1)} %pad_maximum_fusion.refs_1_), channel_id=1, source_target_pairs={{0,192},{64,0},{128,64},{192,128},{1,193},{65,1},{129,65},{193,129... | collective-permute-start | bytes 1204232 | tf_op jit(solution)/shard_map/ppermute | solution.py:32
  60.1 8.8 %collective-permute-start.7 = (f32[8,896]{1,0:T(8,128)S(1)}, f32[8,896]{1,0:T(8,128)S(1)}, u32[]{:S(2)}, u32[]{:S(2)}) collective-permute-start(f32[8,896]{1,0:T(8,128)S(1)} %convert_reduce_fusion.refs_2_), channel_id=1, source_target_pairs={{0,4},{4,0},{1,5},{5,1},{2,6},{6,2},{3,7},{7,3},{8,12},{12,8},{9,1... | collective-permute-start | bytes 86024 | tf_op jit(solution)/shard_map/ppermute | solution.py:36
  68.1 16.8 %copy-start.5 = (bf16[3,56,896]{2,1,0:T(8,128)(2,1)}, bf16[3,56,896]{2,1,0:T(8,128)(2,1)S(1)}, u32[]{:S(2)}) copy-start(bf16[3,56,896]{2,1,0:T(8,128)(2,1)S(1)} %pad_maximum_fusion.1.refs_0_) | copy-start | bytes 903172
  68.1 9.9 %collective-permute-start.4 = (bf16[3,56,896]{2,1,0:T(8,128)(2,1)S(1)}, bf16[3,56,896]{2,1,0:T(8,128)(2,1)S(1)}, u32[]{:S(2)}, u32[]{:S(2)}) collective-permute-start(bf16[3,56,896]{2,1,0:T(8,128)(2,1)S(1)} %pad_maximum_fusion.1.refs_0_), channel_id=1, source_target_pairs={{0,192},{64,0},{128,64},{192,128},{1,193},{65,1},{129,65},{193,129... | collective-permute-start | bytes 903176 | tf_op jit(solution)/shard_map/ppermute | solution.py:32
  74.7 21.0 %collective-permute-start.8 = (bf16[272,896]{1,0:T(8,128)(2,1)}, bf16[272,896]{1,0:T(8,128)(2,1)}, u32[]{:S(2)}, u32[]{:S(2)}) collective-permute-start(bf16[272,896]{1,0:T(8,128)(2,1)} %shard_map.140.refs_5_.refs_9_), channel_id=1, source_target_pairs={{0,4},{4,0},{1,5},{5,1},{2,6},{6,2},{3,7},{7,3},{8,12},{12,8},{9,1... | collective-permute-start | bytes 1462280 | tf_op jit(solution)/shard_map/ppermute | solution.py:36
  78.0 23.0 %copy-start.6 = (bf16[3,56,896]{2,1,0:T(8,128)(2,1)}, bf16[3,56,896]{2,1,0:T(8,128)(2,1)S(1)}, u32[]{:S(2)}) copy-start(bf16[3,56,896]{2,1,0:T(8,128)(2,1)S(1)} %collective-permute-done.4.refs_2_) | copy-start | bytes 903172
  78.0 6.9 %collective-permute-start.19 = (bf16[56,896]{1,0:T(8,128)(2,1)}, bf16[56,896]{1,0:T(8,128)(2,1)S(1)}, u32[]{:S(2)}, u32[]{:S(2)}) collective-permute-start(bf16[56,896]{1,0:T(8,128)(2,1)} %bitcast.6), channel_id=1, source_target_pairs={{0,192},{64,0},{128,64},{192,128},{1,193},{65,1},{129,65},{193,129... | collective-permute-start | bytes 301064 | tf_op jit(solution)/shard_map/ppermute | solution.py:32
  79.9 5.5 %collective-permute-start.21 = (bf16[56,896]{1,0:T(8,128)(2,1)}, bf16[56,896]{1,0:T(8,128)(2,1)}, u32[]{:S(2)}, u32[]{:S(2)}) collective-permute-start(bf16[56,896]{1,0:T(8,128)(2,1)} %bitcast.6), channel_id=1, source_target_pairs={{0,128},{64,192},{128,0},{192,64},{1,129},{65,193},{129,1},{193,65... | collective-permute-start | bytes 301064 | tf_op jit(solution)/shard_map/ppermute | solution.py:32
  80.9 6.7 %collective-permute-start.22 = (bf16[2,56,896]{2,1,0:T(8,128)(2,1)S(1)}, bf16[2,56,896]{2,1,0:T(8,128)(2,1)S(1)}, u32[]{:S(2)}, u32[]{:S(2)}) collective-permute-start(bf16[2,56,896]{2,1,0:T(8,128)(2,1)S(1)} %slice.86), channel_id=1, source_target_pairs={{0,64},{64,128},{128,192},{192,0},{1,65},{65,129},{129,193},{193,1... | collective-permute-start | bytes 602120 | tf_op jit(solution)/shard_map/ppermute | solution.py:32
  82.5 13.2 %collective-permute-start.23 = (bf16[2,56,896]{2,1,0:T(8,128)(2,1)S(1)}, bf16[2,56,896]{2,1,0:T(8,128)(2,1)}, u32[]{:S(2)}, u32[]{:S(2)}) collective-permute-start(bf16[2,56,896]{2,1,0:T(8,128)(2,1)S(1)} %slice.87), channel_id=1, source_target_pairs={{0,192},{64,0},{128,64},{192,128},{1,193},{65,1},{129,65},{193,129... | collective-permute-start | bytes 602120 | tf_op jit(solution)/shard_map/ppermute | solution.py:32
  84.8 10.9 %copy-start.19 = (bf16[56,896]{1,0:T(8,128)(2,1)}, bf16[56,896]{1,0:T(8,128)(2,1)S(1)}, u32[]{:S(2)}) copy-start(bf16[56,896]{1,0:T(8,128)(2,1)S(1)} %collective-permute-done.19) | copy-start | bytes 301060
  84.9 21.0 %collective-permute-start.3 = (bf16[3,56,896]{2,1,0:T(8,128)(2,1)S(1)}, bf16[3,56,896]{2,1,0:T(8,128)(2,1)S(1)}, u32[]{:S(2)}, u32[]{:S(2)}) collective-permute-start(bf16[3,56,896]{2,1,0:T(8,128)(2,1)S(1)} %pad_maximum_fusion.1.refs_0_), channel_id=1, source_target_pairs={{0,64},{64,128},{128,192},{192,0},{1,65},{65,129},{129,193},{193,1... | collective-permute-start | bytes 903176 | tf_op jit(solution)/shard_map/ppermute | solution.py:32
  85.3 28.1 %collective-permute-start.6 = (bf16[2,56,896]{2,1,0:T(8,128)(2,1)S(1)}, bf16[2,56,896]{2,1,0:T(8,128)(2,1)}, u32[]{:S(2)}, u32[]{:S(2)}) collective-permute-start(bf16[2,56,896]{2,1,0:T(8,128)(2,1)S(1)} %slice.75), channel_id=1, source_target_pairs={{0,192},{64,0},{128,64},{192,128},{1,193},{65,1},{129,65},{193,129... | collective-permute-start | bytes 602120 | tf_op jit(solution)/shard_map/ppermute | solution.py:32
  87.6 8.1 %copy-start.16 = (bf16[2,56,896]{2,1,0:T(8,128)(2,1)}, bf16[2,56,896]{2,1,0:T(8,128)(2,1)S(1)}, u32[]{:S(2)}) copy-start(bf16[2,56,896]{2,1,0:T(8,128)(2,1)S(1)} %collective-permute-done.22.refs_7_) | copy-start | bytes 602116
  87.6 18.6 %collective-permute-start.12 = (bf16[32,4,640]{2,1,0:T(4,128)(2,1)S(1)}, bf16[32,4,640]{2,1,0:T(4,128)(2,1)S(1)}, u32[]{:S(2)}, u32[]{:S(2)}) collective-permute-start(bf16[32,4,640]{2,1,0:T(4,128)(2,1)S(1)} %get-tuple-element.33), channel_id=1, source_target_pairs={{0,4},{4,0},{1,5},{5,1},{2,6},{6,2},{3,7},{7,3},{8,12},{12,8},{9,1... | collective-permute-start | bytes 491528 | tf_op jit(solution)/shard_map/ppermute | solution.py:36
  100.9 17.3 %collective-permute-start.24 = (bf16[37,8,512]{2,1,0:T(8,128)(2,1)}, bf16[37,8,512]{2,1,0:T(8,128)(2,1)S(1)}, u32[]{:S(2)}, u32[]{:S(2)}) collective-permute-start(bf16[37,8,512]{2,1,0:T(8,128)(2,1)} %get-tuple-element.26), channel_id=1, source_target_pairs={{0,2},{1,3},{2,0},{3,1},{4,6},{5,7},{6,4},{7,5},{8,10},{9,11},{10,... | collective-permute-start | bytes 909320 | tf_op jit(solution)/shard_map/ppermute | solution.py:32
  103.9 17.0 %collective-permute-start.25 = (bf16[37,8,512]{2,1,0:T(8,128)(2,1)}, bf16[37,8,512]{2,1,0:T(8,128)(2,1)}, u32[]{:S(2)}, u32[]{:S(2)}) collective-permute-start(bf16[37,8,512]{2,1,0:T(8,128)(2,1)} %get-tuple-element.27), channel_id=1, source_target_pairs={{0,1},{1,2},{2,3},{3,0},{4,5},{5,6},{6,7},{7,4},{8,9},{9,10},{10,1... | collective-permute-start | bytes 909320 | tf_op jit(solution)/shard_map/ppermute | solution.py:32
  105.9 7.5 %copy-start.8 = (bf16[3,56,896]{2,1,0:T(8,128)(2,1)}, bf16[3,56,896]{2,1,0:T(8,128)(2,1)S(1)}, u32[]{:S(2)}) copy-start(bf16[3,56,896]{2,1,0:T(8,128)(2,1)S(1)} %collective-permute-done.3.refs_1_) | copy-start | bytes 903172
  105.9 5.4 %collective-permute-start.5 = (bf16[1,56,896]{2,1,0:T(8,128)(2,1)S(1)}, bf16[1,56,896]{2,1,0:T(8,128)(2,1)}, u32[]{:S(2)}, u32[]{:S(2)}) collective-permute-start(bf16[1,56,896]{2,1,0:T(8,128)(2,1)S(1)} %slice.74), channel_id=1, source_target_pairs={{0,64},{64,128},{128,192},{192,0},{1,65},{65,129},{129,193},{193,1... | collective-permute-start | bytes 301064 | tf_op jit(solution)/shard_map/ppermute | solution.py:32
  106.2 16.5 %collective-permute-start.26 = (bf16[37,8,512]{2,1,0:T(8,128)(2,1)}, bf16[37,8,512]{2,1,0:T(8,128)(2,1)S(1)}, u32[]{:S(2)}, u32[]{:S(2)}) collective-permute-start(bf16[37,8,512]{2,1,0:T(8,128)(2,1)} %get-tuple-element.28), channel_id=1, source_target_pairs={{0,3},{1,0},{2,1},{3,2},{4,7},{5,4},{6,5},{7,6},{8,11},{9,8},{10,9... | collective-permute-start | bytes 909320 | tf_op jit(solution)/shard_map/ppermute | solution.py:32
  110.4 7.8 %copy-start.3 = (bf16[32,8,896]{2,1,0:T(8,128)(2,1)}, bf16[32,8,896]{2,1,0:T(8,128)(2,1)S(1)}, u32[]{:S(2)}) copy-start(bf16[32,8,896]{2,1,0:T(8,128)(2,1)S(1)} %slice.72.refs_3_) | copy-start | bytes 1376260
  111.3 48.7 %collective-permute-start.27 = (bf16[32,8,896]{2,1,0:T(8,128)(2,1)S(1)}, bf16[32,8,896]{2,1,0:T(8,128)(2,1)S(1)}, u32[]{:S(2)}, u32[]{:S(2)}) collective-permute-start(bf16[32,8,896]{2,1,0:T(8,128)(2,1)S(1)} %slice.72.refs_3_), channel_id=1, source_target_pairs={{0,4},{4,0},{1,5},{5,1},{2,6},{6,2},{3,7},{7,3},{8,12},{12,8},{9,1... | collective-permute-start | bytes 1376264 | tf_op jit(solution)/shard_map/ppermute | solution.py:36
  118.2 7.9 %collective-permute-start.10 = (bf16[23,8,512]{2,1,0:T(8,128)(2,1)}, bf16[23,8,512]{2,1,0:T(8,128)(2,1)S(1)}, u32[]{:S(2)}, u32[]{:S(2)}) collective-permute-start(bf16[23,8,512]{2,1,0:T(8,128)(2,1)} %get-tuple-element.21), channel_id=1, source_target_pairs={{0,1},{1,2},{2,3},{3,0},{4,5},{5,6},{6,7},{7,4},{8,9},{9,10},{10,1... | collective-permute-start | bytes 565256 | tf_op jit(solution)/shard_map/ppermute | solution.py:32
  118.3 5.1 %copy-start.14 = (bf16[37,8,512]{2,1,0:T(8,128)(2,1)}, bf16[37,8,512]{2,1,0:T(8,128)(2,1)S(1)}, u32[]{:S(2)}) copy-start(bf16[37,8,512]{2,1,0:T(8,128)(2,1)S(1)} %collective-permute-done.24.refs_2_) | copy-start | bytes 909316
  118.3 10.7 %collective-permute-start.11 = (bf16[23,8,512]{2,1,0:T(8,128)(2,1)}, bf16[23,8,512]{2,1,0:T(8,128)(2,1)S(1)}, u32[]{:S(2)}, u32[]{:S(2)}) collective-permute-start(bf16[23,8,512]{2,1,0:T(8,128)(2,1)} %get-tuple-element.22), channel_id=1, source_target_pairs={{0,3},{1,0},{2,1},{3,2},{4,7},{5,4},{6,5},{7,6},{8,11},{9,8},{10,9... | collective-permute-start | bytes 565256 | tf_op jit(solution)/shard_map/ppermute | solution.py:32
  121.0 9.9 %collective-permute-start.9 = (bf16[23,8,512]{2,1,0:T(8,128)(2,1)}, bf16[23,8,512]{2,1,0:T(8,128)(2,1)}, u32[]{:S(2)}, u32[]{:S(2)}) collective-permute-start(bf16[23,8,512]{2,1,0:T(8,128)(2,1)} %get-tuple-element.20), channel_id=1, source_target_pairs={{0,2},{1,3},{2,0},{3,1},{4,6},{5,7},{6,4},{7,5},{8,10},{9,11},{10,... | collective-permute-start | bytes 565256 | tf_op jit(solution)/shard_map/ppermute | solution.py:32
  126.1 4.8 %copy-start.17 = (bf16[23,8,512]{2,1,0:T(8,128)(2,1)}, bf16[23,8,512]{2,1,0:T(8,128)(2,1)S(1)}, u32[]{:S(2)}) copy-start(bf16[23,8,512]{2,1,0:T(8,128)(2,1)S(1)} %collective-permute-done.10.refs_3_) | copy-start | bytes 565252
  133.3 13.6 %all-to-all-start.2 = ((f32[32,1,512]{2,1,0:T(1,128)}), f32[32,1,512]{2,1,0:T(1,128)S(1)}, u32[]{:S(2)}, u32[]{:S(2)}) async-start(f32[32,1,512]{2,1,0:T(1,128)} %shard_map.144), calls=%async_computation.2 | async-start | bytes 131072 | tf_op jit(solution)/shard_map/all_to_all | solution.py:379
  147.6 12.4 %all-to-all-start.3 = ((f32[8,1,512]{2,1,0:T(1,128)}), f32[8,1,512]{2,1,0:T(1,128)S(1)}, u32[]{:S(2)}, u32[]{:S(2)}) async-start(f32[8,1,512]{2,1,0:T(1,128)} %broadcast_in_dim.53), calls=%async_computation.3 | async-start | bytes 32768 | tf_op jit(solution)/shard_map/all_to_all | solution.py:381
  (5 other events, 4.7 us)
